TPU v7x, 32 devices: a whole 2x2x4 slice. The times are simulated.
32 devices in a mesh: grp: 4 (over y, x), shard: 8 (over z, core).
Axes of the slice: x: 2, y: 2, z: 4, core: 2. Of those that a mesh axis runs over, the one named last changes fastest.
Arguments:
- bottom_out: bfloat16 [4096, 128], P(('grp', 'shard')), may hold values from -6 to 6
- lookups: int32 [4096, 1, 4], P(('grp', 'shard')), may hold values from 0 to 62975, as said below
- starts: int32 [4, 32], replicated, may hold values from 0 to 1967
- tables: float32 [1, 62976, 128], P(None, 'shard'), may hold values from -0.3 to 0.3
- top_dense: bfloat16 [128, 1024], replicated, may hold values from -0.5 to 0.5
- top_pairs: float32 [1, 1024], replicated, may hold values from -6 to 6
- cotangent: float32 [4096, 1024], P(('grp', 'shard')), may hold values from -1.5 to 1.5
Outputs:
- activation: bfloat16 [4096, 1024], P(('grp', 'shard'))
- bottom_grad: float32 [4096, 128], P(('grp', 'shard'))
- table_grad: float32 [1, 8, 7872, 128], P(None, 'shard', 'grp')
Inputs may be any that keep to these rules, and one draw needn't show every extreme that they name: lookups % 1968 is below 64, and 63 occurs.
All inputs are finite; a program needn't handle non-finite values.
Results may differ from a plain program's by a relative error of at most 0.0023.
Values sent between devices are 32-bit elements; how exact they have to be, the bound alone decides.
No kernel may reach another device: no remote copies, remote signals or barrier semaphores. Data moves between devices by JAX's collectives and lax.ppermute only.
A program may use at most 64 MiB of HBM per device.

v0:
```python
import math

import jax
import jax.numpy as jnp
from jax import lax
from jax.sharding import PartitionSpec as P

HOT = 64


def pair_list(number):
    return [(former, latter) for former in range(number) for latter in range(former + 1, number)]


def pool_lookups(tables, picked, offset):
    rows_count = picked.shape[0]
    table_count = picked.shape[1]
    bag_count = picked.shape[2]
    rows_block = math.gcd(rows_count, 512)
    bag_block = math.gcd(bag_count, 8)
    bag_turns = bag_count // bag_block
    span_rows = tables.shape[1]
    table_ids = jnp.arange(table_count, dtype=jnp.int32)[None, :, None]

    def pool_step(turn, running):
        row_turn = turn // bag_turns
        bag_turn = turn % bag_turns
        chosen = lax.dynamic_slice(
            picked,
            (row_turn * rows_block, 0, bag_turn * bag_block),
            (rows_block, table_count, bag_block),
        )
        local = chosen - offset
        inside = (local >= 0) & (local < span_rows)
        fetched = tables[table_ids, jnp.clip(local, 0, span_rows - 1)]
        summed = jnp.sum(jnp.where(inside[..., None], fetched, 0.0), axis=2)
        current = lax.dynamic_slice_in_dim(running, row_turn * rows_block, rows_block, 0)
        return lax.dynamic_update_slice_in_dim(running, current + summed, row_turn * rows_block, 0)

    start_value = jnp.zeros((rows_count, table_count, tables.shape[2]), jnp.float32)
    return lax.fori_loop(0, rows_count // rows_block * bag_turns, pool_step, start_value)


def add_lookups(running_grad, grads, picked, offset, span_rows):
    rows_count = picked.shape[0]
    table_count = picked.shape[1]
    bag_count = picked.shape[2]
    rows_block = math.gcd(rows_count, 512)
    bag_block = math.gcd(bag_count, 8)
    bag_turns = bag_count // bag_block
    table_ids = jnp.arange(table_count, dtype=jnp.int32)[None, :, None]

    def add_step(turn, running):
        row_turn = turn // bag_turns
        bag_turn = turn % bag_turns
        chosen = lax.dynamic_slice(
            picked,
            (row_turn * rows_block, 0, bag_turn * bag_block),
            (rows_block, table_count, bag_block),
        )
        grads_block = lax.dynamic_slice_in_dim(grads, row_turn * rows_block, rows_block, 0)
        local = chosen - offset
        inside = (local >= 0) & (local < span_rows)
        updates = jnp.where(inside[..., None], grads_block[:, :, None, :], 0.0)
        return running.at[table_ids, jnp.clip(local, 0, span_rows - 1)].add(updates)

    return lax.fori_loop(0, rows_count // rows_block * bag_turns, add_step, running_grad)


def on_device(bottom_out, lookups, starts, tables, top_dense, top_pairs, cotangent):
    shard_pos = lax.axis_index("shard")
    grp_pos = lax.axis_index("grp")
    group_count = lax.axis_size("grp")
    span_rows = tables.shape[1]
    table_count = tables.shape[0]
    width = tables.shape[2]
    win_size = span_rows // group_count
    offset = shard_pos * span_rows
    my_starts = lax.dynamic_index_in_dim(starts, grp_pos, 0, keepdims=False)
    window = lookups // win_size
    inner = lookups % win_size
    own_rows = window * win_size + (inner + my_starts[window]) % win_size
    group_idx = lax.all_gather(own_rows, "shard", axis=0, tiled=True)
    picked = group_idx
    pooled = lax.psum_scatter(
        pool_lookups(tables, picked, offset), "shard", scatter_dimension=0, tiled=True
    )
    vectors = [bottom_out.astype(jnp.float32)] + [pooled[:, 0]]
    couples = pair_list(table_count + 1)
    pair_dots = jnp.stack(
        [jnp.sum(vectors[former] * vectors[latter], axis=-1) for former, latter in couples], axis=1
    )
    preact = jnp.dot(bottom_out, top_dense, preferred_element_type=jnp.float32)
    preact = preact + jnp.dot(pair_dots, top_pairs, precision=lax.Precision.HIGHEST)
    sigmoid_pre = jax.nn.sigmoid(preact)
    activation = (preact * sigmoid_pre).astype(jnp.bfloat16)
    pre_grad = cotangent * sigmoid_pre * (1.0 + preact * (1.0 - sigmoid_pre))
    pair_grad = jnp.dot(pre_grad, top_pairs.T, precision=lax.Precision.HIGHEST)
    vec_grads = [jnp.zeros_like(vector) for vector in vectors]
    for place, (former, latter) in enumerate(couples):
        vec_grads[former] = pair_grad * vectors[latter]
        vec_grads[latter] = pair_grad * vectors[former]
    pre_half = pre_grad.astype(jnp.bfloat16)
    bottom_grad = (
        lax.dot_general(
            pre_half, top_dense, (((1,), (1,)), ((), ())), preferred_element_type=jnp.float32
        )
        + vec_grads[0]
    )
    pooled_grad = jnp.stack(vec_grads[1:], axis=1)
    start_grad = jnp.zeros((table_count, span_rows, width), jnp.float32)
    picked = group_idx
    local_grad = add_lookups(
        start_grad,
        lax.all_gather(pooled_grad, "shard", axis=0, tiled=True),
        picked,
        offset,
        span_rows,
    )
    hot_range = jnp.arange(HOT, dtype=jnp.int32)
    owner_range = jnp.arange(group_count, dtype=jnp.int32)
    send_starts = lax.dynamic_slice_in_dim(my_starts, shard_pos * group_count, group_count, 0)
    send_index = (
        owner_range[:, None] * win_size + (send_starts[:, None] + hot_range[None, :]) % win_size
    )
    packed = local_grad[:, send_index]
    received = lax.all_to_all(packed, "grp", split_axis=1, concat_axis=1, tiled=True)
    recv_starts = lax.dynamic_slice_in_dim(starts, shard_pos * group_count + grp_pos, 1, 1)[:, 0]
    places = ((recv_starts[:, None] + hot_range[None, :]) % win_size).reshape(-1)
    flat_rows = received.reshape(table_count, group_count * HOT, width)
    table_grad = jnp.zeros((table_count, win_size, width), jnp.float32).at[:, places].add(flat_rows)
    return (activation, bottom_grad, table_grad[:, None])


def solution(mesh):
    in_specs = (
        P(("grp", "shard"), None),
        P(("grp", "shard"), None, None),
        P(),
        P(None, "shard", None),
        P(),
        P(),
        P(("grp", "shard"), None),
    )
    out_specs = (
        P(("grp", "shard"), None),
        P(("grp", "shard"), None),
        P(None, "shard", "grp", None),
    )
    return jax.shard_map(
        on_device, mesh=mesh, in_specs=in_specs, out_specs=out_specs, check_vma=False
    )
```

profile of v0, /device:TPU:0, one launch (start us, length us, event | category | flops | bytes accessed | tf_op | source)
XLA Modules:
  0.0 300.7 jit_solution(15566653151355944525)
XLA Ops:
  7.2 0.7 compare_select_fusion.4
  8.9 3.3 %gather_fusion.1 = s32[512]{0:T(512)S(1)} fusion(s32[32]{0:T(128)S(1)} %dynamic-slice_bitcast_fusion.2, s32[1024]{0:T(1024)S(1)} %pad_clamp_fusion.1), kind=kCustom, calls=%fused_computation.1 | custom fusion | bytes 6144 | tf_op jit(solution)/shard_map/gather | solution.py:82
  12.5 14.5 %all_gather.6 = s32[1024,1,4]{0,2,1:T(4,128)S(1)} all-gather(s32[128,1,4]{0,2,1:T(4,128)S(1)} %fusion.15), channel_id=1, replica_groups=mesh['grp'=4,'shard'=8] {'shard'}, dimensions={0}, use_global_device_ids=true | all-gather | bytes 18432 | tf_op jit(solution)/shard_map/all_gather | solution.py:83
  27.3 161.7 %while.30 = (s32[]{:T(128)}, f32[1024,1,128]{2,1,0:T(1,128)S(1)}, s32[1024,1,4]{0,2,1:T(4,128)S(1)}, s32[]{:T(128)}, f32[1,7872,128]{2,1,0:T(8,128)}, /*index=5*/s32[]{:T(128)}, s32[]{:T(128)}, s32[]{:T(128)}, s32[]{:T(128)}) while((s32[]{:T(128)}, f32[1024,1,128]{2,1,0:T(1,128)S(1)}, s32[1024,1,4]{0,2,1:T(4,128)S(1)}, s32[]{:T(128)}, ...), condition=%wide.region_2.3_spmd, body=%wide.region_0.2_spmd.sunk | while | flops 552966 | bytes 4325543 | solution.py:41
  27.7 77.2 %gather_fusion = f32[2048,128]{1,0:T(8,128)S(1)} fusion(f32[1,7872,128]{2,1,0:T(8,128)} %get-tuple-element.379, s32[2048]{0:T(1024)S(1)} %reshape.281), kind=kCustom, calls=%fused_computation.clone.1 | custom fusion | bytes 2113536 | tf_op jit(solution)/shard_map/while/body/eval_jaxpr/gather | solution.py:35
  105.1 2.9 select_reduce_fusion.2
  108.7 76.8 %gather_fusion = f32[2048,128]{1,0:T(8,128)S(1)} fusion(f32[1,7872,128]{2,1,0:T(8,128)} %get-tuple-element.379, s32[2048]{0:T(1024)S(1)} %reshape.281), kind=kCustom, calls=%fused_computation.clone.1 | custom fusion | bytes 2113536 | tf_op jit(solution)/shard_map/while/body/eval_jaxpr/gather | solution.py:35
  185.8 2.9 select_reduce_fusion.2
  189.0 0.8 copy-done.1
  190.5 29.0 %reduce-scatter.2.cloned.1.call-done = f32[128,1,128]{2,0,1:T(8,128)} async-done(((f32[1024,1,128]{2,0,1:T(8,128)}), f32[128,1,128]{2,0,1:T(8,128)}) %reduce-scatter.2.cloned.1.call-update) | async-done | bytes 65552 | tf_op jit(solution)/shard_map/reduce_scatter | solution.py:85
  219.5 0.9 fusion.11
  220.5 1.1 add_multiply_fusion
  222.2 14.9 %all-gather = f32[1024,128]{1,0:T(8,128)S(1)} all-gather(f32[128,128]{1,0:T(8,128)S(1)} %convert_multiply_fusion), channel_id=2, replica_groups=mesh['grp'=4,'shard'=8] {'shard'}, dimensions={0}, use_global_device_ids=true | all-gather | bytes 589824 | tf_op jit(solution)/shard_map/all_gather | solution.py:115
  237.1 2.1 broadcast_in_dim.113
  239.3 40.0 %while.31 = (s32[]{:T(128)}, f32[1,7872,128]{2,1,0:T(8,128)}, s32[1024,1,4]{0,2,1:T(4,128)S(1)}, s32[]{:T(128)}, f32[1024,1,128]{2,0,1:T(8,128)S(1)}, /*index=5*...) while((s32[]{:T(128)}, f32[1,7872,128]{2,1,0:T(8,128)}, ...), condition=%wide.region_7.8_spmd, body=%wide.region_5.7_spmd.sunk | while | flops 565254 | bytes 5099719 | solution.py:67
  240.0 2.3 broadcast_select_fusion.5
  242.4 17.0 %scatter_fusion = f32[7872,128]{1,0:T(8,128)} fusion(f32[7872,128]{1,0:T(8,128)} %bitcast.73, s32[2048]{0:T(1024)S(1)} %reshape.284, f32[2048,128]{1,0:T(8,128)S(1)} %bitcast.77), kind=kCustom, calls=%fused_computation.3.clone.1 | custom fusion | flops 262144 | bytes 3153920 | tf_op jit(solution)/shard_map/while
  260.1 2.3 broadcast_select_fusion.5
  262.4 16.9 %scatter_fusion = f32[7872,128]{1,0:T(8,128)} fusion(f32[7872,128]{1,0:T(8,128)} %bitcast.73, s32[2048]{0:T(1024)S(1)} %reshape.284, f32[2048,128]{1,0:T(8,128)S(1)} %bitcast.77), kind=kCustom, calls=%fused_computation.3.clone.1 | custom fusion | flops 262144 | bytes 3153920 | tf_op jit(solution)/shard_map/while
  279.3 3.5 %gather_fusion.2 = f32[256,128]{1,0:T(8,128)} fusion(f32[7872,128]{1,0:T(8,128)} %bitcast.75, s32[1024]{0:T(1024)S(1)} %pad_clamp_fusion), kind=kCustom, calls=%fused_computation.2 | custom fusion | bytes 263168 | tf_op jit(solution)/shard_map/gather | solution.py:126
  282.8 3.6 %all-to-all-start = ((f32[1,4,64,128]{3,2,0,1:T(8,128)}), f32[1,4,64,128]{3,2,0,1:T(8,128)S(1)}, u32[]{:S(2)}, u32[]{:S(2)}) async-start(f32[1,4,64,128]{3,2,0,1:T(8,128)} %bitcast.22), calls=%async_computation.1 | async-start | bytes 262144 | tf_op jit(solution)/shard_map/all_to_all | solution.py:127
  286.4 0.9 convolution_add_fusion.1
  287.3 4.2 %all-to-all-done = f32[1,4,64,128]{3,2,0,1:T(8,128)S(1)} async-done(((f32[1,4,64,128]{3,2,0,1:T(8,128)}), f32[1,4,64,128]{3,2,0,1:T(8,128)S(1)}, u32[]{:S(2)}, u32[]{:S(2)}) %all-to-all-start) | async-done | bytes 131104 | tf_op jit(solution)/shard_map/all_to_all | solution.py:127
  291.4 2.4 scatter_custom_fusion.1
  (74 shorter events, 5.9 us)
Async XLA Ops:
  7.2 213.3 %copy-start = (bf16[128,1024]{1,0:T(8,128)(2,1)S(1)}, bf16[128,1024]{1,0:T(8,128)(2,1)}, u32[]{:S(2)}) copy-start(bf16[128,1024]{1,0:T(8,128)(2,1)} %param.15) | copy-start | bytes 786436
  7.2 212.3 %reduce-scatter.2.cloned.1.call-start = ((), (), s32[]{:S(2)}) async-start(), calls=%async_computation.2 | async-start | bytes 589824 | tf_op jit(solution)/shard_map/reduce_scatter | solution.py:85
  8.9 3.5 %copy-start.6 = (s32[128,1,4]{0,2,1:T(4,128)S(1)}, s32[128,1,4]{0,2,1:T(4,128)}, u32[]{:S(2)}) copy-start(s32[128,1,4]{0,2,1:T(4,128)} %param.12) | copy-start | bytes 6148
  27.2 162.6 %copy-start.8 = (s32[4,32]{1,0:T(4,128)S(1)}, s32[4,32]{1,0:T(4,128)}, u32[]{:S(2)}) copy-start(s32[4,32]{1,0:T(4,128)} %param.13) | copy-start | bytes 1540
  27.2 192.2 %copy-start.3 = (bf16[128,128]{1,0:T(8,128)(2,1)S(1)}, bf16[128,128]{1,0:T(8,128)(2,1)}, u32[]{:S(2)}) copy-start(bf16[128,128]{1,0:T(8,128)(2,1)} %param.11) | copy-start | bytes 98308
  27.2 193.2 %copy-start.7 = (f32[1,1024]{1,0:T(1,128)S(1)}, f32[1,1024]{1,0:T(1,128)}, u32[]{:S(2)}) copy-start(f32[1,1024]{1,0:T(1,128)} %param.16) | copy-start | bytes 12292
  27.3 193.2 %copy-start.9 = (f32[128,1024]{1,0:T(8,128)S(1)}, f32[128,1024]{1,0:T(8,128)}, u32[]{:S(2)}) copy-start(f32[128,1024]{1,0:T(8,128)} %param.17) | copy-start | bytes 1572868
  189.0 0.8 copy-start.1
  220.4 18.8 %copy-start.4 = (s32[2]{0:T(128)S(1)}, s32[2]{0:T(128)}, u32[]{:S(2)}) copy-start(s32[2]{0:T(128)} %constant.362) | copy-start | bytes 28
  220.5 18.8 %copy-start.5 = (s32[2]{0:T(128)S(1)}, s32[2]{0:T(128)}, u32[]{:S(2)}) copy-start(s32[2]{0:T(128)} %constant.361) | copy-start | bytes 28
  239.3 47.1 %copy-start.2 = (f32[128,1,128]{2,0,1:T(8,128)S(1)}, f32[128,1,128]{2,0,1:T(8,128)}, u32[]{:S(2)}) copy-start(f32[128,1,128]{2,0,1:T(8,128)} %reduce-scatter.2.cloned.1.call-done) | copy-start | bytes 196612
  282.8 8.6 %all-to-all-start = ((f32[1,4,64,128]{3,2,0,1:T(8,128)}), f32[1,4,64,128]{3,2,0,1:T(8,128)S(1)}, u32[]{:S(2)}, u32[]{:S(2)}) async-start(f32[1,4,64,128]{3,2,0,1:T(8,128)} %bitcast.22), calls=%async_computation.1 | async-start | bytes 262144 | tf_op jit(solution)/shard_map/all_to_all | solution.py:127
Sparse Core Ops, SparseCore 0:
  189.9 29.4 reduce-scatter.1
where the time goes:
time: 302 us; the launch traced here: 301 us
  local copies, waits for them, and re-layouts  168 us (56%)
  other arithmetic  49.8 us (16%)
  waiting for transfers between devices  33.2 us (11%)
  blocking collectives  29.4 us (10%)
  between operations  14.2 us (5%)
  starting transfers between devices  3.66 us (1%)
    gather x2, local copies, waits for them, and re-layouts, pool_step(): fetched = tables[table_ids, jnp.clip(local, 0, span_rows - 1)]  154 us
    while x8, other arithmetic  34.2 us
    reduce_scatter x1, waiting for transfers between devices, on_device(): lax.psum_scatter(pool_lookups(tables, picked, offset), 'shard', scatter_d...  29 us
    all_gather x1, blocking collectives, on_device(): lax.all_gather(pooled_grad, 'shard', axis=0, tiled=True)  14.9 us
    all_gather x1, blocking collectives, on_device(): group_idx = lax.all_gather(own_rows, 'shard', axis=0, tiled=True)  14.5 us
  transfers between devices with their start and end apart: 2, of which 2 were waited for; matrix products, arithmetic and copies ran while one was open for 0% of the time, Pallas kernels for 0%

commit v1 on v0

--- a/solution.py
+++ b/solution.py
@@ -3,6 +3,8 @@
 import jax
 import jax.numpy as jnp
 from jax import lax
+from jax.experimental import pallas as pl
+from jax.experimental.pallas import tpu as pltpu
 from jax.sharding import PartitionSpec as P
 
 HOT = 64
@@ -67,7 +69,7 @@
     return lax.fori_loop(0, rows_count // rows_block * bag_turns, add_step, running_grad)
 
 
-def on_device(bottom_out, lookups, starts, tables, top_dense, top_pairs, cotangent):
+def by_row_sums(bottom_out, lookups, starts, tables, top_dense, top_pairs, cotangent):
     shard_pos = lax.axis_index("shard")
     grp_pos = lax.axis_index("grp")
     group_count = lax.axis_size("grp")
@@ -132,6 +134,349 @@
     return (activation, bottom_grad, table_grad[:, None])
 
 
+def whole(memory=pltpu.VMEM):
+    return pl.BlockSpec(memory_space=memory)
+
+
+def cost(flops, moved):
+    return pl.CostEstimate(flops=int(flops), bytes_accessed=int(moved), transcendentals=0)
+
+
+def two_terms(values):
+    high = values.astype(jnp.bfloat16)
+    low = (values - high.astype(jnp.float32)).astype(jnp.bfloat16)
+    return high, low
+
+
+def dot_two(counts, values):
+    high, low = two_terms(values)
+    return jnp.dot(counts, high, preferred_element_type=jnp.float32) + jnp.dot(
+        counts, low, preferred_element_type=jnp.float32
+    )
+
+
+def pack_hot(starts, looked, bottom_out, table, group_count):
+    span_rows, width = table.shape
+    win_size = span_rows // group_count
+    samples = bottom_out.shape[0]
+    bag = looked.shape[0]
+    head = min(HOT + 8, win_size)
+
+    def kernel(starts_ref, looked_ref, bottom_ref, table_ref, hot_ref, sent_ref, places_ref, held, sems):
+        grp_pos = lax.axis_index("grp")
+        shard_pos = lax.axis_index("shard")
+        shifts = []
+        copies = []
+        for window in range(group_count):
+            start = starts_ref[grp_pos, shard_pos * group_count + window]
+            aligned = jnp.minimum(start // 8 * 8, win_size - head)
+            shifts.append(start - aligned)
+            base = window * win_size
+            first = pltpu.make_async_copy(
+                table_ref.at[pl.ds(pl.multiple_of(base + aligned, 8), head)],
+                held.at[window, pl.ds(0, head)],
+                sems.at[window, 0],
+            )
+            second = pltpu.make_async_copy(
+                table_ref.at[pl.ds(base, HOT)], held.at[window, pl.ds(head, HOT)], sems.at[window, 1]
+            )
+            first.start()
+            second.start()
+            copies += [first, second]
+        found = looked_ref[...]
+        window_of = jnp.floor((found.astype(jnp.float32) + 0.5) * (1.0 / win_size)).astype(jnp.int32)
+        places = (found - window_of * (win_size - HOT)).astype(jnp.float32)
+        places = jnp.concatenate([places, jnp.zeros((8 - bag, samples), jnp.float32)], axis=0)
+        places_ref[...] = places
+        sent_ref[pl.ds(0, samples), :] = bottom_ref[...].astype(jnp.float32)
+        sent_ref[pl.ds(samples, 8), :] = places
+        for copy in copies:
+            copy.wait()
+        for window in range(group_count):
+            hot_ref[pl.ds(window * HOT, HOT), :] = held[window, pl.ds(shifts[window], HOT), :]
+
+    hot_rows = group_count * HOT
+    return pl.pallas_call(
+        kernel,
+        out_shape=(
+            jax.ShapeDtypeStruct((hot_rows, width), jnp.float32),
+            jax.ShapeDtypeStruct((samples + 8, width), jnp.float32),
+            jax.ShapeDtypeStruct((8, samples), jnp.float32),
+        ),
+        in_specs=[whole(pltpu.SMEM), whole(), whole(), whole(pl.ANY)],
+        out_specs=(whole(), whole(), whole()),
+        scratch_shapes=[
+            pltpu.VMEM((group_count, head + HOT, width), jnp.float32),
+            pltpu.SemaphoreType.DMA((group_count, 2)),
+        ],
+        cost_estimate=cost(1e6, 1e6),
+        name="pack_hot",
+    )(starts, looked, bottom_out, table)
+
+
+def count_rows(places_own, places_other, bottom_out, top_dense, bag, block_rows, steps):
+    samples = bottom_out.shape[0]
+    hidden = top_dense.shape[1]
+
+    def kernel(own_ref, other_ref, bottom_ref, dense_ref, counts_ref, linear_ref):
+        shard_pos = lax.axis_index("shard")
+        rows = lax.broadcasted_iota(jnp.int32, (samples, block_rows), 1).astype(jnp.float32)
+        for part, ref in enumerate((own_ref, other_ref)):
+            padded = jnp.concatenate(
+                [ref[...], jnp.zeros((samples - 8, samples), jnp.float32)], axis=0
+            )
+            columns = padded.T
+            for place, step in enumerate(steps):
+                base = (jnp.bitwise_xor(shard_pos, step) * block_rows).astype(jnp.float32)
+                total = jnp.zeros((samples, block_rows), jnp.float32)
+                for slot in range(bag):
+                    total += jnp.where(columns[:, slot : slot + 1] - base == rows, 1.0, 0.0)
+                counts_ref[
+                    pl.ds(part * samples, samples), pl.ds(place * block_rows, block_rows)
+                ] = total.astype(jnp.bfloat16)
+        linear_ref[...] = jnp.dot(bottom_ref[...], dense_ref[...], preferred_element_type=jnp.float32)
+
+    return pl.pallas_call(
+        kernel,
+        out_shape=(
+            jax.ShapeDtypeStruct((2 * samples, len(steps) * block_rows), jnp.bfloat16),
+            jax.ShapeDtypeStruct((samples, hidden), jnp.float32),
+        ),
+        in_specs=[whole()] * 4,
+        out_specs=(whole(), whole()),
+        cost_estimate=cost(3e7, 1e6),
+        name="count_rows",
+    )(places_own, places_other, bottom_out, top_dense)
+
+
+def pool_hot(counts, blocks):
+    block_rows, width = blocks[0].shape
+    samples = counts.shape[0] // 2
+
+    def kernel(counts_ref, *refs):
+        block_refs = refs[: len(blocks)]
+        own_ref, other_ref = refs[len(blocks) :]
+        total = jnp.zeros((2 * samples, width), jnp.float32)
+        for place, ref in enumerate(block_refs):
+            total += dot_two(counts_ref[:, pl.ds(place * block_rows, block_rows)], ref[...])
+        own_ref[...] = total[:samples]
+        other_ref[...] = total[samples:]
+
+    part = jax.ShapeDtypeStruct((samples, width), jnp.float32)
+    return pl.pallas_call(
+        kernel,
+        out_shape=(part, part),
+        in_specs=[whole()] * (1 + len(blocks)),
+        out_specs=(whole(), whole()),
+        cost_estimate=cost(1e8, 1e6),
+        name="pool_hot",
+    )(counts, *blocks)
+
+
+def head_terms(pooled, bottom_ref, linear_ref, pairs_ref, cot_ref):
+    dots = jnp.sum(bottom_ref[...].astype(jnp.float32) * pooled, axis=1, keepdims=True)
+    preact = linear_ref[...] + dots * pairs_ref[...]
+    sig = 1.0 / (1.0 + jnp.exp(-preact))
+    pre_grad = cot_ref[...] * sig * (1.0 + preact * (1.0 - sig))
+    pair_grad = jnp.sum(pre_grad * pairs_ref[...], axis=1, keepdims=True)
+    return preact, sig, pre_grad, pair_grad
+
+
+def score(part_own, part_other, bottom_out, linear, top_pairs, cotangent):
+    samples, width = bottom_out.shape
+
+    def kernel(own_ref, other_ref, bottom_ref, linear_ref, pairs_ref, cot_ref, row_ref, pooled_ref):
+        pooled = own_ref[...] + other_ref[...]
+        pooled_ref[...] = pooled
+        pair_grad = head_terms(pooled, bottom_ref, linear_ref, pairs_ref, cot_ref)[3]
+        down = lax.broadcasted_iota(jnp.int32, (samples, samples), 0)
+        across = lax.broadcasted_iota(jnp.int32, (samples, samples), 1)
+        row_ref[...] = jnp.sum(jnp.where(down == across, pair_grad, 0.0), axis=0, keepdims=True)
+
+    return pl.pallas_call(
+        kernel,
+        out_shape=(
+            jax.ShapeDtypeStruct((1, samples), jnp.float32),
+            jax.ShapeDtypeStruct((samples, width), jnp.float32),
+        ),
+        in_specs=[whole()] * 6,
+        out_specs=(whole(), whole()),
+        cost_estimate=cost(1e7, 1e6),
+        name="score",
+    )(part_own, part_other, bottom_out, linear, top_pairs, cotangent)
+
+
+def finish_dense(pooled, bottom_out, linear, top_pairs, cotangent, top_dense):
+    samples, width = bottom_out.shape
+    hidden = top_dense.shape[1]
+
+    def kernel(pooled_ref, bottom_ref, linear_ref, pairs_ref, cot_ref, dense_ref, act_ref, grad_ref):
+        pooled = pooled_ref[...]
+        preact, sig, pre_grad, pair_grad = head_terms(pooled, bottom_ref, linear_ref, pairs_ref, cot_ref)
+        act_ref[...] = (preact * sig).astype(jnp.bfloat16)
+        grad_ref[...] = (
+            lax.dot_general(
+                pre_grad.astype(jnp.bfloat16),
+                dense_ref[...],
+                (((1,), (1,)), ((), ())),
+                preferred_element_type=jnp.float32,
+            )
+            + pair_grad * pooled
+        )
+
+    return pl.pallas_call(
+        kernel,
+        out_shape=(
+            jax.ShapeDtypeStruct((samples, hidden), jnp.bfloat16),
+            jax.ShapeDtypeStruct((samples, width), jnp.float32),
+        ),
+        in_specs=[whole()] * 6,
+        out_specs=(whole(), whole()),
+        cost_estimate=cost(5e7, 1e6),
+        name="finish_dense",
+    )(pooled, bottom_out, linear, top_pairs, cotangent, top_dense)
+
+
+def row_grads(scores, sent, bag, block_rows):
+    samples = scores[0].shape[1]
+    width = sent[0].shape[1]
+    count = len(scores)
+
+    def kernel(*refs):
+        score_refs = refs[:count]
+        sent_refs = refs[count : 2 * count]
+        own_ref, other_ref = refs[2 * count :]
+        shard_pos = lax.axis_index("shard")
+        rows = lax.broadcasted_iota(jnp.int32, (block_rows, samples), 0).astype(jnp.float32)
+        for side, out_ref in ((1, other_ref), (0, own_ref)):
+            base = (jnp.bitwise_xor(shard_pos, side) * block_rows).astype(jnp.float32)
+            total = jnp.zeros((block_rows, width), jnp.float32)
+            for score_ref, sent_ref in zip(score_refs, sent_refs):
+                places = sent_ref[pl.ds(samples, 8), :] - base
+                times = jnp.zeros((block_rows, samples), jnp.float32)
+                for slot in range(bag):
+                    times += jnp.where(places[slot : slot + 1, :] == rows, 1.0, 0.0)
+                high, low = two_terms(times * score_ref[...])
+                bottom = sent_ref[pl.ds(0, samples), :].astype(jnp.bfloat16)
+                total += jnp.dot(high, bottom, preferred_element_type=jnp.float32)
+                total += jnp.dot(low, bottom, preferred_element_type=jnp.float32)
+            out_ref[...] = total
+
+    part = jax.ShapeDtypeStruct((block_rows, width), jnp.float32)
+    return pl.pallas_call(
+        kernel,
+        out_shape=(part, part),
+        in_specs=[whole()] * (2 * count),
+        out_specs=(whole(), whole()),
+        cost_estimate=cost(2e8, 1e6),
+        name="row_grads",
+    )(*scores, *sent)
+
+
+def split_owners(grad_own, grad_other, group_count):
+    width = grad_own.shape[1]
+
+    def kernel(own_ref, other_ref, *out_refs):
+        grp_pos = lax.axis_index("grp")
+        for step, out_ref in enumerate(out_refs):
+            first = pl.multiple_of(jnp.bitwise_xor(grp_pos, step) * HOT, HOT)
+            out_ref[...] = own_ref[pl.ds(first, HOT), :] + other_ref[pl.ds(first, HOT), :]
+
+    part = jax.ShapeDtypeStruct((HOT, width), jnp.float32)
+    return pl.pallas_call(
+        kernel,
+        out_shape=(part,) * group_count,
+        in_specs=[whole()] * 2,
+        out_specs=(whole(),) * group_count,
+        cost_estimate=cost(1e6, 1e6),
+        name="split_owners",
+    )(grad_own, grad_other)
+
+
+def place_rows(starts, blocks, win_size):
+    width = blocks[0].shape[1]
+    count = len(blocks)
+
+    def kernel(starts_ref, *refs):
+        block_refs = refs[:count]
+        out_ref, held, sem = refs[count:]
+        grp_pos = lax.axis_index("grp")
+        column = lax.axis_index("shard") * count + grp_pos
+        held[...] = jnp.zeros_like(held)
+        for step, ref in enumerate(block_refs):
+            start = starts_ref[jnp.bitwise_xor(grp_pos, step), column]
+            held[pl.ds(start, HOT), :] += ref[...]
+        held[pl.ds(0, HOT), :] += held[pl.ds(win_size, HOT), :]
+        copy = pltpu.make_async_copy(held.at[pl.ds(0, win_size)], out_ref, sem)
+        copy.start()
+        copy.wait()
+
+    return pl.pallas_call(
+        kernel,
+        out_shape=jax.ShapeDtypeStruct((win_size, width), jnp.float32),
+        in_specs=[whole(pltpu.SMEM)] + [whole()] * count,
+        out_specs=whole(pl.ANY),
+        scratch_shapes=[pltpu.VMEM((win_size + HOT, width), jnp.float32), pltpu.SemaphoreType.DMA],
+        cost_estimate=cost(1e6, 2e6),
+        name="place_rows",
+    )(starts, *blocks)
+
+
+def by_hot_rows(bottom_out, lookups, starts, tables, top_dense, top_pairs, cotangent):
+    group_count = lax.axis_size("grp")
+    shard_count = lax.axis_size("shard")
+    bag = lookups.shape[2]
+    win_size = tables.shape[1] // group_count
+    block_rows = group_count * HOT
+
+    def across(axis, values, step):
+        size = lax.axis_size(axis)
+        return lax.ppermute(values, axis, [(pos, pos ^ step) for pos in range(size)])
+
+    steps = list(range(0, shard_count, 2))
+    looked = lookups[:, 0, :].T
+    hot, sent, places = pack_hot(starts, looked, bottom_out, tables[0], group_count)
+    places_other = across("shard", places, 1)
+    hot_blocks = [hot] + [across("shard", hot, step) for step in steps[1:]]
+    sent_blocks = [sent] + [across("shard", sent, step) for step in steps[1:]]
+    counts, linear = count_rows(places, places_other, bottom_out, top_dense, bag, block_rows, steps)
+    part_own, part_other = pool_hot(counts, hot_blocks)
+    part_back = across("shard", part_other, 1)
+    score_row, pooled = score(part_own, part_back, bottom_out, linear, top_pairs, cotangent)
+    scores = [score_row] + [across("shard", score_row, step) for step in steps[1:]]
+    activation, bottom_grad = finish_dense(
+        pooled, bottom_out, linear, top_pairs, cotangent, top_dense
+    )
+    grad_own, grad_other = row_grads(scores, sent_blocks, bag, block_rows)
+    grad_back = across("shard", grad_other, 1)
+    owned = split_owners(grad_own, grad_back, group_count)
+    blocks = [owned[0]] + [across("grp", owned[step], step) for step in range(1, group_count)]
+    table_grad = place_rows(starts, blocks, win_size)
+    return activation, bottom_grad, table_grad[None, None]
+
+
+def is_power(number):
+    return number & (number - 1) == 0
+
+
+def on_device(bottom_out, lookups, starts, tables, top_dense, top_pairs, cotangent):
+    group_count = lax.axis_size("grp")
+    shard_count = lax.axis_size("shard")
+    group_lookups = lookups.shape[0] * lookups.shape[2] * shard_count
+    hot_rows = group_count * HOT * shard_count
+    fits = (
+        tables.shape[0] == 1
+        and lookups.shape[2] <= 8
+        and bottom_out.shape[0] == tables.shape[2]
+        and is_power(group_count)
+        and is_power(shard_count)
+        and tables.shape[1] // group_count % 8 == 0
+        and hot_rows <= group_lookups
+    )
+    plan = by_hot_rows if fits else by_row_sums
+    return plan(bottom_out, lookups, starts, tables, top_dense, top_pairs, cotangent)
+
+
 def solution(mesh):
     in_specs = (
         P(("grp", "shard"), None),

time: 302 us -> 57.2 us (0.19)
  local copies, waits for them, and re-layouts: 168 us -> 3.15 us
  other arithmetic: 49.8 us -> 0 us
  blocking collectives: 29.4 us -> 0 us
  waiting for transfers between devices: 33.2 us -> 14.5 us
  Pallas kernels: 0 us -> 18 us
  starting transfers between devices: 3.66 us -> 20.3 us
  between operations: 14.2 us -> 0.74 us
    gather x6 -> x0, local copies, waits for them, and re-layouts: 161 us -> none  [the longest x2 154 us: pool_step(): fetched = tables[table_ids, jnp.clip(local, 0, span_rows - 1)]]
    while x8 -> x0, other arithmetic: 34.2 us -> none
    all_gather x2 -> x0, blocking collectives: 29.4 us -> none  [the longest x1 14.9 us: on_device(): lax.all_gather(pooled_grad, 'shard', axis=0, tiled=True)]
    reduce_scatter x1 -> x0, waiting for transfers between devices: 29 us -> none  [on_device(): lax.psum_scatter(pool_lookups(tables, picked, offset), 'shard', scatter_d...]
    ppermute x0 -> x15, starting transfers between devices: none -> 20.3 us  [across(): lax.ppermute(values, axis, [(pos, pos ^ step) for pos in range(size)])]
    pallas_call x0 -> x8, Pallas kernels: none -> 18 us  [the longest x1 2.66 us: count_rows(): pl.pallas_call(kernel, out_shape=(jax.ShapeDtypeStruct((2 * samples, len(...]
    ppermute x0 -> x15, waiting for transfers between devices: none -> 14.5 us  [across(): lax.ppermute(values, axis, [(pos, pos ^ step) for pos in range(size)])]
    reduce_sum x3 -> x0, other arithmetic: 6.79 us -> none  [the longest x2 5.84 us: pool_step(): summed = jnp.sum(jnp.where(inside[..., None], fetched, 0.0), axis=2)]
  transfers between devices with their start and end apart: 2 -> 15, of which waited for: 2 -> 7; matrix products, arithmetic and copies ran while one was open for 0% -> 0% of each run, Pallas kernels for 0% -> 17%
where the time goes in v1:
time: 57.2 us; the launch traced here: 56.7 us
  starting transfers between devices  20.3 us (35%)
  Pallas kernels  18 us (31%)
  waiting for transfers between devices  14.5 us (25%)
  local copies, waits for them, and re-layouts  3.15 us (6%)
  between operations  0.74 us (1%)
    ppermute x15, starting transfers between devices, across(): lax.ppermute(values, axis, [(pos, pos ^ step) for pos in range(size)])  20.3 us
    ppermute x15, waiting for transfers between devices, across(): lax.ppermute(values, axis, [(pos, pos ^ step) for pos in range(size)])  14.5 us
    unnamed x30, local copies, waits for them, and re-layouts  3.15 us
    pallas_call x1, Pallas kernels, count_rows(): pl.pallas_call(kernel, out_shape=(jax.ShapeDtypeStruct((2 * samples, len(...  2.66 us
    pallas_call x1, Pallas kernels, finish_dense(): pl.pallas_call(kernel, out_shape=(jax.ShapeDtypeStruct((samples, hidden),...  2.48 us
    pallas_call x1, Pallas kernels, pack_hot(): pl.pallas_call(kernel, out_shape=(jax.ShapeDtypeStruct((hot_rows, width),...  2.44 us
    pallas_call x1, Pallas kernels, row_grads(): pl.pallas_call(kernel, out_shape=(part, part), in_specs=[whole()] * (2 *...  2.42 us
    pallas_call x1, Pallas kernels, pool_hot(): pl.pallas_call(kernel, out_shape=(part, part), in_specs=[whole()] * (1 +...  2.27 us
  transfers between devices with their start and end apart: 15, of which 7 were waited for; matrix products, arithmetic and copies ran while one was open for 0% of the time, Pallas kernels for 17%

profile of v1, /device:TPU:0, one launch (start us, length us, event | category | flops | bytes accessed | tf_op | source)
XLA Modules:
  0.0 56.7 jit_solution(10481598829811292688)
XLA Ops:
  0.6 2.4 %pack_hot.1 = (f32[256,128]{1,0:T(8,128)}, f32[136,128]{1,0:T(8,128)}, f32[8,128]{1,0:T(8,128)}) custom-call(s32[4,32]{1,0:T(4,128)} %starts_ref.3, s32[4,128]{1,0:T(4,128)} %bitcast.7, bf16[128,128]{1,0:T(8,128)(2,1)} %bottom_ref.7, f32[7872,128]{1,0:T(8,128)} %bitcast.5), custom_call_target="tpu_custom_call" | custom-call | flops 1000000 | bytes 1000000 | tf_op jit(solution)/shard_map/pack_hot/pallas_call | solution.py:199
  3.1 3.1 %collective-permute-start.1 = (f32[256,128]{1,0:T(8,128)}, f32[256,128]{1,0:T(8,128)S(1)}, u32[]{:S(2)}, u32[]{:S(2)}) collective-permute-start(f32[256,128]{1,0:T(8,128)} %get-tuple-element.22.refs_0_), channel_id=1, source_target_pairs={{0,2},{1,3},{2,0},{3,1},{4,6},{5,7},{6,4},{7,5},{8,10},{9,11},{10,... | collective-permute-start | bytes 393224 | tf_op jit(solution)/shard_map/ppermute | solution.py:434
  6.2 2.6 %collective-permute-start.2 = (f32[256,128]{1,0:T(8,128)}, f32[256,128]{1,0:T(8,128)S(1)}, u32[]{:S(2)}, u32[]{:S(2)}) collective-permute-start(f32[256,128]{1,0:T(8,128)} %get-tuple-element.22.refs_0_), channel_id=1, source_target_pairs={{0,4},{1,5},{2,6},{3,7},{4,0},{5,1},{6,2},{7,3},{8,12},{9,13},{10,... | collective-permute-start | bytes 393224 | tf_op jit(solution)/shard_map/ppermute | solution.py:434
  8.8 0.9 %collective-permute-start.8 = (f32[136,128]{1,0:T(8,128)}, f32[136,128]{1,0:T(8,128)S(1)}, u32[]{:S(2)}, u32[]{:S(2)}) collective-permute-start(f32[136,128]{1,0:T(8,128)} %get-tuple-element.30.refs_4_), channel_id=1, source_target_pairs={{0,2},{1,3},{2,0},{3,1},{4,6},{5,7},{6,4},{7,5},{8,10},{9,11},{10,... | collective-permute-start | bytes 208904 | tf_op jit(solution)/shard_map/ppermute | solution.py:434
  10.2 3.0 %collective-permute-start.9 = (f32[136,128]{1,0:T(8,128)}, f32[136,128]{1,0:T(8,128)S(1)}, u32[]{:S(2)}, u32[]{:S(2)}) collective-permute-start(f32[136,128]{1,0:T(8,128)} %get-tuple-element.30.refs_4_), channel_id=1, source_target_pairs={{0,4},{1,5},{2,6},{3,7},{4,0},{5,1},{6,2},{7,3},{8,12},{9,13},{10,... | collective-permute-start | bytes 208904 | tf_op jit(solution)/shard_map/ppermute | solution.py:434
  13.2 2.7 %count_rows.1 = (bf16[256,1024]{1,0:T(8,128)(2,1)}, f32[128,1024]{1,0:T(8,128)}) custom-call(f32[8,128]{1,0:T(8,128)} %get-tuple-element.20.own_ref, f32[8,128]{1,0:T(8,128)} %copy-done.8, bf16[128,128]{1,0:T(8,128)(2,1)} %bottom_ref.7, bf16[128,1024]{1,0:T(8,128)(2,1)} %dense_ref.3), custom_call_target="tpu_custom_call" | custom-call | flops 30000000 | bytes 1000000 | tf_op jit(solution)/shard_map/count_rows/pallas_call | solution.py:239
  15.9 1.5 %collective-permute-start.10 = (f32[136,128]{1,0:T(8,128)}, f32[136,128]{1,0:T(8,128)S(1)}, u32[]{:S(2)}, u32[]{:S(2)}) collective-permute-start(f32[136,128]{1,0:T(8,128)} %get-tuple-element.30.refs_4_), channel_id=1, source_target_pairs={{0,6},{1,7},{2,4},{3,5},{4,2},{5,3},{6,0},{7,1},{8,14},{9,15},{10,... | collective-permute-start | bytes 208904 | tf_op jit(solution)/shard_map/ppermute | solution.py:434
  17.3 5.0 %collective-permute-done.2.refs_2_ = f32[256,128]{1,0:T(8,128)S(1)} collective-permute-done((f32[256,128]{1,0:T(8,128)}, f32[256,128]{1,0:T(8,128)S(1)}, u32[]{:S(2)}, u32[]{:S(2)}) %collective-permute-start.2) | collective-permute-done | bytes 131104 | tf_op jit(solution)/shard_map/ppermute | solution.py:434
  23.0 2.3 %pool_hot.1 = (f32[128,128]{1,0:T(8,128)}, f32[128,128]{1,0:T(8,128)}) custom-call(bf16[256,1024]{1,0:T(8,128)(2,1)} %get-tuple-element.21.counts_ref, f32[256,128]{1,0:T(8,128)} %get-tuple-element.22.refs_0_, f32[256,128]{1,0:T(8,128)} %copy-done.1, f32[256,128]{1,0:T(8,128)} %copy-done.2, f32[256,128]{1,0:T(8,128)} %copy-done.3), custom_call_target="tpu_custom_call" | custom-call | flops 100000000 | bytes 1000000 | tf_op jit(solution)/shard_map/pool_hot/pallas_call | solution.py:266
  25.3 1.5 %collective-permute-done.4.other_ref = f32[128,128]{1,0:T(8,128)S(1)} collective-permute-done((f32[128,128]{1,0:T(8,128)}, f32[128,128]{1,0:T(8,128)S(1)}, u32[]{:S(2)}, u32[]{:S(2)}) %collective-permute-start.4) | collective-permute-done | bytes 65568 | tf_op jit(solution)/shard_map/ppermute | solution.py:434
  27.4 2.2 %score.1 = (f32[1,128]{1,0:T(1,128)}, f32[128,128]{1,0:T(8,128)}) custom-call(f32[128,128]{1,0:T(8,128)} %get-tuple-element.23.own_ref, f32[128,128]{1,0:T(8,128)} %copy-done.4, bf16[128,128]{1,0:T(8,128)(2,1)} %bottom_ref.7, f32[128,1024]{1,0:T(8,128)} %get-tuple-element.25.linear_ref, f32[1,1024]{1,0:T(1,128)} %pairs_ref.3, f32[128,1024]{1,0:T(8,128)} %cot_ref.3), custom_call_target="tpu_custom_call" | custom-call | flops 10000000 | bytes 1000000 | tf_op jit(solution)/shard_map/score/pallas_call | solution.py:296
  29.6 3.3 %collective-permute-start.5 = (f32[1,128]{1,0:T(1,128)}, f32[1,128]{1,0:T(1,128)S(1)}, u32[]{:S(2)}, u32[]{:S(2)}) collective-permute-start(f32[1,128]{1,0:T(1,128)} %get-tuple-element.29.refs_0_), channel_id=1, source_target_pairs={{0,2},{1,3},{2,0},{3,1},{4,6},{5,7},{6,4},{7,5},{8,10},{9,11},{10,... | collective-permute-start | bytes 1544 | tf_op jit(solution)/shard_map/ppermute | solution.py:434
  32.9 0.9 %collective-permute-start.6 = (f32[1,128]{1,0:T(1,128)}, f32[1,128]{1,0:T(1,128)S(1)}, u32[]{:S(2)}, u32[]{:S(2)}) collective-permute-start(f32[1,128]{1,0:T(1,128)} %get-tuple-element.29.refs_0_), channel_id=1, source_target_pairs={{0,4},{1,5},{2,6},{3,7},{4,0},{5,1},{6,2},{7,3},{8,12},{9,13},{10,... | collective-permute-start | bytes 1544 | tf_op jit(solution)/shard_map/ppermute | solution.py:434
  33.8 1.5 %collective-permute-start.7 = (f32[1,128]{1,0:T(1,128)}, f32[1,128]{1,0:T(1,128)S(1)}, u32[]{:S(2)}, u32[]{:S(2)}) collective-permute-start(f32[1,128]{1,0:T(1,128)} %get-tuple-element.29.refs_0_), channel_id=1, source_target_pairs={{0,6},{1,7},{2,4},{3,5},{4,2},{5,3},{6,0},{7,1},{8,14},{9,15},{10,... | collective-permute-start | bytes 1544 | tf_op jit(solution)/shard_map/ppermute | solution.py:434
  35.3 2.2 %collective-permute-done.6.refs_2_ = f32[1,128]{1,0:T(1,128)S(1)} collective-permute-done((f32[1,128]{1,0:T(1,128)}, f32[1,128]{1,0:T(1,128)S(1)}, u32[]{:S(2)}, u32[]{:S(2)}) %collective-permute-start.6) | collective-permute-done | bytes 544 | tf_op jit(solution)/shard_map/ppermute | solution.py:434
  37.6 1.8 %collective-permute-done.7.refs_3_ = f32[1,128]{1,0:T(1,128)S(1)} collective-permute-done((f32[1,128]{1,0:T(1,128)}, f32[1,128]{1,0:T(1,128)S(1)}, u32[]{:S(2)}, u32[]{:S(2)}) %collective-permute-start.7) | collective-permute-done | bytes 544 | tf_op jit(solution)/shard_map/ppermute | solution.py:434
  39.9 2.4 %row_grads.1 = (f32[256,128]{1,0:T(8,128)}, f32[256,128]{1,0:T(8,128)}) custom-call(f32[1,128]{1,0:T(1,128)} %get-tuple-element.29.refs_0_, f32[1,128]{1,0:T(1,128)} %copy-done.12, f32[1,128]{1,0:T(1,128)} %copy-done.13, f32[1,128]{1,0:T(1,128)} %copy-done.14, f32[136,128]{1,0:T(8,128)} %get-tuple-element.30.refs_4_, f32[136,128]{1,0:T(8,128)} %copy-done.9, ...), custom_call_target="tpu_custom_call" | custom-call | flops 200000000 | bytes 1000000 | tf_op jit(solution)/shard_map/row_grads/pallas_call | solution.py:366
  42.3 1.6 %collective-permute-done.11.other_ref = f32[256,128]{1,0:T(8,128)S(1)} collective-permute-done((f32[256,128]{1,0:T(8,128)}, f32[256,128]{1,0:T(8,128)S(1)}, u32[]{:S(2)}, u32[]{:S(2)}) %collective-permute-start.11) | collective-permute-done | bytes 131104 | tf_op jit(solution)/shard_map/ppermute | solution.py:434
  44.5 1.6 %split_owners.1 = (f32[64,128]{1,0:T(8,128)}, f32[64,128]{1,0:T(8,128)}, f32[64,128]{1,0:T(8,128)}, f32[64,128]{1,0:T(8,128)}) custom-call(f32[256,128]{1,0:T(8,128)} %get-tuple-element.31.own_ref, f32[256,128]{1,0:T(8,128)} %copy-done), custom_call_target="tpu_custom_call" | custom-call | flops 1000000 | bytes 1000000 | tf_op jit(solution)/shard_map/split_owners/pallas_call | solution.py:386
  46.2 1.5 %collective-permute-start.12 = (f32[64,128]{1,0:T(8,128)}, f32[64,128]{1,0:T(8,128)S(1)}, u32[]{:S(2)}, u32[]{:S(2)}) collective-permute-start(f32[64,128]{1,0:T(8,128)} %get-tuple-element.34), channel_id=1, source_target_pairs={{0,8},{8,0},{16,24},{24,16},{1,9},{9,1},{17,25},{25,17},{2,10},{10... | collective-permute-start | bytes 98312 | tf_op jit(solution)/shard_map/ppermute | solution.py:434
  47.7 1.5 %collective-permute-start.13 = (f32[64,128]{1,0:T(8,128)}, f32[64,128]{1,0:T(8,128)S(1)}, u32[]{:S(2)}, u32[]{:S(2)}) collective-permute-start(f32[64,128]{1,0:T(8,128)} %get-tuple-element.35), channel_id=1, source_target_pairs={{0,16},{8,24},{16,0},{24,8},{1,17},{9,25},{17,1},{25,9},{2,18},{10... | collective-permute-start | bytes 98312 | tf_op jit(solution)/shard_map/ppermute | solution.py:434
  49.7 2.5 %finish_dense.1 = (bf16[128,1024]{1,0:T(8,128)(2,1)}, f32[128,128]{1,0:T(8,128)}) custom-call(f32[128,128]{1,0:T(8,128)} %get-tuple-element.26.pooled_ref, bf16[128,128]{1,0:T(8,128)(2,1)} %bottom_ref.7, f32[128,1024]{1,0:T(8,128)} %get-tuple-element.25.linear_ref, f32[1,1024]{1,0:T(1,128)} %pairs_ref.3, f32[128,1024]{1,0:T(8,128)} %cot_ref.3, ...), custom_call_target="tpu_custom_call" | custom-call | flops 50000000 | bytes 1000000 | tf_op jit(solution)/shard_map/finish_dense/pallas_call | solution.py:327
  52.2 2.0 %collective-permute-done.14.refs_3_ = f32[64,128]{1,0:T(8,128)S(1)} collective-permute-done((f32[64,128]{1,0:T(8,128)}, f32[64,128]{1,0:T(8,128)S(1)}, u32[]{:S(2)}, u32[]{:S(2)}) %collective-permute-start.14) | collective-permute-done | bytes 32800 | tf_op jit(solution)/shard_map/ppermute | solution.py:434
  54.8 1.9 %place_rows.1 = f32[1968,128]{1,0:T(8,128)} custom-call(s32[4,32]{1,0:T(4,128)} %starts_ref.3, f32[64,128]{1,0:T(8,128)} %get-tuple-element.33.refs_0_, f32[64,128]{1,0:T(8,128)} %copy-done.5, f32[64,128]{1,0:T(8,128)} %copy-done.6, f32[64,128]{1,0:T(8,128)} %copy-done.7), custom_call_target="tpu_custom_call" | custom-call | flops 1000000 | bytes 2000000 | tf_op jit(solution)/shard_map/place_rows/pallas_call | solution.py:414
  (44 shorter events, 4.1 us)
Async XLA Ops:
  3.1 12.8 %collective-permute-start.1 = (f32[256,128]{1,0:T(8,128)}, f32[256,128]{1,0:T(8,128)S(1)}, u32[]{:S(2)}, u32[]{:S(2)}) collective-permute-start(f32[256,128]{1,0:T(8,128)} %get-tuple-element.22.refs_0_), channel_id=1, source_target_pairs={{0,2},{1,3},{2,0},{3,1},{4,6},{5,7},{6,4},{7,5},{8,10},{9,11},{10,... | collective-permute-start | bytes 393224 | tf_op jit(solution)/shard_map/ppermute | solution.py:434
  6.2 16.1 %collective-permute-start.2 = (f32[256,128]{1,0:T(8,128)}, f32[256,128]{1,0:T(8,128)S(1)}, u32[]{:S(2)}, u32[]{:S(2)}) collective-permute-start(f32[256,128]{1,0:T(8,128)} %get-tuple-element.22.refs_0_), channel_id=1, source_target_pairs={{0,4},{1,5},{2,6},{3,7},{4,0},{5,1},{6,2},{7,3},{8,12},{9,13},{10,... | collective-permute-start | bytes 393224 | tf_op jit(solution)/shard_map/ppermute | solution.py:434
  8.8 13.5 %collective-permute-start.3 = (f32[256,128]{1,0:T(8,128)}, f32[256,128]{1,0:T(8,128)S(1)}, u32[]{:S(2)}, u32[]{:S(2)}) collective-permute-start(f32[256,128]{1,0:T(8,128)} %get-tuple-element.22.refs_0_), channel_id=1, source_target_pairs={{0,6},{1,7},{2,4},{3,5},{4,2},{5,3},{6,0},{7,1},{8,14},{9,15},{10,... | collective-permute-start | bytes 393224 | tf_op jit(solution)/shard_map/ppermute | solution.py:434
  8.8 1.4 %collective-permute-start = (f32[8,128]{1,0:T(8,128)}, f32[8,128]{1,0:T(8,128)S(1)}, u32[]{:S(2)}, u32[]{:S(2)}) collective-permute-start(f32[8,128]{1,0:T(8,128)} %get-tuple-element.20.own_ref), channel_id=1, source_target_pairs={{0,1},{1,0},{2,3},{3,2},{4,5},{5,4},{6,7},{7,6},{8,9},{9,8},{10,11... | collective-permute-start | bytes 12296 | tf_op jit(solution)/shard_map/ppermute | solution.py:434
  8.8 25.0 %collective-permute-start.8 = (f32[136,128]{1,0:T(8,128)}, f32[136,128]{1,0:T(8,128)S(1)}, u32[]{:S(2)}, u32[]{:S(2)}) collective-permute-start(f32[136,128]{1,0:T(8,128)} %get-tuple-element.30.refs_4_), channel_id=1, source_target_pairs={{0,2},{1,3},{2,0},{3,1},{4,6},{5,7},{6,4},{7,5},{8,10},{9,11},{10,... | collective-permute-start | bytes 208904 | tf_op jit(solution)/shard_map/ppermute | solution.py:434
  10.2 3.0 %copy-start.8 = (f32[8,128]{1,0:T(8,128)}, f32[8,128]{1,0:T(8,128)S(1)}, u32[]{:S(2)}) copy-start(f32[8,128]{1,0:T(8,128)S(1)} %collective-permute-done.other_ref) | copy-start | bytes 12292
  10.2 25.1 %collective-permute-start.9 = (f32[136,128]{1,0:T(8,128)}, f32[136,128]{1,0:T(8,128)S(1)}, u32[]{:S(2)}, u32[]{:S(2)}) collective-permute-start(f32[136,128]{1,0:T(8,128)} %get-tuple-element.30.refs_4_), channel_id=1, source_target_pairs={{0,4},{1,5},{2,6},{3,7},{4,0},{5,1},{6,2},{7,3},{8,12},{9,13},{10,... | collective-permute-start | bytes 208904 | tf_op jit(solution)/shard_map/ppermute | solution.py:434
  15.9 6.4 %copy-start.1 = (f32[256,128]{1,0:T(8,128)}, f32[256,128]{1,0:T(8,128)S(1)}, u32[]{:S(2)}) copy-start(f32[256,128]{1,0:T(8,128)S(1)} %collective-permute-done.1.refs_1_) | copy-start | bytes 393220
  15.9 19.4 %collective-permute-start.10 = (f32[136,128]{1,0:T(8,128)}, f32[136,128]{1,0:T(8,128)S(1)}, u32[]{:S(2)}, u32[]{:S(2)}) collective-permute-start(f32[136,128]{1,0:T(8,128)} %get-tuple-element.30.refs_4_), channel_id=1, source_target_pairs={{0,6},{1,7},{2,4},{3,5},{4,2},{5,3},{6,0},{7,1},{8,14},{9,15},{10,... | collective-permute-start | bytes 208904 | tf_op jit(solution)/shard_map/ppermute | solution.py:434
  25.3 1.5 %collective-permute-start.4 = (f32[128,128]{1,0:T(8,128)}, f32[128,128]{1,0:T(8,128)S(1)}, u32[]{:S(2)}, u32[]{:S(2)}) collective-permute-start(f32[128,128]{1,0:T(8,128)} %get-tuple-element.24), channel_id=1, source_target_pairs={{0,1},{1,0},{2,3},{3,2},{4,5},{5,4},{6,7},{7,6},{8,9},{9,8},{10,11... | collective-permute-start | bytes 196616 | tf_op jit(solution)/shard_map/ppermute | solution.py:434
  29.6 5.7 %collective-permute-start.5 = (f32[1,128]{1,0:T(1,128)}, f32[1,128]{1,0:T(1,128)S(1)}, u32[]{:S(2)}, u32[]{:S(2)}) collective-permute-start(f32[1,128]{1,0:T(1,128)} %get-tuple-element.29.refs_0_), channel_id=1, source_target_pairs={{0,2},{1,3},{2,0},{3,1},{4,6},{5,7},{6,4},{7,5},{8,10},{9,11},{10,... | collective-permute-start | bytes 1544 | tf_op jit(solution)/shard_map/ppermute | solution.py:434
  32.9 4.7 %collective-permute-start.6 = (f32[1,128]{1,0:T(1,128)}, f32[1,128]{1,0:T(1,128)S(1)}, u32[]{:S(2)}, u32[]{:S(2)}) collective-permute-start(f32[1,128]{1,0:T(1,128)} %get-tuple-element.29.refs_0_), channel_id=1, source_target_pairs={{0,4},{1,5},{2,6},{3,7},{4,0},{5,1},{6,2},{7,3},{8,12},{9,13},{10,... | collective-permute-start | bytes 1544 | tf_op jit(solution)/shard_map/ppermute | solution.py:434
  33.8 5.6 %copy-start.9 = (f32[136,128]{1,0:T(8,128)}, f32[136,128]{1,0:T(8,128)S(1)}, u32[]{:S(2)}) copy-start(f32[136,128]{1,0:T(8,128)S(1)} %collective-permute-done.8.refs_5_) | copy-start | bytes 208900
  33.8 5.6 %collective-permute-start.7 = (f32[1,128]{1,0:T(1,128)}, f32[1,128]{1,0:T(1,128)S(1)}, u32[]{:S(2)}, u32[]{:S(2)}) collective-permute-start(f32[1,128]{1,0:T(1,128)} %get-tuple-element.29.refs_0_), channel_id=1, source_target_pairs={{0,6},{1,7},{2,4},{3,5},{4,2},{5,3},{6,0},{7,1},{8,14},{9,15},{10,... | collective-permute-start | bytes 1544 | tf_op jit(solution)/shard_map/ppermute | solution.py:434
  35.3 4.0 %copy-start.10 = (f32[136,128]{1,0:T(8,128)}, f32[136,128]{1,0:T(8,128)S(1)}, u32[]{:S(2)}) copy-start(f32[136,128]{1,0:T(8,128)S(1)} %collective-permute-done.9.refs_6_) | copy-start | bytes 208900
  35.3 4.0 %copy-start.11 = (f32[136,128]{1,0:T(8,128)}, f32[136,128]{1,0:T(8,128)S(1)}, u32[]{:S(2)}) copy-start(f32[136,128]{1,0:T(8,128)S(1)} %collective-permute-done.10.refs_7_) | copy-start | bytes 208900
  35.3 4.0 %copy-start.12 = (f32[1,128]{1,0:T(1,128)}, f32[1,128]{1,0:T(1,128)S(1)}, u32[]{:S(2)}) copy-start(f32[1,128]{1,0:T(1,128)S(1)} %collective-permute-done.5.refs_1_) | copy-start | bytes 1540
  37.6 1.8 %copy-start.13 = (f32[1,128]{1,0:T(1,128)}, f32[1,128]{1,0:T(1,128)S(1)}, u32[]{:S(2)}) copy-start(f32[1,128]{1,0:T(1,128)S(1)} %collective-permute-done.6.refs_2_) | copy-start | bytes 1540
  42.3 1.6 %collective-permute-start.11 = (f32[256,128]{1,0:T(8,128)}, f32[256,128]{1,0:T(8,128)S(1)}, u32[]{:S(2)}, u32[]{:S(2)}) collective-permute-start(f32[256,128]{1,0:T(8,128)} %get-tuple-element.32), channel_id=1, source_target_pairs={{0,1},{1,0},{2,3},{3,2},{4,5},{5,4},{6,7},{7,6},{8,9},{9,8},{10,11... | collective-permute-start | bytes 393224 | tf_op jit(solution)/shard_map/ppermute | solution.py:434
  46.2 6.0 %collective-permute-start.12 = (f32[64,128]{1,0:T(8,128)}, f32[64,128]{1,0:T(8,128)S(1)}, u32[]{:S(2)}, u32[]{:S(2)}) collective-permute-start(f32[64,128]{1,0:T(8,128)} %get-tuple-element.34), channel_id=1, source_target_pairs={{0,8},{8,0},{16,24},{24,16},{1,9},{9,1},{17,25},{25,17},{2,10},{10... | collective-permute-start | bytes 98312 | tf_op jit(solution)/shard_map/ppermute | solution.py:434
  47.7 4.5 %collective-permute-start.13 = (f32[64,128]{1,0:T(8,128)}, f32[64,128]{1,0:T(8,128)S(1)}, u32[]{:S(2)}, u32[]{:S(2)}) collective-permute-start(f32[64,128]{1,0:T(8,128)} %get-tuple-element.35), channel_id=1, source_target_pairs={{0,16},{8,24},{16,0},{24,8},{1,17},{9,25},{17,1},{25,9},{2,18},{10... | collective-permute-start | bytes 98312 | tf_op jit(solution)/shard_map/ppermute | solution.py:434
  49.2 5.0 %collective-permute-start.14 = (f32[64,128]{1,0:T(8,128)}, f32[64,128]{1,0:T(8,128)S(1)}, u32[]{:S(2)}, u32[]{:S(2)}) collective-permute-start(f32[64,128]{1,0:T(8,128)} %get-tuple-element.36), channel_id=1, source_target_pairs={{0,24},{8,16},{16,8},{24,0},{1,25},{9,17},{17,9},{25,1},{2,26},{10... | collective-permute-start | bytes 98312 | tf_op jit(solution)/shard_map/ppermute | solution.py:434
  52.1 2.1 %copy-start.5 = (f32[64,128]{1,0:T(8,128)}, f32[64,128]{1,0:T(8,128)S(1)}, u32[]{:S(2)}) copy-start(f32[64,128]{1,0:T(8,128)S(1)} %collective-permute-done.12.refs_1_) | copy-start | bytes 98308
  52.2 2.1 %copy-start.6 = (f32[64,128]{1,0:T(8,128)}, f32[64,128]{1,0:T(8,128)S(1)}, u32[]{:S(2)}) copy-start(f32[64,128]{1,0:T(8,128)S(1)} %collective-permute-done.13.refs_2_) | copy-start | bytes 98308
  (6 other events, 3.8 us)

commit v2 on v1

--- a/solution.py
+++ b/solution.py
@@ -8,6 +8,8 @@
 from jax.sharding import PartitionSpec as P
 
 HOT = 64
+GRANT = 8 * 1024 * 1024
+WIDE_GRANT = 52 * 1024 * 1024
 
 
 def pair_list(number):
@@ -210,6 +212,7 @@
             pltpu.SemaphoreType.DMA((group_count, 2)),
         ],
         cost_estimate=cost(1e6, 1e6),
+        compiler_params=pltpu.CompilerParams(vmem_limit_bytes=WIDE_GRANT),
         name="pack_hot",
     )(starts, looked, bottom_out, table)
 
@@ -245,6 +248,7 @@
         in_specs=[whole()] * 4,
         out_specs=(whole(), whole()),
         cost_estimate=cost(3e7, 1e6),
+        compiler_params=pltpu.CompilerParams(vmem_limit_bytes=GRANT),
         name="count_rows",
     )(places_own, places_other, bottom_out, top_dense)
 
@@ -269,6 +273,7 @@
         in_specs=[whole()] * (1 + len(blocks)),
         out_specs=(whole(), whole()),
         cost_estimate=cost(1e8, 1e6),
+        compiler_params=pltpu.CompilerParams(vmem_limit_bytes=GRANT),
         name="pool_hot",
     )(counts, *blocks)
 
@@ -302,6 +307,7 @@
         in_specs=[whole()] * 6,
         out_specs=(whole(), whole()),
         cost_estimate=cost(1e7, 1e6),
+        compiler_params=pltpu.CompilerParams(vmem_limit_bytes=GRANT),
         name="score",
     )(part_own, part_other, bottom_out, linear, top_pairs, cotangent)
 
@@ -333,6 +339,7 @@
         in_specs=[whole()] * 6,
         out_specs=(whole(), whole()),
         cost_estimate=cost(5e7, 1e6),
+        compiler_params=pltpu.CompilerParams(vmem_limit_bytes=GRANT),
         name="finish_dense",
     )(pooled, bottom_out, linear, top_pairs, cotangent, top_dense)
 
@@ -369,6 +376,7 @@
         in_specs=[whole()] * (2 * count),
         out_specs=(whole(), whole()),
         cost_estimate=cost(2e8, 1e6),
+        compiler_params=pltpu.CompilerParams(vmem_limit_bytes=GRANT),
         name="row_grads",
     )(*scores, *sent)
 
@@ -389,6 +397,7 @@
         in_specs=[whole()] * 2,
         out_specs=(whole(),) * group_count,
         cost_estimate=cost(1e6, 1e6),
+        compiler_params=pltpu.CompilerParams(vmem_limit_bytes=GRANT),
         name="split_owners",
     )(grad_own, grad_other)
 
@@ -418,6 +427,7 @@
         out_specs=whole(pl.ANY),
         scratch_shapes=[pltpu.VMEM((win_size + HOT, width), jnp.float32), pltpu.SemaphoreType.DMA],
         cost_estimate=cost(1e6, 2e6),
+        compiler_params=pltpu.CompilerParams(vmem_limit_bytes=GRANT),
         name="place_rows",
     )(starts, *blocks)
 

time: 57.2 us -> 47.2 us (0.83)
  Pallas kernels: 18 us -> 6.63 us
  waiting for transfers between devices: 14.5 us -> 16.9 us
  local copies, waits for them, and re-layouts: 3.15 us -> 2.2 us
    ppermute x15, waiting for transfers between devices: 14.5 us -> 16.9 us  [across(): lax.ppermute(values, axis, [(pos, pos ^ step) for pos in range(size)])]
    pallas_call x1, Pallas kernels: 2.66 us -> 0.76 us  [count_rows(): pl.pallas_call(kernel, out_shape=(jax.ShapeDtypeStruct((2 * samples, len(...]
    pallas_call x1, Pallas kernels: 2.27 us -> 0.42 us  [pool_hot(): pl.pallas_call(kernel, out_shape=(part, part), in_specs=[whole()] * (1 +...]
    pallas_call x1, Pallas kernels: 2.23 us -> 0.41 us  [score(): pl.pallas_call(kernel, out_shape=(jax.ShapeDtypeStruct((1, samples), jnp....]
    pallas_call x1, Pallas kernels: 2.42 us -> 0.71 us  [row_grads(): pl.pallas_call(kernel, out_shape=(part, part), in_specs=[whole()] * (2 *...]
    pallas_call x1, Pallas kernels: 1.63 us -> 0.02 us  [split_owners(): pl.pallas_call(kernel, out_shape=(part,) * group_count, in_specs=[whole()...]
    pallas_call x1, Pallas kernels: 2.48 us -> 1.15 us  [finish_dense(): pl.pallas_call(kernel, out_shape=(jax.ShapeDtypeStruct((samples, hidden),...]
    unnamed x30 -> x12, local copies, waits for them, and re-layouts: 3.15 us -> 2.2 us
  transfers between devices with their start and end apart: 15 -> 15, of which waited for: 7 -> 8; matrix products, arithmetic and copies ran while one was open for 0% -> 0% of each run, Pallas kernels for 17% -> 6%
where the time goes in v2:
time: 47.2 us; the launch traced here: 46.9 us
  starting transfers between devices  20.5 us (43%)
  waiting for transfers between devices  16.9 us (36%)
  Pallas kernels  6.63 us (14%)
  local copies, waits for them, and re-layouts  2.2 us (5%)
  between operations  0.73 us (2%)
    ppermute x15, starting transfers between devices, across(): lax.ppermute(values, axis, [(pos, pos ^ step) for pos in range(size)])  20.5 us
    ppermute x15, waiting for transfers between devices, across(): lax.ppermute(values, axis, [(pos, pos ^ step) for pos in range(size)])  16.9 us
    unnamed x12, local copies, waits for them, and re-layouts  2.2 us
    pallas_call x1, Pallas kernels, place_rows(): pl.pallas_call(kernel, out_shape=jax.ShapeDtypeStruct((win_size, width),...  1.61 us
    pallas_call x1, Pallas kernels, pack_hot(): pl.pallas_call(kernel, out_shape=(jax.ShapeDtypeStruct((hot_rows, width),...  1.55 us
    pallas_call x1, Pallas kernels, finish_dense(): pl.pallas_call(kernel, out_shape=(jax.ShapeDtypeStruct((samples, hidden),...  1.15 us
  transfers between devices with their start and end apart: 15, of which 8 were waited for; matrix products, arithmetic and copies ran while one was open for 0% of the time, Pallas kernels for 6%

profile of v2, /device:TPU:0, one launch (start us, length us, event | category | flops | bytes accessed | tf_op | source)
XLA Modules:
  0.0 46.9 jit_solution(9677819225441225427)
XLA Ops:
  0.7 0.8 %copy-done.2 = bf16[128,128]{1,0:T(8,128)(2,1)S(1)} copy-done((bf16[128,128]{1,0:T(8,128)(2,1)S(1)}, bf16[128,128]{1,0:T(8,128)(2,1)}, u32[]{:S(2)}) %copy-start.2) | copy-done | bytes 32792
  1.5 0.7 %copy-done.4 = s32[4,32]{1,0:T(4,128)S(1)} copy-done((s32[4,32]{1,0:T(4,128)S(1)}, s32[4,32]{1,0:T(4,128)}, u32[]{:S(2)}) %copy-start.4) | copy-done | bytes 536
  2.8 1.5 %pack_hot.1 = (f32[256,128]{1,0:T(8,128)S(1)}, f32[136,128]{1,0:T(8,128)S(1)}, f32[8,128]{1,0:T(8,128)S(1)}) custom-call(s32[4,32]{1,0:T(4,128)S(1)} %copy-done.4, s32[4,128]{1,0:T(4,128)S(1)} %bitcast.5, bf16[128,128]{1,0:T(8,128)(2,1)S(1)} %copy-done.2, f32[7872,128]{1,0:T(8,128)} %bitcast.6), custom_call_target="tpu_custom_call" | custom-call | flops 1000000 | bytes 1000000 | tf_op jit(solution)/shard_map/pack_hot/pallas_call | solution.py:201
  4.4 3.1 %collective-permute-start.1 = (f32[256,128]{1,0:T(8,128)S(1)}, f32[256,128]{1,0:T(8,128)S(1)}, u32[]{:S(2)}, u32[]{:S(2)}) collective-permute-start(f32[256,128]{1,0:T(8,128)S(1)} %get-tuple-element.22.refs_0_), channel_id=1, source_target_pairs={{0,2},{1,3},{2,0},{3,1},{4,6},{5,7},{6,4},{7,5},{8,10},{9,11},{10,... | collective-permute-start | bytes 393224 | tf_op jit(solution)/shard_map/ppermute | solution.py:444
  7.5 2.6 %collective-permute-start.2 = (f32[256,128]{1,0:T(8,128)S(1)}, f32[256,128]{1,0:T(8,128)S(1)}, u32[]{:S(2)}, u32[]{:S(2)}) collective-permute-start(f32[256,128]{1,0:T(8,128)S(1)} %get-tuple-element.22.refs_0_), channel_id=1, source_target_pairs={{0,4},{1,5},{2,6},{3,7},{4,0},{5,1},{6,2},{7,3},{8,12},{9,13},{10,... | collective-permute-start | bytes 393224 | tf_op jit(solution)/shard_map/ppermute | solution.py:444
  10.1 0.9 %collective-permute-start.8 = (f32[136,128]{1,0:T(8,128)S(1)}, f32[136,128]{1,0:T(8,128)S(1)}, u32[]{:S(2)}, u32[]{:S(2)}) collective-permute-start(f32[136,128]{1,0:T(8,128)S(1)} %get-tuple-element.30.refs_4_), channel_id=1, source_target_pairs={{0,2},{1,3},{2,0},{3,1},{4,6},{5,7},{6,4},{7,5},{8,10},{9,11},{10,... | collective-permute-start | bytes 208904 | tf_op jit(solution)/shard_map/ppermute | solution.py:444
  11.3 3.2 %collective-permute-start.9 = (f32[136,128]{1,0:T(8,128)S(1)}, f32[136,128]{1,0:T(8,128)S(1)}, u32[]{:S(2)}, u32[]{:S(2)}) collective-permute-start(f32[136,128]{1,0:T(8,128)S(1)} %get-tuple-element.30.refs_4_), channel_id=1, source_target_pairs={{0,4},{1,5},{2,6},{3,7},{4,0},{5,1},{6,2},{7,3},{8,12},{9,13},{10,... | collective-permute-start | bytes 208904 | tf_op jit(solution)/shard_map/ppermute | solution.py:444
  14.5 0.8 %count_rows.1 = (bf16[256,1024]{1,0:T(8,128)(2,1)S(1)}, f32[128,1024]{1,0:T(8,128)S(1)}) custom-call(f32[8,128]{1,0:T(8,128)S(1)} %get-tuple-element.20.own_ref, f32[8,128]{1,0:T(8,128)S(1)} %collective-permute-done.other_ref, bf16[128,128]{1,0:T(8,128)(2,1)S(1)} %copy-done.2, bf16[128,1024]{1,0:T(8,128)(2,1)S(1)} %copy-done.1), custom_call_target="tpu_custom_call" | custom-call | flops 30000000 | bytes 1000000 | tf_op jit(solution)/shard_map/count_rows/pallas_call | solution.py:242
  15.3 1.1 %collective-permute-start.10 = (f32[136,128]{1,0:T(8,128)S(1)}, f32[136,128]{1,0:T(8,128)S(1)}, u32[]{:S(2)}, u32[]{:S(2)}) collective-permute-start(f32[136,128]{1,0:T(8,128)S(1)} %get-tuple-element.30.refs_4_), channel_id=1, source_target_pairs={{0,6},{1,7},{2,4},{3,5},{4,2},{5,3},{6,0},{7,1},{8,14},{9,15},{10,... | collective-permute-start | bytes 208904 | tf_op jit(solution)/shard_map/ppermute | solution.py:444
  16.4 7.0 %collective-permute-done.2.refs_2_ = f32[256,128]{1,0:T(8,128)S(1)} collective-permute-done((f32[256,128]{1,0:T(8,128)S(1)}, f32[256,128]{1,0:T(8,128)S(1)}, u32[]{:S(2)}, u32[]{:S(2)}) %collective-permute-start.2) | collective-permute-done | bytes 131104 | tf_op jit(solution)/shard_map/ppermute | solution.py:444
  23.9 1.2 %collective-permute-done.4.other_ref = f32[128,128]{1,0:T(8,128)S(1)} collective-permute-done((f32[128,128]{1,0:T(8,128)S(1)}, f32[128,128]{1,0:T(8,128)S(1)}, u32[]{:S(2)}, u32[]{:S(2)}) %collective-permute-start.4) | collective-permute-done | bytes 65568 | tf_op jit(solution)/shard_map/ppermute | solution.py:444
  25.6 3.4 %collective-permute-start.5 = (f32[1,128]{1,0:T(1,128)S(1)}, f32[1,128]{1,0:T(1,128)S(1)}, u32[]{:S(2)}, u32[]{:S(2)}) collective-permute-start(f32[1,128]{1,0:T(1,128)S(1)} %get-tuple-element.29.refs_0_), channel_id=1, source_target_pairs={{0,2},{1,3},{2,0},{3,1},{4,6},{5,7},{6,4},{7,5},{8,10},{9,11},{10,... | collective-permute-start | bytes 1544 | tf_op jit(solution)/shard_map/ppermute | solution.py:444
  29.0 0.9 %collective-permute-start.6 = (f32[1,128]{1,0:T(1,128)S(1)}, f32[1,128]{1,0:T(1,128)S(1)}, u32[]{:S(2)}, u32[]{:S(2)}) collective-permute-start(f32[1,128]{1,0:T(1,128)S(1)} %get-tuple-element.29.refs_0_), channel_id=1, source_target_pairs={{0,4},{1,5},{2,6},{3,7},{4,0},{5,1},{6,2},{7,3},{8,12},{9,13},{10,... | collective-permute-start | bytes 1544 | tf_op jit(solution)/shard_map/ppermute | solution.py:444
  29.9 1.5 %collective-permute-start.7 = (f32[1,128]{1,0:T(1,128)S(1)}, f32[1,128]{1,0:T(1,128)S(1)}, u32[]{:S(2)}, u32[]{:S(2)}) collective-permute-start(f32[1,128]{1,0:T(1,128)S(1)} %get-tuple-element.29.refs_0_), channel_id=1, source_target_pairs={{0,6},{1,7},{2,4},{3,5},{4,2},{5,3},{6,0},{7,1},{8,14},{9,15},{10,... | collective-permute-start | bytes 1544 | tf_op jit(solution)/shard_map/ppermute | solution.py:444
  31.4 2.0 %collective-permute-done.6.refs_2_ = f32[1,128]{1,0:T(1,128)S(1)} collective-permute-done((f32[1,128]{1,0:T(1,128)S(1)}, f32[1,128]{1,0:T(1,128)S(1)}, u32[]{:S(2)}, u32[]{:S(2)}) %collective-permute-start.6) | collective-permute-done | bytes 544 | tf_op jit(solution)/shard_map/ppermute | solution.py:444
  33.4 1.8 %collective-permute-done.7.refs_3_ = f32[1,128]{1,0:T(1,128)S(1)} collective-permute-done((f32[1,128]{1,0:T(1,128)S(1)}, f32[1,128]{1,0:T(1,128)S(1)}, u32[]{:S(2)}, u32[]{:S(2)}) %collective-permute-start.7) | collective-permute-done | bytes 544 | tf_op jit(solution)/shard_map/ppermute | solution.py:444
  35.3 0.7 %row_grads.1 = (f32[256,128]{1,0:T(8,128)S(1)}, f32[256,128]{1,0:T(8,128)S(1)}) custom-call(f32[1,128]{1,0:T(1,128)S(1)} %get-tuple-element.29.refs_0_, f32[1,128]{1,0:T(1,128)S(1)} %collective-permute-done.5.refs_1_, f32[1,128]{1,0:T(1,128)S(1)} %collective-permute-done.6.refs_2_, f32[1,128]{1,0:T(1,128)S(1)} %collective-permute-done.7.refs_3_, ...), custom_call_target="tpu_custom_call" | custom-call | flops 200000000 | bytes 1000000 | tf_op jit(solution)/shard_map/row_grads/pallas_call | solution.py:373
  36.1 1.3 %collective-permute-done.11.other_ref = f32[256,128]{1,0:T(8,128)S(1)} collective-permute-done((f32[256,128]{1,0:T(8,128)S(1)}, f32[256,128]{1,0:T(8,128)S(1)}, u32[]{:S(2)}, u32[]{:S(2)}) %collective-permute-start.11) | collective-permute-done | bytes 131104 | tf_op jit(solution)/shard_map/ppermute | solution.py:444
  37.4 1.6 %collective-permute-start.12 = (f32[64,128]{1,0:T(8,128)S(1)}, f32[64,128]{1,0:T(8,128)S(1)}, u32[]{:S(2)}, u32[]{:S(2)}) collective-permute-start(f32[64,128]{1,0:T(8,128)S(1)} %get-tuple-element.34), channel_id=1, source_target_pairs={{0,8},{8,0},{16,24},{24,16},{1,9},{9,1},{17,25},{25,17},{2,10},{10... | collective-permute-start | bytes 98312 | tf_op jit(solution)/shard_map/ppermute | solution.py:444
  39.0 1.5 %collective-permute-start.13 = (f32[64,128]{1,0:T(8,128)S(1)}, f32[64,128]{1,0:T(8,128)S(1)}, u32[]{:S(2)}, u32[]{:S(2)}) collective-permute-start(f32[64,128]{1,0:T(8,128)S(1)} %get-tuple-element.35), channel_id=1, source_target_pairs={{0,16},{8,24},{16,0},{24,8},{1,17},{9,25},{17,1},{25,9},{2,18},{10... | collective-permute-start | bytes 98312 | tf_op jit(solution)/shard_map/ppermute | solution.py:444
  41.0 1.1 %finish_dense.1 = (bf16[128,1024]{1,0:T(8,128)(2,1)}, f32[128,128]{1,0:T(8,128)}) custom-call(f32[128,128]{1,0:T(8,128)S(1)} %get-tuple-element.26.pooled_ref, bf16[128,128]{1,0:T(8,128)(2,1)S(1)} %copy-done.2, f32[128,1024]{1,0:T(8,128)S(1)} %get-tuple-element.25.linear_ref, f32[1,1024]{1,0:T(1,128)S(1)} %copy-done.3, f32[128,1024]{1,0:T(8,128)S(1)} %copy-done, ...), custom_call_target="tpu_custom_call" | custom-call | flops 50000000 | bytes 1000000 | tf_op jit(solution)/shard_map/finish_dense/pallas_call | solution.py:333
  42.1 0.8 %collective-permute-done.13.refs_2_ = f32[64,128]{1,0:T(8,128)S(1)} collective-permute-done((f32[64,128]{1,0:T(8,128)S(1)}, f32[64,128]{1,0:T(8,128)S(1)}, u32[]{:S(2)}, u32[]{:S(2)}) %collective-permute-start.13) | collective-permute-done | bytes 32800 | tf_op jit(solution)/shard_map/ppermute | solution.py:444
  42.9 2.4 %collective-permute-done.14.refs_3_ = f32[64,128]{1,0:T(8,128)S(1)} collective-permute-done((f32[64,128]{1,0:T(8,128)S(1)}, f32[64,128]{1,0:T(8,128)S(1)}, u32[]{:S(2)}, u32[]{:S(2)}) %collective-permute-start.14) | collective-permute-done | bytes 32800 | tf_op jit(solution)/shard_map/ppermute | solution.py:444
  45.3 1.6 %place_rows.1 = f32[1968,128]{1,0:T(8,128)} custom-call(s32[4,32]{1,0:T(4,128)S(1)} %copy-done.4, f32[64,128]{1,0:T(8,128)S(1)} %get-tuple-element.33.refs_0_, f32[64,128]{1,0:T(8,128)S(1)} %collective-permute-done.12.refs_1_, f32[64,128]{1,0:T(8,128)S(1)} %collective-permute-done.13.refs_2_, f32[64,128]{1,0:T(8,128)S(1)} %collective-permute-done.14.refs_3_), custom_call_target="tpu_custom_call" | custom-call | flops 1000000 | bytes 2000000 | tf_op jit(solution)/shard_map/place_rows/pallas_call | solution.py:423
  (26 shorter events, 2.5 us)
Async XLA Ops:
  0.6 13.9 %copy-start.1 = (bf16[128,1024]{1,0:T(8,128)(2,1)S(1)}, bf16[128,1024]{1,0:T(8,128)(2,1)}, u32[]{:S(2)}) copy-start(bf16[128,1024]{1,0:T(8,128)(2,1)} %dense_ref.3) | copy-start | bytes 786436
  0.6 24.5 %copy-start = (f32[128,1024]{1,0:T(8,128)S(1)}, f32[128,1024]{1,0:T(8,128)}, u32[]{:S(2)}) copy-start(f32[128,1024]{1,0:T(8,128)} %cot_ref.3) | copy-start | bytes 1572868
  0.7 0.8 %copy-start.2 = (bf16[128,128]{1,0:T(8,128)(2,1)S(1)}, bf16[128,128]{1,0:T(8,128)(2,1)}, u32[]{:S(2)}) copy-start(bf16[128,128]{1,0:T(8,128)(2,1)} %bottom_ref.7) | copy-start | bytes 98308
  1.5 0.7 %copy-start.4 = (s32[4,32]{1,0:T(4,128)S(1)}, s32[4,32]{1,0:T(4,128)}, u32[]{:S(2)}) copy-start(s32[4,32]{1,0:T(4,128)} %starts_ref.3) | copy-start | bytes 1540
  2.2 0.7 %copy-start.5 = (s32[128,1,4]{0,2,1:T(4,128)S(1)}, s32[128,1,4]{0,2,1:T(4,128)}, u32[]{:S(2)}) copy-start(s32[128,1,4]{0,2,1:T(4,128)} %param.8) | copy-start | bytes 6148
  2.8 22.3 %copy-start.3 = (f32[1,1024]{1,0:T(1,128)S(1)}, f32[1,1024]{1,0:T(1,128)}, u32[]{:S(2)}) copy-start(f32[1,1024]{1,0:T(1,128)} %pairs_ref.3) | copy-start | bytes 12292
  4.4 10.9 %collective-permute-start.1 = (f32[256,128]{1,0:T(8,128)S(1)}, f32[256,128]{1,0:T(8,128)S(1)}, u32[]{:S(2)}, u32[]{:S(2)}) collective-permute-start(f32[256,128]{1,0:T(8,128)S(1)} %get-tuple-element.22.refs_0_), channel_id=1, source_target_pairs={{0,2},{1,3},{2,0},{3,1},{4,6},{5,7},{6,4},{7,5},{8,10},{9,11},{10,... | collective-permute-start | bytes 393224 | tf_op jit(solution)/shard_map/ppermute | solution.py:444
  7.5 15.9 %collective-permute-start.2 = (f32[256,128]{1,0:T(8,128)S(1)}, f32[256,128]{1,0:T(8,128)S(1)}, u32[]{:S(2)}, u32[]{:S(2)}) collective-permute-start(f32[256,128]{1,0:T(8,128)S(1)} %get-tuple-element.22.refs_0_), channel_id=1, source_target_pairs={{0,4},{1,5},{2,6},{3,7},{4,0},{5,1},{6,2},{7,3},{8,12},{9,13},{10,... | collective-permute-start | bytes 393224 | tf_op jit(solution)/shard_map/ppermute | solution.py:444
  10.1 13.3 %collective-permute-start.3 = (f32[256,128]{1,0:T(8,128)S(1)}, f32[256,128]{1,0:T(8,128)S(1)}, u32[]{:S(2)}, u32[]{:S(2)}) collective-permute-start(f32[256,128]{1,0:T(8,128)S(1)} %get-tuple-element.22.refs_0_), channel_id=1, source_target_pairs={{0,6},{1,7},{2,4},{3,5},{4,2},{5,3},{6,0},{7,1},{8,14},{9,15},{10,... | collective-permute-start | bytes 393224 | tf_op jit(solution)/shard_map/ppermute | solution.py:444
  10.1 1.2 %collective-permute-start = (f32[8,128]{1,0:T(8,128)S(1)}, f32[8,128]{1,0:T(8,128)S(1)}, u32[]{:S(2)}, u32[]{:S(2)}) collective-permute-start(f32[8,128]{1,0:T(8,128)S(1)} %get-tuple-element.20.own_ref), channel_id=1, source_target_pairs={{0,1},{1,0},{2,3},{3,2},{4,5},{5,4},{6,7},{7,6},{8,9},{9,8},{10,11... | collective-permute-start | bytes 12296 | tf_op jit(solution)/shard_map/ppermute | solution.py:444
  10.1 19.8 %collective-permute-start.8 = (f32[136,128]{1,0:T(8,128)S(1)}, f32[136,128]{1,0:T(8,128)S(1)}, u32[]{:S(2)}, u32[]{:S(2)}) collective-permute-start(f32[136,128]{1,0:T(8,128)S(1)} %get-tuple-element.30.refs_4_), channel_id=1, source_target_pairs={{0,2},{1,3},{2,0},{3,1},{4,6},{5,7},{6,4},{7,5},{8,10},{9,11},{10,... | collective-permute-start | bytes 208904 | tf_op jit(solution)/shard_map/ppermute | solution.py:444
  11.3 20.1 %collective-permute-start.9 = (f32[136,128]{1,0:T(8,128)S(1)}, f32[136,128]{1,0:T(8,128)S(1)}, u32[]{:S(2)}, u32[]{:S(2)}) collective-permute-start(f32[136,128]{1,0:T(8,128)S(1)} %get-tuple-element.30.refs_4_), channel_id=1, source_target_pairs={{0,4},{1,5},{2,6},{3,7},{4,0},{5,1},{6,2},{7,3},{8,12},{9,13},{10,... | collective-permute-start | bytes 208904 | tf_op jit(solution)/shard_map/ppermute | solution.py:444
  15.3 16.1 %collective-permute-start.10 = (f32[136,128]{1,0:T(8,128)S(1)}, f32[136,128]{1,0:T(8,128)S(1)}, u32[]{:S(2)}, u32[]{:S(2)}) collective-permute-start(f32[136,128]{1,0:T(8,128)S(1)} %get-tuple-element.30.refs_4_), channel_id=1, source_target_pairs={{0,6},{1,7},{2,4},{3,5},{4,2},{5,3},{6,0},{7,1},{8,14},{9,15},{10,... | collective-permute-start | bytes 208904 | tf_op jit(solution)/shard_map/ppermute | solution.py:444
  23.8 1.3 %collective-permute-start.4 = (f32[128,128]{1,0:T(8,128)S(1)}, f32[128,128]{1,0:T(8,128)S(1)}, u32[]{:S(2)}, u32[]{:S(2)}) collective-permute-start(f32[128,128]{1,0:T(8,128)S(1)} %get-tuple-element.24), channel_id=1, source_target_pairs={{0,1},{1,0},{2,3},{3,2},{4,5},{5,4},{6,7},{7,6},{8,9},{9,8},{10,11... | collective-permute-start | bytes 196616 | tf_op jit(solution)/shard_map/ppermute | solution.py:444
  25.6 5.9 %collective-permute-start.5 = (f32[1,128]{1,0:T(1,128)S(1)}, f32[1,128]{1,0:T(1,128)S(1)}, u32[]{:S(2)}, u32[]{:S(2)}) collective-permute-start(f32[1,128]{1,0:T(1,128)S(1)} %get-tuple-element.29.refs_0_), channel_id=1, source_target_pairs={{0,2},{1,3},{2,0},{3,1},{4,6},{5,7},{6,4},{7,5},{8,10},{9,11},{10,... | collective-permute-start | bytes 1544 | tf_op jit(solution)/shard_map/ppermute | solution.py:444
  29.0 4.5 %collective-permute-start.6 = (f32[1,128]{1,0:T(1,128)S(1)}, f32[1,128]{1,0:T(1,128)S(1)}, u32[]{:S(2)}, u32[]{:S(2)}) collective-permute-start(f32[1,128]{1,0:T(1,128)S(1)} %get-tuple-element.29.refs_0_), channel_id=1, source_target_pairs={{0,4},{1,5},{2,6},{3,7},{4,0},{5,1},{6,2},{7,3},{8,12},{9,13},{10,... | collective-permute-start | bytes 1544 | tf_op jit(solution)/shard_map/ppermute | solution.py:444
  29.9 5.4 %collective-permute-start.7 = (f32[1,128]{1,0:T(1,128)S(1)}, f32[1,128]{1,0:T(1,128)S(1)}, u32[]{:S(2)}, u32[]{:S(2)}) collective-permute-start(f32[1,128]{1,0:T(1,128)S(1)} %get-tuple-element.29.refs_0_), channel_id=1, source_target_pairs={{0,6},{1,7},{2,4},{3,5},{4,2},{5,3},{6,0},{7,1},{8,14},{9,15},{10,... | collective-permute-start | bytes 1544 | tf_op jit(solution)/shard_map/ppermute | solution.py:444
  36.0 1.4 %collective-permute-start.11 = (f32[256,128]{1,0:T(8,128)S(1)}, f32[256,128]{1,0:T(8,128)S(1)}, u32[]{:S(2)}, u32[]{:S(2)}) collective-permute-start(f32[256,128]{1,0:T(8,128)S(1)} %get-tuple-element.32), channel_id=1, source_target_pairs={{0,1},{1,0},{2,3},{3,2},{4,5},{5,4},{6,7},{7,6},{8,9},{9,8},{10,11... | collective-permute-start | bytes 393224 | tf_op jit(solution)/shard_map/ppermute | solution.py:444
  37.4 4.7 %collective-permute-start.12 = (f32[64,128]{1,0:T(8,128)S(1)}, f32[64,128]{1,0:T(8,128)S(1)}, u32[]{:S(2)}, u32[]{:S(2)}) collective-permute-start(f32[64,128]{1,0:T(8,128)S(1)} %get-tuple-element.34), channel_id=1, source_target_pairs={{0,8},{8,0},{16,24},{24,16},{1,9},{9,1},{17,25},{25,17},{2,10},{10... | collective-permute-start | bytes 98312 | tf_op jit(solution)/shard_map/ppermute | solution.py:444
  39.0 3.9 %collective-permute-start.13 = (f32[64,128]{1,0:T(8,128)S(1)}, f32[64,128]{1,0:T(8,128)S(1)}, u32[]{:S(2)}, u32[]{:S(2)}) collective-permute-start(f32[64,128]{1,0:T(8,128)S(1)} %get-tuple-element.35), channel_id=1, source_target_pairs={{0,16},{8,24},{16,0},{24,8},{1,17},{9,25},{17,1},{25,9},{2,18},{10... | collective-permute-start | bytes 98312 | tf_op jit(solution)/shard_map/ppermute | solution.py:444
  40.5 4.8 %collective-permute-start.14 = (f32[64,128]{1,0:T(8,128)S(1)}, f32[64,128]{1,0:T(8,128)S(1)}, u32[]{:S(2)}, u32[]{:S(2)}) collective-permute-start(f32[64,128]{1,0:T(8,128)S(1)} %get-tuple-element.36), channel_id=1, source_target_pairs={{0,24},{8,16},{16,8},{24,0},{1,25},{9,17},{17,9},{25,1},{2,26},{10... | collective-permute-start | bytes 98312 | tf_op jit(solution)/shard_map/ppermute | solution.py:444

commit v3 on v2

--- a/solution.py
+++ b/solution.py
@@ -9,7 +9,6 @@
 
 HOT = 64
 GRANT = 8 * 1024 * 1024
-WIDE_GRANT = 52 * 1024 * 1024
 
 
 def pair_list(number):
@@ -157,14 +156,40 @@
     )
 
 
-def pack_hot(starts, looked, bottom_out, table, group_count):
+def stay(values):
+    return pltpu.with_memory_space_constraint(values, pltpu.HBM)
+
+
+def pack_sent(looked, bottom_out, win_size):
+    samples, width = bottom_out.shape
+    bag = looked.shape[0]
+
+    def kernel(looked_ref, bottom_ref, sent_ref):
+        found = looked_ref[...]
+        window_of = jnp.floor((found.astype(jnp.float32) + 0.5) * (1.0 / win_size)).astype(jnp.int32)
+        places = (found - window_of * (win_size - HOT)).astype(jnp.float32)
+        sent_ref[pl.ds(samples, 8), :] = jnp.concatenate(
+            [places, jnp.zeros((8 - bag, samples), jnp.float32)], axis=0
+        )
+        sent_ref[pl.ds(0, samples), :] = bottom_ref[...].astype(jnp.float32)
+
+    return pl.pallas_call(
+        kernel,
+        out_shape=jax.ShapeDtypeStruct((samples + 8, width), jnp.float32),
+        in_specs=[whole()] * 2,
+        out_specs=whole(),
+        cost_estimate=cost(1e6, 1e5),
+        compiler_params=pltpu.CompilerParams(vmem_limit_bytes=GRANT),
+        name="pack_sent",
+    )(stay(looked), stay(bottom_out))
+
+
+def load_hot(starts, table, group_count):
     span_rows, width = table.shape
     win_size = span_rows // group_count
-    samples = bottom_out.shape[0]
-    bag = looked.shape[0]
     head = min(HOT + 8, win_size)
 
-    def kernel(starts_ref, looked_ref, bottom_ref, table_ref, hot_ref, sent_ref, places_ref, held, sems):
+    def kernel(starts_ref, table_ref, hot_ref, held, sems):
         grp_pos = lax.axis_index("grp")
         shard_pos = lax.axis_index("shard")
         shifts = []
@@ -185,97 +210,69 @@
             first.start()
             second.start()
             copies += [first, second]
-        found = looked_ref[...]
-        window_of = jnp.floor((found.astype(jnp.float32) + 0.5) * (1.0 / win_size)).astype(jnp.int32)
-        places = (found - window_of * (win_size - HOT)).astype(jnp.float32)
-        places = jnp.concatenate([places, jnp.zeros((8 - bag, samples), jnp.float32)], axis=0)
-        places_ref[...] = places
-        sent_ref[pl.ds(0, samples), :] = bottom_ref[...].astype(jnp.float32)
-        sent_ref[pl.ds(samples, 8), :] = places
         for copy in copies:
             copy.wait()
         for window in range(group_count):
             hot_ref[pl.ds(window * HOT, HOT), :] = held[window, pl.ds(shifts[window], HOT), :]
 
-    hot_rows = group_count * HOT
-    return pl.pallas_call(
-        kernel,
-        out_shape=(
-            jax.ShapeDtypeStruct((hot_rows, width), jnp.float32),
-            jax.ShapeDtypeStruct((samples + 8, width), jnp.float32),
-            jax.ShapeDtypeStruct((8, samples), jnp.float32),
-        ),
-        in_specs=[whole(pltpu.SMEM), whole(), whole(), whole(pl.ANY)],
-        out_specs=(whole(), whole(), whole()),
+    return pl.pallas_call(
+        kernel,
+        out_shape=jax.ShapeDtypeStruct((group_count * HOT, width), jnp.float32),
+        in_specs=[whole(pltpu.SMEM), whole(pl.ANY)],
+        out_specs=whole(),
         scratch_shapes=[
             pltpu.VMEM((group_count, head + HOT, width), jnp.float32),
             pltpu.SemaphoreType.DMA((group_count, 2)),
         ],
         cost_estimate=cost(1e6, 1e6),
-        compiler_params=pltpu.CompilerParams(vmem_limit_bytes=WIDE_GRANT),
-        name="pack_hot",
-    )(starts, looked, bottom_out, table)
-
-
-def count_rows(places_own, places_other, bottom_out, top_dense, bag, block_rows, steps):
-    samples = bottom_out.shape[0]
-    hidden = top_dense.shape[1]
-
-    def kernel(own_ref, other_ref, bottom_ref, dense_ref, counts_ref, linear_ref):
+        compiler_params=pltpu.CompilerParams(vmem_limit_bytes=GRANT),
+        name="load_hot",
+    )(stay(starts), stay(table))
+
+
+def linear_part(bottom_out, top_dense):
+    def kernel(bottom_ref, dense_ref, linear_ref):
+        linear_ref[...] = jnp.dot(bottom_ref[...], dense_ref[...], preferred_element_type=jnp.float32)
+
+    return pl.pallas_call(
+        kernel,
+        out_shape=jax.ShapeDtypeStruct((bottom_out.shape[0], top_dense.shape[1]), jnp.float32),
+        in_specs=[whole()] * 2,
+        out_specs=whole(),
+        cost_estimate=cost(3e7, 1e6),
+        compiler_params=pltpu.CompilerParams(vmem_limit_bytes=GRANT),
+        name="linear_part",
+    )(bottom_out, top_dense)
+
+
+def pool_rows(sent, hot_own, hot_other, bag):
+    block_rows, width = hot_own.shape
+    samples = sent.shape[0] - 8
+
+    def kernel(sent_ref, own_ref, other_ref, part_ref):
         shard_pos = lax.axis_index("shard")
         rows = lax.broadcasted_iota(jnp.int32, (samples, block_rows), 1).astype(jnp.float32)
-        for part, ref in enumerate((own_ref, other_ref)):
-            padded = jnp.concatenate(
-                [ref[...], jnp.zeros((samples - 8, samples), jnp.float32)], axis=0
-            )
-            columns = padded.T
-            for place, step in enumerate(steps):
-                base = (jnp.bitwise_xor(shard_pos, step) * block_rows).astype(jnp.float32)
-                total = jnp.zeros((samples, block_rows), jnp.float32)
-                for slot in range(bag):
-                    total += jnp.where(columns[:, slot : slot + 1] - base == rows, 1.0, 0.0)
-                counts_ref[
-                    pl.ds(part * samples, samples), pl.ds(place * block_rows, block_rows)
-                ] = total.astype(jnp.bfloat16)
-        linear_ref[...] = jnp.dot(bottom_ref[...], dense_ref[...], preferred_element_type=jnp.float32)
-
-    return pl.pallas_call(
-        kernel,
-        out_shape=(
-            jax.ShapeDtypeStruct((2 * samples, len(steps) * block_rows), jnp.bfloat16),
-            jax.ShapeDtypeStruct((samples, hidden), jnp.float32),
-        ),
-        in_specs=[whole()] * 4,
-        out_specs=(whole(), whole()),
-        cost_estimate=cost(3e7, 1e6),
-        compiler_params=pltpu.CompilerParams(vmem_limit_bytes=GRANT),
-        name="count_rows",
-    )(places_own, places_other, bottom_out, top_dense)
-
-
-def pool_hot(counts, blocks):
-    block_rows, width = blocks[0].shape
-    samples = counts.shape[0] // 2
-
-    def kernel(counts_ref, *refs):
-        block_refs = refs[: len(blocks)]
-        own_ref, other_ref = refs[len(blocks) :]
-        total = jnp.zeros((2 * samples, width), jnp.float32)
-        for place, ref in enumerate(block_refs):
-            total += dot_two(counts_ref[:, pl.ds(place * block_rows, block_rows)], ref[...])
-        own_ref[...] = total[:samples]
-        other_ref[...] = total[samples:]
-
-    part = jax.ShapeDtypeStruct((samples, width), jnp.float32)
-    return pl.pallas_call(
-        kernel,
-        out_shape=(part, part),
-        in_specs=[whole()] * (1 + len(blocks)),
-        out_specs=(whole(), whole()),
-        cost_estimate=cost(1e8, 1e6),
-        compiler_params=pltpu.CompilerParams(vmem_limit_bytes=GRANT),
-        name="pool_hot",
-    )(counts, *blocks)
+        columns = jnp.concatenate(
+            [sent_ref[pl.ds(samples, 8), :], jnp.zeros((samples - 8, samples), jnp.float32)], axis=0
+        ).T
+        total = jnp.zeros((samples, width), jnp.float32)
+        for side, ref in enumerate((own_ref, other_ref)):
+            base = (jnp.bitwise_xor(shard_pos, side) * block_rows).astype(jnp.float32)
+            times = jnp.zeros((samples, block_rows), jnp.float32)
+            for slot in range(bag):
+                times += jnp.where(columns[:, slot : slot + 1] - base == rows, 1.0, 0.0)
+            total += dot_two(times.astype(jnp.bfloat16), ref[...])
+        part_ref[...] = total
+
+    return pl.pallas_call(
+        kernel,
+        out_shape=jax.ShapeDtypeStruct((samples, width), jnp.float32),
+        in_specs=[whole()] * 3,
+        out_specs=whole(),
+        cost_estimate=cost(5e7, 1e6),
+        compiler_params=pltpu.CompilerParams(vmem_limit_bytes=GRANT),
+        name="pool_rows",
+    )(sent, hot_own, hot_other)
 
 
 def head_terms(pooled, bottom_ref, linear_ref, pairs_ref, cot_ref):
@@ -287,11 +284,15 @@
     return preact, sig, pre_grad, pair_grad
 
 
-def score(part_own, part_other, bottom_out, linear, top_pairs, cotangent):
+def score(parts, bottom_out, linear, top_pairs, cotangent):
     samples, width = bottom_out.shape
-
-    def kernel(own_ref, other_ref, bottom_ref, linear_ref, pairs_ref, cot_ref, row_ref, pooled_ref):
-        pooled = own_ref[...] + other_ref[...]
+    count = len(parts)
+
+    def kernel(*refs):
+        bottom_ref, linear_ref, pairs_ref, cot_ref, row_ref, pooled_ref = refs[count:]
+        pooled = refs[0][...]
+        for ref in refs[1:count]:
+            pooled = pooled + ref[...]
         pooled_ref[...] = pooled
         pair_grad = head_terms(pooled, bottom_ref, linear_ref, pairs_ref, cot_ref)[3]
         down = lax.broadcasted_iota(jnp.int32, (samples, samples), 0)
@@ -304,12 +305,12 @@
             jax.ShapeDtypeStruct((1, samples), jnp.float32),
             jax.ShapeDtypeStruct((samples, width), jnp.float32),
         ),
-        in_specs=[whole()] * 6,
+        in_specs=[whole()] * (count + 4),
         out_specs=(whole(), whole()),
         cost_estimate=cost(1e7, 1e6),
         compiler_params=pltpu.CompilerParams(vmem_limit_bytes=GRANT),
         name="score",
-    )(part_own, part_other, bottom_out, linear, top_pairs, cotangent)
+    )(*parts, bottom_out, linear, top_pairs, cotangent)
 
 
 def finish_dense(pooled, bottom_out, linear, top_pairs, cotangent, top_dense):
@@ -445,14 +446,14 @@
 
     steps = list(range(0, shard_count, 2))
     looked = lookups[:, 0, :].T
-    hot, sent, places = pack_hot(starts, looked, bottom_out, tables[0], group_count)
-    places_other = across("shard", places, 1)
-    hot_blocks = [hot] + [across("shard", hot, step) for step in steps[1:]]
+    sent = pack_sent(looked, bottom_out, win_size)
     sent_blocks = [sent] + [across("shard", sent, step) for step in steps[1:]]
-    counts, linear = count_rows(places, places_other, bottom_out, top_dense, bag, block_rows, steps)
-    part_own, part_other = pool_hot(counts, hot_blocks)
-    part_back = across("shard", part_other, 1)
-    score_row, pooled = score(part_own, part_back, bottom_out, linear, top_pairs, cotangent)
+    hot_own = load_hot(starts, tables[0], group_count)
+    hot_other = across("shard", hot_own, 1)
+    linear = linear_part(bottom_out, top_dense)
+    sums = [pool_rows(block, hot_own, hot_other, bag) for block in sent_blocks]
+    parts = [sums[0]] + [across("shard", part, step) for part, step in zip(sums[1:], steps[1:])]
+    score_row, pooled = score(parts, bottom_out, linear, top_pairs, cotangent)
     scores = [score_row] + [across("shard", score_row, step) for step in steps[1:]]
     activation, bottom_grad = finish_dense(
         pooled, bottom_out, linear, top_pairs, cotangent, top_dense
@@ -482,6 +483,7 @@
         and is_power(shard_count)
         and tables.shape[1] // group_count % 8 == 0
         and hot_rows <= group_lookups
+        and shard_count % 2 == 0
     )
     plan = by_hot_rows if fits else by_row_sums
     return plan(bottom_out, lookups, starts, tables, top_dense, top_pairs, cotangent)

time: 47.2 us -> 42 us (0.89)
  waiting for transfers between devices: 16.9 us -> 13.1 us
  local copies, waits for them, and re-layouts: 2.2 us -> 0.03 us
  Pallas kernels: 6.63 us -> 8.65 us
  starting transfers between devices: 20.5 us -> 19.3 us
    ppermute x15 -> x14, waiting for transfers between devices: 16.9 us -> 13.1 us  [across(): lax.ppermute(values, axis, [(pos, pos ^ step) for pos in range(size)])]
    unnamed x12 -> x10, local copies, waits for them, and re-layouts: 2.2 us -> 0.03 us
    pallas_call x3 -> x7, Pallas kernels: 2.73 us -> 4.74 us  [the longest x4 1.94 us: pool_rows(): pl.pallas_call(kernel, out_shape=jax.ShapeDtypeStruct((samples, width), j...]
    ppermute x15 -> x14, starting transfers between devices: 20.5 us -> 19.3 us  [across(): lax.ppermute(values, axis, [(pos, pos ^ step) for pos in range(size)])]
  transfers between devices with their start and end apart: 15 -> 14, of which waited for: 8 -> 10; matrix products, arithmetic and copies ran while one was open for 0% -> 0% of each run, Pallas kernels for 6% -> 10%
where the time goes in v3:
time: 42 us; the launch traced here: 41.8 us
  starting transfers between devices  19.3 us (46%)
  waiting for transfers between devices  13.1 us (31%)
  Pallas kernels  8.65 us (21%)
  between operations  0.74 us (2%)
    ppermute x14, starting transfers between devices, across(): lax.ppermute(values, axis, [(pos, pos ^ step) for pos in range(size)])  19.3 us
    ppermute x14, waiting for transfers between devices, across(): lax.ppermute(values, axis, [(pos, pos ^ step) for pos in range(size)])  13.1 us
    pallas_call x4, Pallas kernels, pool_rows(): pl.pallas_call(kernel, out_shape=jax.ShapeDtypeStruct((samples, width), j...  1.94 us
    pallas_call x1, Pallas kernels, load_hot(): pl.pallas_call(kernel, out_shape=jax.ShapeDtypeStruct((group_count * HOT,...  1.81 us
    pallas_call x1, Pallas kernels, place_rows(): pl.pallas_call(kernel, out_shape=jax.ShapeDtypeStruct((win_size, width),...  1.62 us
    pallas_call x1, Pallas kernels, finish_dense(): pl.pallas_call(kernel, out_shape=(jax.ShapeDtypeStruct((samples, hidden),...  1.15 us
  transfers between devices with their start and end apart: 14, of which 10 were waited for; matrix products, arithmetic and copies ran while one was open for 0% of the time, Pallas kernels for 10%

profile of v3, /device:TPU:0, one launch (start us, length us, event | category | flops | bytes accessed | tf_op | source)
XLA Modules:
  0.0 41.8 jit_solution(17042249447071292062)
XLA Ops:
  0.7 1.8 %load_hot.1.own_ref = f32[256,128]{1,0:T(8,128)S(1)} custom-call(s32[4,32]{1,0:T(4,128)} %starts_ref.3, f32[7872,128]{1,0:T(8,128)} %bitcast.5), custom_call_target="tpu_custom_call" | custom-call | flops 1000000 | bytes 1000000 | tf_op jit(solution)/shard_map/load_hot/pallas_call | solution.py:218
  2.5 0.6 %collective-permute-start = (f32[256,128]{1,0:T(8,128)S(1)}, f32[256,128]{1,0:T(8,128)S(1)}, u32[]{:S(2)}, u32[]{:S(2)}) collective-permute-start(f32[256,128]{1,0:T(8,128)S(1)} %load_hot.1.own_ref), channel_id=1, source_target_pairs={{0,1},{1,0},{2,3},{3,2},{4,5},{5,4},{6,7},{7,6},{8,9},{9,8},{10,11... | collective-permute-start | bytes 393224 | tf_op jit(solution)/shard_map/ppermute | solution.py:445
  3.1 0.8 %pack_sent.1.sent_ref.refs_4_ = f32[136,128]{1,0:T(8,128)S(1)} custom-call(s32[4,128]{1,0:T(4,128)} %bitcast.7, bf16[128,128]{1,0:T(8,128)(2,1)} %bottom_ref.5), custom_call_target="tpu_custom_call" | custom-call | flops 1000000 | bytes 100000 | tf_op jit(solution)/shard_map/pack_sent/pallas_call | solution.py:176
  3.8 2.6 %collective-permute-start.1 = (f32[136,128]{1,0:T(8,128)S(1)}, f32[136,128]{1,0:T(8,128)S(1)}, u32[]{:S(2)}, u32[]{:S(2)}) collective-permute-start(f32[136,128]{1,0:T(8,128)S(1)} %pack_sent.1.sent_ref.refs_4_), channel_id=1, source_target_pairs={{0,2},{1,3},{2,0},{3,1},{4,6},{5,7},{6,4},{7,5},{8,10},{9,11},{10,... | collective-permute-start | bytes 208904 | tf_op jit(solution)/shard_map/ppermute | solution.py:445
  6.5 2.6 %collective-permute-start.3 = (f32[136,128]{1,0:T(8,128)S(1)}, f32[136,128]{1,0:T(8,128)S(1)}, u32[]{:S(2)}, u32[]{:S(2)}) collective-permute-start(f32[136,128]{1,0:T(8,128)S(1)} %pack_sent.1.sent_ref.refs_4_), channel_id=1, source_target_pairs={{0,4},{1,5},{2,6},{3,7},{4,0},{5,1},{6,2},{7,3},{8,12},{9,13},{10,... | collective-permute-start | bytes 208904 | tf_op jit(solution)/shard_map/ppermute | solution.py:445
  9.8 1.8 %collective-permute-start.2 = (f32[128,128]{1,0:T(8,128)S(1)}, f32[128,128]{1,0:T(8,128)S(1)}, u32[]{:S(2)}, u32[]{:S(2)}) collective-permute-start(f32[128,128]{1,0:T(8,128)S(1)} %pool_rows.5), channel_id=1, source_target_pairs={{0,2},{1,3},{2,0},{3,1},{4,6},{5,7},{6,4},{7,5},{8,10},{9,11},{10,... | collective-permute-start | bytes 196616 | tf_op jit(solution)/shard_map/ppermute | solution.py:445
  11.6 2.7 %collective-permute-done.3.sent_ref.refs_6_ = f32[136,128]{1,0:T(8,128)S(1)} collective-permute-done((f32[136,128]{1,0:T(8,128)S(1)}, f32[136,128]{1,0:T(8,128)S(1)}, u32[]{:S(2)}, u32[]{:S(2)}) %collective-permute-start.3) | collective-permute-done | bytes 69664 | tf_op jit(solution)/shard_map/ppermute | solution.py:445
  14.8 0.8 %collective-permute-start.4 = (f32[128,128]{1,0:T(8,128)S(1)}, f32[128,128]{1,0:T(8,128)S(1)}, u32[]{:S(2)}, u32[]{:S(2)}) collective-permute-start(f32[128,128]{1,0:T(8,128)S(1)} %pool_rows.6), channel_id=1, source_target_pairs={{0,4},{1,5},{2,6},{3,7},{4,0},{5,1},{6,2},{7,3},{8,12},{9,13},{10,... | collective-permute-start | bytes 196616 | tf_op jit(solution)/shard_map/ppermute | solution.py:445
  16.2 2.8 %collective-permute-start.6 = (f32[128,128]{1,0:T(8,128)S(1)}, f32[128,128]{1,0:T(8,128)S(1)}, u32[]{:S(2)}, u32[]{:S(2)}) collective-permute-start(f32[128,128]{1,0:T(8,128)S(1)} %pool_rows.7), channel_id=1, source_target_pairs={{0,6},{1,7},{2,4},{3,5},{4,2},{5,3},{6,0},{7,1},{8,14},{9,15},{10,... | collective-permute-start | bytes 196616 | tf_op jit(solution)/shard_map/ppermute | solution.py:445
  19.2 0.5 %pool_rows.4.refs_0_ = f32[128,128]{1,0:T(8,128)S(1)} custom-call(f32[136,128]{1,0:T(8,128)S(1)} %pack_sent.1.sent_ref.refs_4_, f32[256,128]{1,0:T(8,128)S(1)} %load_hot.1.own_ref, f32[256,128]{1,0:T(8,128)S(1)} %collective-permute-done.other_ref), custom_call_target="tpu_custom_call" | custom-call | flops 50000000 | bytes 1000000 | tf_op jit(solution)/shard_map/pool_rows/pallas_call | solution.py:267
  19.7 1.9 %collective-permute-done.4.refs_2_ = f32[128,128]{1,0:T(8,128)S(1)} collective-permute-done((f32[128,128]{1,0:T(8,128)S(1)}, f32[128,128]{1,0:T(8,128)S(1)}, u32[]{:S(2)}, u32[]{:S(2)}) %collective-permute-start.4) | collective-permute-done | bytes 65568 | tf_op jit(solution)/shard_map/ppermute | solution.py:445
  21.6 0.8 %collective-permute-done.6.refs_3_ = f32[128,128]{1,0:T(8,128)S(1)} collective-permute-done((f32[128,128]{1,0:T(8,128)S(1)}, f32[128,128]{1,0:T(8,128)S(1)}, u32[]{:S(2)}, u32[]{:S(2)}) %collective-permute-start.6) | collective-permute-done | bytes 65568 | tf_op jit(solution)/shard_map/ppermute | solution.py:445
  22.8 2.9 %collective-permute-start.9 = (f32[1,128]{1,0:T(1,128)S(1)}, f32[1,128]{1,0:T(1,128)S(1)}, u32[]{:S(2)}, u32[]{:S(2)}) collective-permute-start(f32[1,128]{1,0:T(1,128)S(1)} %get-tuple-element.16.refs_0_), channel_id=1, source_target_pairs={{0,6},{1,7},{2,4},{3,5},{4,2},{5,3},{6,0},{7,1},{8,14},{9,15},{10,... | collective-permute-start | bytes 1544 | tf_op jit(solution)/shard_map/ppermute | solution.py:445
  25.8 1.5 %collective-permute-start.7 = (f32[1,128]{1,0:T(1,128)S(1)}, f32[1,128]{1,0:T(1,128)S(1)}, u32[]{:S(2)}, u32[]{:S(2)}) collective-permute-start(f32[1,128]{1,0:T(1,128)S(1)} %get-tuple-element.16.refs_0_), channel_id=1, source_target_pairs={{0,2},{1,3},{2,0},{3,1},{4,6},{5,7},{6,4},{7,5},{8,10},{9,11},{10,... | collective-permute-start | bytes 1544 | tf_op jit(solution)/shard_map/ppermute | solution.py:445
  27.2 1.0 %collective-permute-done.9.refs_3_ = f32[1,128]{1,0:T(1,128)S(1)} collective-permute-done((f32[1,128]{1,0:T(1,128)S(1)}, f32[1,128]{1,0:T(1,128)S(1)}, u32[]{:S(2)}, u32[]{:S(2)}) %collective-permute-start.9) | collective-permute-done | bytes 544 | tf_op jit(solution)/shard_map/ppermute | solution.py:445
  28.2 1.9 %collective-permute-done.8.refs_2_ = f32[1,128]{1,0:T(1,128)S(1)} collective-permute-done((f32[1,128]{1,0:T(1,128)S(1)}, f32[1,128]{1,0:T(1,128)S(1)}, u32[]{:S(2)}, u32[]{:S(2)}) %collective-permute-start.8) | collective-permute-done | bytes 544 | tf_op jit(solution)/shard_map/ppermute | solution.py:445
  30.1 0.7 %row_grads.1 = (f32[256,128]{1,0:T(8,128)S(1)}, f32[256,128]{1,0:T(8,128)S(1)}) custom-call(f32[1,128]{1,0:T(1,128)S(1)} %get-tuple-element.16.refs_0_, f32[1,128]{1,0:T(1,128)S(1)} %collective-permute-done.7.refs_1_, f32[1,128]{1,0:T(1,128)S(1)} %collective-permute-done.8.refs_2_, f32[1,128]{1,0:T(1,128)S(1)} %collective-permute-done.9.refs_3_, ...), custom_call_target="tpu_custom_call" | custom-call | flops 200000000 | bytes 1000000 | tf_op jit(solution)/shard_map/row_grads/pallas_call | solution.py:374
  30.9 1.3 %collective-permute-done.10.other_ref = f32[256,128]{1,0:T(8,128)S(1)} collective-permute-done((f32[256,128]{1,0:T(8,128)S(1)}, f32[256,128]{1,0:T(8,128)S(1)}, u32[]{:S(2)}, u32[]{:S(2)}) %collective-permute-start.10) | collective-permute-done | bytes 131104 | tf_op jit(solution)/shard_map/ppermute | solution.py:445
  32.3 1.6 %collective-permute-start.11 = (f32[64,128]{1,0:T(8,128)S(1)}, f32[64,128]{1,0:T(8,128)S(1)}, u32[]{:S(2)}, u32[]{:S(2)}) collective-permute-start(f32[64,128]{1,0:T(8,128)S(1)} %get-tuple-element.20), channel_id=1, source_target_pairs={{0,8},{8,0},{16,24},{24,16},{1,9},{9,1},{17,25},{25,17},{2,10},{10... | collective-permute-start | bytes 98312 | tf_op jit(solution)/shard_map/ppermute | solution.py:445
  33.8 1.5 %collective-permute-start.12 = (f32[64,128]{1,0:T(8,128)S(1)}, f32[64,128]{1,0:T(8,128)S(1)}, u32[]{:S(2)}, u32[]{:S(2)}) collective-permute-start(f32[64,128]{1,0:T(8,128)S(1)} %get-tuple-element.21), channel_id=1, source_target_pairs={{0,16},{8,24},{16,0},{24,8},{1,17},{9,25},{17,1},{25,9},{2,18},{10... | collective-permute-start | bytes 98312 | tf_op jit(solution)/shard_map/ppermute | solution.py:445
  35.8 1.2 %finish_dense.1 = (bf16[128,1024]{1,0:T(8,128)(2,1)}, f32[128,128]{1,0:T(8,128)}) custom-call(f32[128,128]{1,0:T(8,128)S(1)} %get-tuple-element.13.pooled_ref, bf16[128,128]{1,0:T(8,128)(2,1)S(1)} %copy-done.2, f32[128,1024]{1,0:T(8,128)S(1)} %linear_part.1.refs_5_.linear_ref, f32[1,1024]{1,0:T(1,128)S(1)} %copy-done.3, f32[128,1024]{1,0:T(8,128)S(1)} %copy-done, ...), custom_call_target="tpu_custom_call" | custom-call | flops 50000000 | bytes 1000000 | tf_op jit(solution)/shard_map/finish_dense/pallas_call | solution.py:334
  37.0 0.8 %collective-permute-done.12.refs_2_ = f32[64,128]{1,0:T(8,128)S(1)} collective-permute-done((f32[64,128]{1,0:T(8,128)S(1)}, f32[64,128]{1,0:T(8,128)S(1)}, u32[]{:S(2)}, u32[]{:S(2)}) %collective-permute-start.12) | collective-permute-done | bytes 32800 | tf_op jit(solution)/shard_map/ppermute | solution.py:445
  37.7 2.4 %collective-permute-done.13.refs_3_ = f32[64,128]{1,0:T(8,128)S(1)} collective-permute-done((f32[64,128]{1,0:T(8,128)S(1)}, f32[64,128]{1,0:T(8,128)S(1)}, u32[]{:S(2)}, u32[]{:S(2)}) %collective-permute-start.13) | collective-permute-done | bytes 32800 | tf_op jit(solution)/shard_map/ppermute | solution.py:445
  40.2 1.6 %place_rows.1 = f32[1968,128]{1,0:T(8,128)} custom-call(s32[4,32]{1,0:T(4,128)S(1)} %copy-done.4, f32[64,128]{1,0:T(8,128)S(1)} %get-tuple-element.19.refs_0_, f32[64,128]{1,0:T(8,128)S(1)} %collective-permute-done.11.refs_1_, f32[64,128]{1,0:T(8,128)S(1)} %collective-permute-done.12.refs_2_, f32[64,128]{1,0:T(8,128)S(1)} %collective-permute-done.13.refs_3_), custom_call_target="tpu_custom_call" | custom-call | flops 1000000 | bytes 2000000 | tf_op jit(solution)/shard_map/place_rows/pallas_call | solution.py:424
  (26 shorter events, 3.1 us)
Async XLA Ops:
  0.6 18.4 %copy-start.2 = (bf16[128,128]{1,0:T(8,128)(2,1)S(1)}, bf16[128,128]{1,0:T(8,128)(2,1)}, u32[]{:S(2)}) copy-start(bf16[128,128]{1,0:T(8,128)(2,1)} %bottom_ref.5) | copy-start | bytes 98308
  0.6 18.4 %copy-start.1 = (bf16[128,1024]{1,0:T(8,128)(2,1)S(1)}, bf16[128,1024]{1,0:T(8,128)(2,1)}, u32[]{:S(2)}) copy-start(bf16[128,1024]{1,0:T(8,128)(2,1)} %dense_ref.3) | copy-start | bytes 786436
  0.7 21.7 %copy-start = (f32[128,1024]{1,0:T(8,128)S(1)}, f32[128,1024]{1,0:T(8,128)}, u32[]{:S(2)}) copy-start(f32[128,1024]{1,0:T(8,128)} %cot_ref.1) | copy-start | bytes 1572868
  0.7 21.7 %copy-start.3 = (f32[1,1024]{1,0:T(1,128)S(1)}, f32[1,1024]{1,0:T(1,128)}, u32[]{:S(2)}) copy-start(f32[1,1024]{1,0:T(1,128)} %pairs_ref.1) | copy-start | bytes 12292
  2.5 37.7 %copy-start.4 = (s32[4,32]{1,0:T(4,128)S(1)}, s32[4,32]{1,0:T(4,128)}, u32[]{:S(2)}) copy-start(s32[4,32]{1,0:T(4,128)} %starts_ref.3) | copy-start | bytes 1540
  2.5 6.8 %collective-permute-start = (f32[256,128]{1,0:T(8,128)S(1)}, f32[256,128]{1,0:T(8,128)S(1)}, u32[]{:S(2)}, u32[]{:S(2)}) collective-permute-start(f32[256,128]{1,0:T(8,128)S(1)} %load_hot.1.own_ref), channel_id=1, source_target_pairs={{0,1},{1,0},{2,3},{3,2},{4,5},{5,4},{6,7},{7,6},{8,9},{9,8},{10,11... | collective-permute-start | bytes 393224 | tf_op jit(solution)/shard_map/ppermute | solution.py:445
  3.8 5.5 %collective-permute-start.1 = (f32[136,128]{1,0:T(8,128)S(1)}, f32[136,128]{1,0:T(8,128)S(1)}, u32[]{:S(2)}, u32[]{:S(2)}) collective-permute-start(f32[136,128]{1,0:T(8,128)S(1)} %pack_sent.1.sent_ref.refs_4_), channel_id=1, source_target_pairs={{0,2},{1,3},{2,0},{3,1},{4,6},{5,7},{6,4},{7,5},{8,10},{9,11},{10,... | collective-permute-start | bytes 208904 | tf_op jit(solution)/shard_map/ppermute | solution.py:445
  6.5 7.9 %collective-permute-start.3 = (f32[136,128]{1,0:T(8,128)S(1)}, f32[136,128]{1,0:T(8,128)S(1)}, u32[]{:S(2)}, u32[]{:S(2)}) collective-permute-start(f32[136,128]{1,0:T(8,128)S(1)} %pack_sent.1.sent_ref.refs_4_), channel_id=1, source_target_pairs={{0,4},{1,5},{2,6},{3,7},{4,0},{5,1},{6,2},{7,3},{8,12},{9,13},{10,... | collective-permute-start | bytes 208904 | tf_op jit(solution)/shard_map/ppermute | solution.py:445
  9.1 6.7 %collective-permute-start.5 = (f32[136,128]{1,0:T(8,128)S(1)}, f32[136,128]{1,0:T(8,128)S(1)}, u32[]{:S(2)}, u32[]{:S(2)}) collective-permute-start(f32[136,128]{1,0:T(8,128)S(1)} %pack_sent.1.sent_ref.refs_4_), channel_id=1, source_target_pairs={{0,6},{1,7},{2,4},{3,5},{4,2},{5,3},{6,0},{7,1},{8,14},{9,15},{10,... | collective-permute-start | bytes 208904 | tf_op jit(solution)/shard_map/ppermute | solution.py:445
  9.8 9.9 %collective-permute-start.2 = (f32[128,128]{1,0:T(8,128)S(1)}, f32[128,128]{1,0:T(8,128)S(1)}, u32[]{:S(2)}, u32[]{:S(2)}) collective-permute-start(f32[128,128]{1,0:T(8,128)S(1)} %pool_rows.5), channel_id=1, source_target_pairs={{0,2},{1,3},{2,0},{3,1},{4,6},{5,7},{6,4},{7,5},{8,10},{9,11},{10,... | collective-permute-start | bytes 196616 | tf_op jit(solution)/shard_map/ppermute | solution.py:445
  14.8 6.8 %collective-permute-start.4 = (f32[128,128]{1,0:T(8,128)S(1)}, f32[128,128]{1,0:T(8,128)S(1)}, u32[]{:S(2)}, u32[]{:S(2)}) collective-permute-start(f32[128,128]{1,0:T(8,128)S(1)} %pool_rows.6), channel_id=1, source_target_pairs={{0,4},{1,5},{2,6},{3,7},{4,0},{5,1},{6,2},{7,3},{8,12},{9,13},{10,... | collective-permute-start | bytes 196616 | tf_op jit(solution)/shard_map/ppermute | solution.py:445
  16.2 6.1 %collective-permute-start.6 = (f32[128,128]{1,0:T(8,128)S(1)}, f32[128,128]{1,0:T(8,128)S(1)}, u32[]{:S(2)}, u32[]{:S(2)}) collective-permute-start(f32[128,128]{1,0:T(8,128)S(1)} %pool_rows.7), channel_id=1, source_target_pairs={{0,6},{1,7},{2,4},{3,5},{4,2},{5,3},{6,0},{7,1},{8,14},{9,15},{10,... | collective-permute-start | bytes 196616 | tf_op jit(solution)/shard_map/ppermute | solution.py:445
  22.8 5.4 %collective-permute-start.9 = (f32[1,128]{1,0:T(1,128)S(1)}, f32[1,128]{1,0:T(1,128)S(1)}, u32[]{:S(2)}, u32[]{:S(2)}) collective-permute-start(f32[1,128]{1,0:T(1,128)S(1)} %get-tuple-element.16.refs_0_), channel_id=1, source_target_pairs={{0,6},{1,7},{2,4},{3,5},{4,2},{5,3},{6,0},{7,1},{8,14},{9,15},{10,... | collective-permute-start | bytes 1544 | tf_op jit(solution)/shard_map/ppermute | solution.py:445
  25.7 4.5 %collective-permute-start.8 = (f32[1,128]{1,0:T(1,128)S(1)}, f32[1,128]{1,0:T(1,128)S(1)}, u32[]{:S(2)}, u32[]{:S(2)}) collective-permute-start(f32[1,128]{1,0:T(1,128)S(1)} %get-tuple-element.16.refs_0_), channel_id=1, source_target_pairs={{0,4},{1,5},{2,6},{3,7},{4,0},{5,1},{6,2},{7,3},{8,12},{9,13},{10,... | collective-permute-start | bytes 1544 | tf_op jit(solution)/shard_map/ppermute | solution.py:445
  25.8 4.4 %collective-permute-start.7 = (f32[1,128]{1,0:T(1,128)S(1)}, f32[1,128]{1,0:T(1,128)S(1)}, u32[]{:S(2)}, u32[]{:S(2)}) collective-permute-start(f32[1,128]{1,0:T(1,128)S(1)} %get-tuple-element.16.refs_0_), channel_id=1, source_target_pairs={{0,2},{1,3},{2,0},{3,1},{4,6},{5,7},{6,4},{7,5},{8,10},{9,11},{10,... | collective-permute-start | bytes 1544 | tf_op jit(solution)/shard_map/ppermute | solution.py:445
  30.8 1.4 %collective-permute-start.10 = (f32[256,128]{1,0:T(8,128)S(1)}, f32[256,128]{1,0:T(8,128)S(1)}, u32[]{:S(2)}, u32[]{:S(2)}) collective-permute-start(f32[256,128]{1,0:T(8,128)S(1)} %get-tuple-element.18), channel_id=1, source_target_pairs={{0,1},{1,0},{2,3},{3,2},{4,5},{5,4},{6,7},{7,6},{8,9},{9,8},{10,11... | collective-permute-start | bytes 393224 | tf_op jit(solution)/shard_map/ppermute | solution.py:445
  32.3 4.7 %collective-permute-start.11 = (f32[64,128]{1,0:T(8,128)S(1)}, f32[64,128]{1,0:T(8,128)S(1)}, u32[]{:S(2)}, u32[]{:S(2)}) collective-permute-start(f32[64,128]{1,0:T(8,128)S(1)} %get-tuple-element.20), channel_id=1, source_target_pairs={{0,8},{8,0},{16,24},{24,16},{1,9},{9,1},{17,25},{25,17},{2,10},{10... | collective-permute-start | bytes 98312 | tf_op jit(solution)/shard_map/ppermute | solution.py:445
  33.8 3.9 %collective-permute-start.12 = (f32[64,128]{1,0:T(8,128)S(1)}, f32[64,128]{1,0:T(8,128)S(1)}, u32[]{:S(2)}, u32[]{:S(2)}) collective-permute-start(f32[64,128]{1,0:T(8,128)S(1)} %get-tuple-element.21), channel_id=1, source_target_pairs={{0,16},{8,24},{16,0},{24,8},{1,17},{9,25},{17,1},{25,9},{2,18},{10... | collective-permute-start | bytes 98312 | tf_op jit(solution)/shard_map/ppermute | solution.py:445
  35.4 4.8 %collective-permute-start.13 = (f32[64,128]{1,0:T(8,128)S(1)}, f32[64,128]{1,0:T(8,128)S(1)}, u32[]{:S(2)}, u32[]{:S(2)}) collective-permute-start(f32[64,128]{1,0:T(8,128)S(1)} %get-tuple-element.22), channel_id=1, source_target_pairs={{0,24},{8,16},{16,8},{24,0},{1,25},{9,17},{17,9},{25,1},{2,26},{10... | collective-permute-start | bytes 98312 | tf_op jit(solution)/shard_map/ppermute | solution.py:445

commit v4 on v3

--- a/solution.py
+++ b/solution.py
@@ -160,36 +160,14 @@
     return pltpu.with_memory_space_constraint(values, pltpu.HBM)
 
 
-def pack_sent(looked, bottom_out, win_size):
-    samples, width = bottom_out.shape
-    bag = looked.shape[0]
-
-    def kernel(looked_ref, bottom_ref, sent_ref):
-        found = looked_ref[...]
-        window_of = jnp.floor((found.astype(jnp.float32) + 0.5) * (1.0 / win_size)).astype(jnp.int32)
-        places = (found - window_of * (win_size - HOT)).astype(jnp.float32)
-        sent_ref[pl.ds(samples, 8), :] = jnp.concatenate(
-            [places, jnp.zeros((8 - bag, samples), jnp.float32)], axis=0
-        )
-        sent_ref[pl.ds(0, samples), :] = bottom_ref[...].astype(jnp.float32)
-
-    return pl.pallas_call(
-        kernel,
-        out_shape=jax.ShapeDtypeStruct((samples + 8, width), jnp.float32),
-        in_specs=[whole()] * 2,
-        out_specs=whole(),
-        cost_estimate=cost(1e6, 1e5),
-        compiler_params=pltpu.CompilerParams(vmem_limit_bytes=GRANT),
-        name="pack_sent",
-    )(stay(looked), stay(bottom_out))
-
-
-def load_hot(starts, table, group_count):
+def load_first(starts, looked, bottom_out, table, group_count):
     span_rows, width = table.shape
     win_size = span_rows // group_count
+    samples = bottom_out.shape[0]
+    bag = looked.shape[0]
     head = min(HOT + 8, win_size)
 
-    def kernel(starts_ref, table_ref, hot_ref, held, sems):
+    def kernel(starts_ref, looked_ref, bottom_ref, table_ref, hot_ref, places_ref, wide_ref, held, sems):
         grp_pos = lax.axis_index("grp")
         shard_pos = lax.axis_index("shard")
         shifts = []
@@ -210,6 +188,13 @@
             first.start()
             second.start()
             copies += [first, second]
+        found = looked_ref[...]
+        window_of = jnp.floor((found.astype(jnp.float32) + 0.5) * (1.0 / win_size)).astype(jnp.int32)
+        places = (found - window_of * (win_size - HOT)).astype(jnp.float32)
+        places_ref[...] = jnp.concatenate(
+            [places, jnp.zeros((8 - bag, samples), jnp.float32)], axis=0
+        )
+        wide_ref[...] = bottom_ref[...].astype(jnp.float32)
         for copy in copies:
             copy.wait()
         for window in range(group_count):
@@ -217,17 +202,21 @@
 
     return pl.pallas_call(
         kernel,
-        out_shape=jax.ShapeDtypeStruct((group_count * HOT, width), jnp.float32),
-        in_specs=[whole(pltpu.SMEM), whole(pl.ANY)],
-        out_specs=whole(),
+        out_shape=(
+            jax.ShapeDtypeStruct((group_count * HOT, width), jnp.float32),
+            jax.ShapeDtypeStruct((8, samples), jnp.float32),
+            jax.ShapeDtypeStruct((samples, width), jnp.float32),
+        ),
+        in_specs=[whole(pltpu.SMEM), whole(), whole(), whole(pl.ANY)],
+        out_specs=(whole(), whole(), whole()),
         scratch_shapes=[
             pltpu.VMEM((group_count, head + HOT, width), jnp.float32),
             pltpu.SemaphoreType.DMA((group_count, 2)),
         ],
         cost_estimate=cost(1e6, 1e6),
         compiler_params=pltpu.CompilerParams(vmem_limit_bytes=GRANT),
-        name="load_hot",
-    )(stay(starts), stay(table))
+        name="load_first",
+    )(stay(starts), stay(looked), stay(bottom_out), stay(table))
 
 
 def linear_part(bottom_out, top_dense):
@@ -245,15 +234,15 @@
     )(bottom_out, top_dense)
 
 
-def pool_rows(sent, hot_own, hot_other, bag):
+def pool_rows(places, hot_own, hot_other, bag):
     block_rows, width = hot_own.shape
-    samples = sent.shape[0] - 8
-
-    def kernel(sent_ref, own_ref, other_ref, part_ref):
+    samples = places.shape[1]
+
+    def kernel(places_ref, own_ref, other_ref, part_ref):
         shard_pos = lax.axis_index("shard")
         rows = lax.broadcasted_iota(jnp.int32, (samples, block_rows), 1).astype(jnp.float32)
         columns = jnp.concatenate(
-            [sent_ref[pl.ds(samples, 8), :], jnp.zeros((samples - 8, samples), jnp.float32)], axis=0
+            [places_ref[...], jnp.zeros((samples - 8, samples), jnp.float32)], axis=0
         ).T
         total = jnp.zeros((samples, width), jnp.float32)
         for side, ref in enumerate((own_ref, other_ref)):
@@ -272,7 +261,7 @@
         cost_estimate=cost(5e7, 1e6),
         compiler_params=pltpu.CompilerParams(vmem_limit_bytes=GRANT),
         name="pool_rows",
-    )(sent, hot_own, hot_other)
+    )(places, hot_own, hot_other)
 
 
 def head_terms(pooled, bottom_ref, linear_ref, pairs_ref, cot_ref):
@@ -345,51 +334,49 @@
     )(pooled, bottom_out, linear, top_pairs, cotangent, top_dense)
 
 
-def row_grads(scores, sent, bag, block_rows):
-    samples = scores[0].shape[1]
-    width = sent[0].shape[1]
+def row_grads(scores, places, wides, bag, group_count, kept):
+    samples, width = wides[0].shape
     count = len(scores)
 
     def kernel(*refs):
-        score_refs = refs[:count]
-        sent_refs = refs[count : 2 * count]
-        own_ref, other_ref = refs[2 * count :]
+        score_refs, place_refs, wide_refs = refs[:count], refs[count : 2 * count], refs[2 * count : -1]
+        grp_pos = lax.axis_index("grp")
         shard_pos = lax.axis_index("shard")
-        rows = lax.broadcasted_iota(jnp.int32, (block_rows, samples), 0).astype(jnp.float32)
-        for side, out_ref in ((1, other_ref), (0, own_ref)):
-            base = (jnp.bitwise_xor(shard_pos, side) * block_rows).astype(jnp.float32)
-            total = jnp.zeros((block_rows, width), jnp.float32)
-            for score_ref, sent_ref in zip(score_refs, sent_refs):
-                places = sent_ref[pl.ds(samples, 8), :] - base
-                times = jnp.zeros((block_rows, samples), jnp.float32)
-                for slot in range(bag):
-                    times += jnp.where(places[slot : slot + 1, :] == rows, 1.0, 0.0)
-                high, low = two_terms(times * score_ref[...])
-                bottom = sent_ref[pl.ds(0, samples), :].astype(jnp.bfloat16)
-                total += jnp.dot(high, bottom, preferred_element_type=jnp.float32)
-                total += jnp.dot(low, bottom, preferred_element_type=jnp.float32)
-            out_ref[...] = total
-
-    part = jax.ShapeDtypeStruct((block_rows, width), jnp.float32)
-    return pl.pallas_call(
-        kernel,
-        out_shape=(part, part),
-        in_specs=[whole()] * (2 * count),
-        out_specs=(whole(), whole()),
-        cost_estimate=cost(2e8, 1e6),
-        compiler_params=pltpu.CompilerParams(vmem_limit_bytes=GRANT),
-        name="row_grads",
-    )(*scores, *sent)
-
-
-def split_owners(grad_own, grad_other, group_count):
-    width = grad_own.shape[1]
-
-    def kernel(own_ref, other_ref, *out_refs):
-        grp_pos = lax.axis_index("grp")
+        ids = []
+        for step in range(group_count):
+            holder = shard_pos if kept == (step == 0) else jnp.bitwise_xor(shard_pos, 1)
+            first = (holder * group_count + jnp.bitwise_xor(grp_pos, step)) * HOT
+            ids.append(lax.broadcasted_iota(jnp.int32, (HOT, samples), 0) + first)
+        rows = jnp.concatenate(ids, axis=0).astype(jnp.float32)
+        total = jnp.zeros((group_count * HOT, width), jnp.float32)
+        for score_ref, place_ref, wide_ref in zip(score_refs, place_refs, wide_refs):
+            times = jnp.zeros(rows.shape, jnp.float32)
+            for slot in range(bag):
+                times += jnp.where(place_ref[pl.ds(slot, 1), :] == rows, 1.0, 0.0)
+            high, low = two_terms(times * score_ref[...])
+            bottom = wide_ref[...].astype(jnp.bfloat16)
+            total += jnp.dot(high, bottom, preferred_element_type=jnp.float32)
+            total += jnp.dot(low, bottom, preferred_element_type=jnp.float32)
+        refs[-1][...] = total
+
+    return pl.pallas_call(
+        kernel,
+        out_shape=jax.ShapeDtypeStruct((group_count * HOT, width), jnp.float32),
+        in_specs=[whole()] * (3 * count),
+        out_specs=whole(),
+        cost_estimate=cost(1e8, 1e6),
+        compiler_params=pltpu.CompilerParams(vmem_limit_bytes=GRANT),
+        name="row_grads_kept" if kept else "row_grads_given",
+    )(*scores, *places, *wides)
+
+
+def split_owners(kept, received, group_count):
+    width = kept.shape[1]
+
+    def kernel(kept_ref, received_ref, *out_refs):
         for step, out_ref in enumerate(out_refs):
-            first = pl.multiple_of(jnp.bitwise_xor(grp_pos, step) * HOT, HOT)
-            out_ref[...] = own_ref[pl.ds(first, HOT), :] + other_ref[pl.ds(first, HOT), :]
+            chosen = pl.ds(step * HOT, HOT)
+            out_ref[...] = kept_ref[chosen, :] + received_ref[chosen, :]
 
     part = jax.ShapeDtypeStruct((HOT, width), jnp.float32)
     return pl.pallas_call(
@@ -400,7 +387,7 @@
         cost_estimate=cost(1e6, 1e6),
         compiler_params=pltpu.CompilerParams(vmem_limit_bytes=GRANT),
         name="split_owners",
-    )(grad_own, grad_other)
+    )(kept, received)
 
 
 def place_rows(starts, blocks, win_size):
@@ -438,30 +425,39 @@
     shard_count = lax.axis_size("shard")
     bag = lookups.shape[2]
     win_size = tables.shape[1] // group_count
-    block_rows = group_count * HOT
-
-    def across(axis, values, step):
-        size = lax.axis_size(axis)
-        return lax.ppermute(values, axis, [(pos, pos ^ step) for pos in range(size)])
-
-    steps = list(range(0, shard_count, 2))
+
+    def across(label, values, grp_step, shard_step):
+        pairs = [
+            (grp * shard_count + shard, (grp ^ grp_step) * shard_count + (shard ^ shard_step))
+            for grp in range(group_count)
+            for shard in range(shard_count)
+        ]
+        with jax.named_scope(label):
+            return lax.ppermute(values, ("grp", "shard"), pairs)
+
+    steps = list(range(shard_count - 1, 1, -2))
     looked = lookups[:, 0, :].T
-    sent = pack_sent(looked, bottom_out, win_size)
-    sent_blocks = [sent] + [across("shard", sent, step) for step in steps[1:]]
-    hot_own = load_hot(starts, tables[0], group_count)
-    hot_other = across("shard", hot_own, 1)
+    hot_own, places_own, wide_own = load_first(starts, looked, bottom_out, tables[0], group_count)
+    hot_other = across("hot", hot_own, 0, 1)
+    places = [places_own] + [across(f"place{step}", places_own, 0, step) for step in steps]
     linear = linear_part(bottom_out, top_dense)
-    sums = [pool_rows(block, hot_own, hot_other, bag) for block in sent_blocks]
-    parts = [sums[0]] + [across("shard", part, step) for part, step in zip(sums[1:], steps[1:])]
+    sums = [pool_rows(block, hot_own, hot_other, bag) for block in places]
+    parts = [sums[0]] + [
+        across(f"part{step}", part, 0, step) for part, step in zip(sums[1:], steps)
+    ]
+    wides = [wide_own] + [across(f"wide{step}", wide_own, 0, step) for step in steps]
     score_row, pooled = score(parts, bottom_out, linear, top_pairs, cotangent)
-    scores = [score_row] + [across("shard", score_row, step) for step in steps[1:]]
+    scores = [score_row] + [across(f"score{step}", score_row, 0, step) for step in steps]
     activation, bottom_grad = finish_dense(
         pooled, bottom_out, linear, top_pairs, cotangent, top_dense
     )
-    grad_own, grad_other = row_grads(scores, sent_blocks, bag, block_rows)
-    grad_back = across("shard", grad_other, 1)
-    owned = split_owners(grad_own, grad_back, group_count)
-    blocks = [owned[0]] + [across("grp", owned[step], step) for step in range(1, group_count)]
+    given = row_grads(scores, places, wides, bag, group_count, False)
+    received = across("rows", given, 0, 1)
+    kept = row_grads(scores, places, wides, bag, group_count, True)
+    owned = split_owners(kept, received, group_count)
+    blocks = [owned[0]] + [
+        across(f"owned{step}", owned[step], step, 1) for step in range(1, group_count)
+    ]
     table_grad = place_rows(starts, blocks, win_size)
     return activation, bottom_grad, table_grad[None, None]
 

time: 42 us -> 43.2 us (1.029)
  starting transfers between devices: 19.3 us -> 21.6 us
  Pallas kernels: 8.65 us -> 8.05 us
  waiting for transfers between devices: 13.1 us -> 12.6 us
    ppermute x14 -> x17, starting transfers between devices: 19.3 us -> 21.6 us  [across(): return lax.ppermute(values, ('grp', 'shard'), pairs)]
    pallas_call x3, Pallas kernels: 3.3 us -> 2.69 us  [the longest x1 1.84 us: load_first(): pl.pallas_call(kernel, out_shape=(jax.ShapeDtypeStruct((group_count * HOT...]
    ppermute x14 -> x17, waiting for transfers between devices: 13.1 us -> 12.6 us  [across(): return lax.ppermute(values, ('grp', 'shard'), pairs)]
  transfers between devices with their start and end apart: 14 -> 17, of which waited for: 10 -> 9; matrix products, arithmetic and copies ran while one was open for 0% -> 0% of each run, Pallas kernels for 10% -> 9%
where the time goes in v4:
time: 43.2 us; the launch traced here: 43 us
  starting transfers between devices  21.6 us (50%)
  waiting for transfers between devices  12.6 us (29%)
  Pallas kernels  8.05 us (19%)
  between operations  0.75 us (2%)
    ppermute x17, starting transfers between devices, across(): return lax.ppermute(values, ('grp', 'shard'), pairs)  21.6 us
    ppermute x17, waiting for transfers between devices, across(): return lax.ppermute(values, ('grp', 'shard'), pairs)  12.6 us
    pallas_call x4, Pallas kernels, pool_rows(): pl.pallas_call(kernel, out_shape=jax.ShapeDtypeStruct((samples, width), j...  1.94 us
    pallas_call x1, Pallas kernels, load_first(): pl.pallas_call(kernel, out_shape=(jax.ShapeDtypeStruct((group_count * HOT...  1.84 us
    pallas_call x1, Pallas kernels, place_rows(): pl.pallas_call(kernel, out_shape=jax.ShapeDtypeStruct((win_size, width),...  1.62 us
    pallas_call x1, Pallas kernels, finish_dense(): pl.pallas_call(kernel, out_shape=(jax.ShapeDtypeStruct((samples, hidden),...  1.15 us
  transfers between devices with their start and end apart: 17, of which 9 were waited for; matrix products, arithmetic and copies ran while one was open for 0% of the time, Pallas kernels for 9%

profile of v4, /device:TPU:0, one launch (start us, length us, event | category | flops | bytes accessed | tf_op | source)
XLA Modules:
  0.0 43.0 jit_solution(16368880395145967300)
XLA Ops:
  0.7 1.8 %load_first.1 = (f32[256,128]{1,0:T(8,128)S(1)}, f32[8,128]{1,0:T(8,128)S(1)}, f32[128,128]{1,0:T(8,128)S(1)}) custom-call(s32[4,32]{1,0:T(4,128)} %starts_ref.3, s32[4,128]{1,0:T(4,128)} %bitcast.7, bf16[128,128]{1,0:T(8,128)(2,1)} %bottom_ref.5, f32[7872,128]{1,0:T(8,128)} %bitcast.5), custom_call_target="tpu_custom_call" | custom-call | flops 1000000 | bytes 1000000 | tf_op jit(solution)/shard_map/load_first/pallas_call | solution.py:203
  2.5 0.6 %collective-permute-start = (f32[256,128]{1,0:T(8,128)S(1)}, f32[256,128]{1,0:T(8,128)S(1)}, u32[]{:S(2)}, u32[]{:S(2)}) collective-permute-start(f32[256,128]{1,0:T(8,128)S(1)} %get-tuple-element.15.own_ref), channel_id=1, source_target_pairs={{0,1},{1,0},{2,3},{3,2},{4,5},{5,4},{6,7},{7,6},{8,9},{9,8},{10,11... | collective-permute-start | bytes 393224 | tf_op jit(solution)/shard_map/hot/ppermute | solution.py:436
  3.1 4.7 %collective-permute-start.1 = (f32[8,128]{1,0:T(8,128)S(1)}, f32[8,128]{1,0:T(8,128)S(1)}, u32[]{:S(2)}, u32[]{:S(2)}) collective-permute-start(f32[8,128]{1,0:T(8,128)S(1)} %get-tuple-element.14.places_ref.refs_4_), channel_id=1, source_target_pairs={{0,7},{1,6},{2,5},{3,4},{4,3},{5,2},{6,1},{7,0},{8,15},{9,14},{10,... | collective-permute-start | bytes 12296 | tf_op jit(solution)/shard_map/place7/ppermute | solution.py:436
  7.8 1.3 %collective-permute-done.1.places_ref.refs_5_ = f32[8,128]{1,0:T(8,128)S(1)} collective-permute-done((f32[8,128]{1,0:T(8,128)S(1)}, f32[8,128]{1,0:T(8,128)S(1)}, u32[]{:S(2)}, u32[]{:S(2)}) %collective-permute-start.1) | collective-permute-done | bytes 4128 | tf_op jit(solution)/shard_map/place7/ppermute | solution.py:436
  9.1 0.5 %pool_rows.5 = f32[128,128]{1,0:T(8,128)S(1)} custom-call(f32[8,128]{1,0:T(8,128)S(1)} %collective-permute-done.1.places_ref.refs_5_, f32[256,128]{1,0:T(8,128)S(1)} %get-tuple-element.15.own_ref, f32[256,128]{1,0:T(8,128)S(1)} %collective-permute-done.other_ref), custom_call_target="tpu_custom_call" | custom-call | flops 50000000 | bytes 1000000 | tf_op jit(solution)/shard_map/pool_rows/pallas_call | solution.py:256
  9.6 3.6 %collective-permute-start.2 = (f32[128,128]{1,0:T(8,128)S(1)}, f32[128,128]{1,0:T(8,128)S(1)}, u32[]{:S(2)}, u32[]{:S(2)}) collective-permute-start(f32[128,128]{1,0:T(8,128)S(1)} %pool_rows.5), channel_id=1, source_target_pairs={{0,7},{1,6},{2,5},{3,4},{4,3},{5,2},{6,1},{7,0},{8,15},{9,14},{10,... | collective-permute-start | bytes 196616 | tf_op jit(solution)/shard_map/part7/ppermute | solution.py:436
  13.5 3.6 %collective-permute-done.3.places_ref.refs_6_ = f32[8,128]{1,0:T(8,128)S(1)} collective-permute-done((f32[8,128]{1,0:T(8,128)S(1)}, f32[8,128]{1,0:T(8,128)S(1)}, u32[]{:S(2)}, u32[]{:S(2)}) %collective-permute-start.3) | collective-permute-done | bytes 4128 | tf_op jit(solution)/shard_map/place5/ppermute | solution.py:436
  17.6 0.9 %collective-permute-start.4 = (f32[128,128]{1,0:T(8,128)S(1)}, f32[128,128]{1,0:T(8,128)S(1)}, u32[]{:S(2)}, u32[]{:S(2)}) collective-permute-start(f32[128,128]{1,0:T(8,128)S(1)} %pool_rows.6), channel_id=1, source_target_pairs={{0,5},{1,4},{2,7},{3,6},{4,1},{5,0},{6,3},{7,2},{8,13},{9,12},{10,... | collective-permute-start | bytes 196616 | tf_op jit(solution)/shard_map/part5/ppermute | solution.py:436
  18.5 0.5 %pool_rows.7 = f32[128,128]{1,0:T(8,128)S(1)} custom-call(f32[8,128]{1,0:T(8,128)S(1)} %collective-permute-done.5.places_ref.refs_7_, f32[256,128]{1,0:T(8,128)S(1)} %get-tuple-element.15.own_ref, f32[256,128]{1,0:T(8,128)S(1)} %collective-permute-done.other_ref), custom_call_target="tpu_custom_call" | custom-call | flops 50000000 | bytes 1000000 | tf_op jit(solution)/shard_map/pool_rows/pallas_call | solution.py:256
  19.1 1.7 %collective-permute-start.12 = (f32[128,128]{1,0:T(8,128)S(1)}, f32[128,128]{1,0:T(8,128)S(1)}, u32[]{:S(2)}, u32[]{:S(2)}) collective-permute-start(f32[128,128]{1,0:T(8,128)S(1)} %get-tuple-element.20.refs_8_), channel_id=1, source_target_pairs={{0,3},{1,2},{2,1},{3,0},{4,7},{5,6},{6,5},{7,4},{8,11},{9,10},{10,... | collective-permute-start | bytes 196616 | tf_op jit(solution)/shard_map/wide3/ppermute | solution.py:436
  20.8 1.8 %collective-permute-start.11 = (f32[128,128]{1,0:T(8,128)S(1)}, f32[128,128]{1,0:T(8,128)S(1)}, u32[]{:S(2)}, u32[]{:S(2)}) collective-permute-start(f32[128,128]{1,0:T(8,128)S(1)} %get-tuple-element.20.refs_8_), channel_id=1, source_target_pairs={{0,5},{1,4},{2,7},{3,6},{4,1},{5,0},{6,3},{7,2},{8,13},{9,12},{10,... | collective-permute-start | bytes 196616 | tf_op jit(solution)/shard_map/wide5/ppermute | solution.py:436
  23.1 0.5 %pool_rows.4.refs_0_ = f32[128,128]{1,0:T(8,128)S(1)} custom-call(f32[8,128]{1,0:T(8,128)S(1)} %get-tuple-element.14.places_ref.refs_4_, f32[256,128]{1,0:T(8,128)S(1)} %get-tuple-element.15.own_ref, f32[256,128]{1,0:T(8,128)S(1)} %collective-permute-done.other_ref), custom_call_target="tpu_custom_call" | custom-call | flops 50000000 | bytes 1000000 | tf_op jit(solution)/shard_map/pool_rows/pallas_call | solution.py:256
  23.6 0.7 %collective-permute-done.6.refs_3_ = f32[128,128]{1,0:T(8,128)S(1)} collective-permute-done((f32[128,128]{1,0:T(8,128)S(1)}, f32[128,128]{1,0:T(8,128)S(1)}, u32[]{:S(2)}, u32[]{:S(2)}) %collective-permute-start.6) | collective-permute-done | bytes 65568 | tf_op jit(solution)/shard_map/part3/ppermute | solution.py:436
  24.9 2.7 %collective-permute-start.8 = (f32[1,128]{1,0:T(1,128)S(1)}, f32[1,128]{1,0:T(1,128)S(1)}, u32[]{:S(2)}, u32[]{:S(2)}) collective-permute-start(f32[1,128]{1,0:T(1,128)S(1)} %get-tuple-element.19.refs_0_), channel_id=1, source_target_pairs={{0,5},{1,4},{2,7},{3,6},{4,1},{5,0},{6,3},{7,2},{8,13},{9,12},{10,... | collective-permute-start | bytes 1544 | tf_op jit(solution)/shard_map/score5/ppermute | solution.py:436
  27.6 1.0 %collective-permute-start.7 = (f32[1,128]{1,0:T(1,128)S(1)}, f32[1,128]{1,0:T(1,128)S(1)}, u32[]{:S(2)}, u32[]{:S(2)}) collective-permute-start(f32[1,128]{1,0:T(1,128)S(1)} %get-tuple-element.19.refs_0_), channel_id=1, source_target_pairs={{0,7},{1,6},{2,5},{3,4},{4,3},{5,2},{6,1},{7,0},{8,15},{9,14},{10,... | collective-permute-start | bytes 1544 | tf_op jit(solution)/shard_map/score7/ppermute | solution.py:436
  28.9 1.3 %collective-permute-done.8.refs_2_ = f32[1,128]{1,0:T(1,128)S(1)} collective-permute-done((f32[1,128]{1,0:T(1,128)S(1)}, f32[1,128]{1,0:T(1,128)S(1)}, u32[]{:S(2)}, u32[]{:S(2)}) %collective-permute-start.8) | collective-permute-done | bytes 544 | tf_op jit(solution)/shard_map/score5/ppermute | solution.py:436
  30.1 2.3 %collective-permute-done.7.refs_1_ = f32[1,128]{1,0:T(1,128)S(1)} collective-permute-done((f32[1,128]{1,0:T(1,128)S(1)}, f32[1,128]{1,0:T(1,128)S(1)}, u32[]{:S(2)}, u32[]{:S(2)}) %collective-permute-start.7) | collective-permute-done | bytes 544 | tf_op jit(solution)/shard_map/score7/ppermute | solution.py:436
  33.8 0.5 %collective-permute-done.13.received_ref = f32[256,128]{1,0:T(8,128)S(1)} collective-permute-done((f32[256,128]{1,0:T(8,128)S(1)}, f32[256,128]{1,0:T(8,128)S(1)}, u32[]{:S(2)}, u32[]{:S(2)}) %collective-permute-start.13) | collective-permute-done | bytes 131104 | tf_op jit(solution)/shard_map/rows/ppermute | solution.py:436
  34.4 1.5 %collective-permute-start.14 = (f32[64,128]{1,0:T(8,128)S(1)}, f32[64,128]{1,0:T(8,128)S(1)}, u32[]{:S(2)}, u32[]{:S(2)}) collective-permute-start(f32[64,128]{1,0:T(8,128)S(1)} %get-tuple-element.22), channel_id=1, source_target_pairs={{0,9},{1,8},{2,11},{3,10},{4,13},{5,12},{6,15},{7,14},{8,1},{9,0},... | collective-permute-start | bytes 98312 | tf_op jit(solution)/shard_map/owned1/ppermute | solution.py:436
  35.9 1.3 %collective-permute-start.15 = (f32[64,128]{1,0:T(8,128)S(1)}, f32[64,128]{1,0:T(8,128)S(1)}, u32[]{:S(2)}, u32[]{:S(2)}) collective-permute-start(f32[64,128]{1,0:T(8,128)S(1)} %get-tuple-element.23), channel_id=1, source_target_pairs={{0,17},{1,16},{2,19},{3,18},{4,21},{5,20},{6,23},{7,22},{8,25},{9,... | collective-permute-start | bytes 98312 | tf_op jit(solution)/shard_map/owned2/ppermute | solution.py:436
  37.6 1.1 %finish_dense.1 = (bf16[128,1024]{1,0:T(8,128)(2,1)}, f32[128,128]{1,0:T(8,128)}) custom-call(f32[128,128]{1,0:T(8,128)S(1)} %get-tuple-element.16.pooled_ref, bf16[128,128]{1,0:T(8,128)(2,1)S(1)} %copy-done.2, f32[128,1024]{1,0:T(8,128)S(1)} %linear_part.1.refs_5_.linear_ref, f32[1,1024]{1,0:T(1,128)S(1)} %copy-done.3, f32[128,1024]{1,0:T(8,128)S(1)} %copy-done, ...), custom_call_target="tpu_custom_call" | custom-call | flops 50000000 | bytes 1000000 | tf_op jit(solution)/shard_map/finish_dense/pallas_call | solution.py:323
  38.7 0.5 %collective-permute-done.15.refs_2_ = f32[64,128]{1,0:T(8,128)S(1)} collective-permute-done((f32[64,128]{1,0:T(8,128)S(1)}, f32[64,128]{1,0:T(8,128)S(1)}, u32[]{:S(2)}, u32[]{:S(2)}) %collective-permute-start.15) | collective-permute-done | bytes 32800 | tf_op jit(solution)/shard_map/owned2/ppermute | solution.py:436
  39.2 2.1 %collective-permute-done.16.refs_3_ = f32[64,128]{1,0:T(8,128)S(1)} collective-permute-done((f32[64,128]{1,0:T(8,128)S(1)}, f32[64,128]{1,0:T(8,128)S(1)}, u32[]{:S(2)}, u32[]{:S(2)}) %collective-permute-start.16) | collective-permute-done | bytes 32800 | tf_op jit(solution)/shard_map/owned3/ppermute | solution.py:436
  41.4 1.6 %place_rows.1 = f32[1968,128]{1,0:T(8,128)} custom-call(s32[4,32]{1,0:T(4,128)S(1)} %copy-done.4, f32[64,128]{1,0:T(8,128)S(1)} %get-tuple-element.21.refs_0_, f32[64,128]{1,0:T(8,128)S(1)} %collective-permute-done.14.refs_1_, f32[64,128]{1,0:T(8,128)S(1)} %collective-permute-done.15.refs_2_, f32[64,128]{1,0:T(8,128)S(1)} %collective-permute-done.16.refs_3_), custom_call_target="tpu_custom_call" | custom-call | flops 1000000 | bytes 2000000 | tf_op jit(solution)/shard_map/place_rows/pallas_call | solution.py:411
  (32 shorter events, 4.0 us)
Async XLA Ops:
  0.6 22.3 %copy-start.2 = (bf16[128,128]{1,0:T(8,128)(2,1)S(1)}, bf16[128,128]{1,0:T(8,128)(2,1)}, u32[]{:S(2)}) copy-start(bf16[128,128]{1,0:T(8,128)(2,1)} %bottom_ref.5) | copy-start | bytes 98308
  0.6 22.3 %copy-start.1 = (bf16[128,1024]{1,0:T(8,128)(2,1)S(1)}, bf16[128,1024]{1,0:T(8,128)(2,1)}, u32[]{:S(2)}) copy-start(bf16[128,1024]{1,0:T(8,128)(2,1)} %dense_ref.3) | copy-start | bytes 786436
  0.7 23.7 %copy-start = (f32[128,1024]{1,0:T(8,128)S(1)}, f32[128,1024]{1,0:T(8,128)}, u32[]{:S(2)}) copy-start(f32[128,1024]{1,0:T(8,128)} %cot_ref.1) | copy-start | bytes 1572868
  0.7 23.7 %copy-start.3 = (f32[1,1024]{1,0:T(1,128)S(1)}, f32[1,1024]{1,0:T(1,128)}, u32[]{:S(2)}) copy-start(f32[1,1024]{1,0:T(1,128)} %pairs_ref.1) | copy-start | bytes 12292
  0.7 40.7 %copy-start.4 = (s32[4,32]{1,0:T(4,128)S(1)}, s32[4,32]{1,0:T(4,128)}, u32[]{:S(2)}) copy-start(s32[4,32]{1,0:T(4,128)} %starts_ref.3) | copy-start | bytes 1540
  2.5 6.6 %collective-permute-start = (f32[256,128]{1,0:T(8,128)S(1)}, f32[256,128]{1,0:T(8,128)S(1)}, u32[]{:S(2)}, u32[]{:S(2)}) collective-permute-start(f32[256,128]{1,0:T(8,128)S(1)} %get-tuple-element.15.own_ref), channel_id=1, source_target_pairs={{0,1},{1,0},{2,3},{3,2},{4,5},{5,4},{6,7},{7,6},{8,9},{9,8},{10,11... | collective-permute-start | bytes 393224 | tf_op jit(solution)/shard_map/hot/ppermute | solution.py:436
  3.1 6.0 %collective-permute-start.1 = (f32[8,128]{1,0:T(8,128)S(1)}, f32[8,128]{1,0:T(8,128)S(1)}, u32[]{:S(2)}, u32[]{:S(2)}) collective-permute-start(f32[8,128]{1,0:T(8,128)S(1)} %get-tuple-element.14.places_ref.refs_4_), channel_id=1, source_target_pairs={{0,7},{1,6},{2,5},{3,4},{4,3},{5,2},{6,1},{7,0},{8,15},{9,14},{10,... | collective-permute-start | bytes 12296 | tf_op jit(solution)/shard_map/place7/ppermute | solution.py:436
  9.6 13.0 %collective-permute-start.2 = (f32[128,128]{1,0:T(8,128)S(1)}, f32[128,128]{1,0:T(8,128)S(1)}, u32[]{:S(2)}, u32[]{:S(2)}) collective-permute-start(f32[128,128]{1,0:T(8,128)S(1)} %pool_rows.5), channel_id=1, source_target_pairs={{0,7},{1,6},{2,5},{3,4},{4,3},{5,2},{6,1},{7,0},{8,15},{9,14},{10,... | collective-permute-start | bytes 196616 | tf_op jit(solution)/shard_map/part7/ppermute | solution.py:436
  13.2 3.9 %collective-permute-start.3 = (f32[8,128]{1,0:T(8,128)S(1)}, f32[8,128]{1,0:T(8,128)S(1)}, u32[]{:S(2)}, u32[]{:S(2)}) collective-permute-start(f32[8,128]{1,0:T(8,128)S(1)} %get-tuple-element.14.places_ref.refs_4_), channel_id=1, source_target_pairs={{0,5},{1,4},{2,7},{3,6},{4,1},{5,0},{6,3},{7,2},{8,13},{9,12},{10,... | collective-permute-start | bytes 12296 | tf_op jit(solution)/shard_map/place5/ppermute | solution.py:436
  13.2 5.4 %collective-permute-start.5 = (f32[8,128]{1,0:T(8,128)S(1)}, f32[8,128]{1,0:T(8,128)S(1)}, u32[]{:S(2)}, u32[]{:S(2)}) collective-permute-start(f32[8,128]{1,0:T(8,128)S(1)} %get-tuple-element.14.places_ref.refs_4_), channel_id=1, source_target_pairs={{0,3},{1,2},{2,1},{3,0},{4,7},{5,6},{6,5},{7,4},{8,11},{9,10},{10,... | collective-permute-start | bytes 12296 | tf_op jit(solution)/shard_map/place3/ppermute | solution.py:436
  17.6 6.0 %collective-permute-start.4 = (f32[128,128]{1,0:T(8,128)S(1)}, f32[128,128]{1,0:T(8,128)S(1)}, u32[]{:S(2)}, u32[]{:S(2)}) collective-permute-start(f32[128,128]{1,0:T(8,128)S(1)} %pool_rows.6), channel_id=1, source_target_pairs={{0,5},{1,4},{2,7},{3,6},{4,1},{5,0},{6,3},{7,2},{8,13},{9,12},{10,... | collective-permute-start | bytes 196616 | tf_op jit(solution)/shard_map/part5/ppermute | solution.py:436
  19.0 5.3 %collective-permute-start.6 = (f32[128,128]{1,0:T(8,128)S(1)}, f32[128,128]{1,0:T(8,128)S(1)}, u32[]{:S(2)}, u32[]{:S(2)}) collective-permute-start(f32[128,128]{1,0:T(8,128)S(1)} %pool_rows.7), channel_id=1, source_target_pairs={{0,3},{1,2},{2,1},{3,0},{4,7},{5,6},{6,5},{7,4},{8,11},{9,10},{10,... | collective-permute-start | bytes 196616 | tf_op jit(solution)/shard_map/part3/ppermute | solution.py:436
  19.1 8.5 %collective-permute-start.12 = (f32[128,128]{1,0:T(8,128)S(1)}, f32[128,128]{1,0:T(8,128)S(1)}, u32[]{:S(2)}, u32[]{:S(2)}) collective-permute-start(f32[128,128]{1,0:T(8,128)S(1)} %get-tuple-element.20.refs_8_), channel_id=1, source_target_pairs={{0,3},{1,2},{2,1},{3,0},{4,7},{5,6},{6,5},{7,4},{8,11},{9,10},{10,... | collective-permute-start | bytes 196616 | tf_op jit(solution)/shard_map/wide3/ppermute | solution.py:436
  20.8 7.8 %collective-permute-start.11 = (f32[128,128]{1,0:T(8,128)S(1)}, f32[128,128]{1,0:T(8,128)S(1)}, u32[]{:S(2)}, u32[]{:S(2)}) collective-permute-start(f32[128,128]{1,0:T(8,128)S(1)} %get-tuple-element.20.refs_8_), channel_id=1, source_target_pairs={{0,5},{1,4},{2,7},{3,6},{4,1},{5,0},{6,3},{7,2},{8,13},{9,12},{10,... | collective-permute-start | bytes 196616 | tf_op jit(solution)/shard_map/wide5/ppermute | solution.py:436
  22.6 6.3 %collective-permute-start.10 = (f32[128,128]{1,0:T(8,128)S(1)}, f32[128,128]{1,0:T(8,128)S(1)}, u32[]{:S(2)}, u32[]{:S(2)}) collective-permute-start(f32[128,128]{1,0:T(8,128)S(1)} %get-tuple-element.20.refs_8_), channel_id=1, source_target_pairs={{0,7},{1,6},{2,5},{3,4},{4,3},{5,2},{6,1},{7,0},{8,15},{9,14},{10,... | collective-permute-start | bytes 196616 | tf_op jit(solution)/shard_map/wide7/ppermute | solution.py:436
  24.8 4.1 %collective-permute-start.9 = (f32[1,128]{1,0:T(1,128)S(1)}, f32[1,128]{1,0:T(1,128)S(1)}, u32[]{:S(2)}, u32[]{:S(2)}) collective-permute-start(f32[1,128]{1,0:T(1,128)S(1)} %get-tuple-element.19.refs_0_), channel_id=1, source_target_pairs={{0,3},{1,2},{2,1},{3,0},{4,7},{5,6},{6,5},{7,4},{8,11},{9,10},{10,... | collective-permute-start | bytes 1544 | tf_op jit(solution)/shard_map/score3/ppermute | solution.py:436
  24.9 5.2 %collective-permute-start.8 = (f32[1,128]{1,0:T(1,128)S(1)}, f32[1,128]{1,0:T(1,128)S(1)}, u32[]{:S(2)}, u32[]{:S(2)}) collective-permute-start(f32[1,128]{1,0:T(1,128)S(1)} %get-tuple-element.19.refs_0_), channel_id=1, source_target_pairs={{0,5},{1,4},{2,7},{3,6},{4,1},{5,0},{6,3},{7,2},{8,13},{9,12},{10,... | collective-permute-start | bytes 1544 | tf_op jit(solution)/shard_map/score5/ppermute | solution.py:436
  27.6 4.8 %collective-permute-start.7 = (f32[1,128]{1,0:T(1,128)S(1)}, f32[1,128]{1,0:T(1,128)S(1)}, u32[]{:S(2)}, u32[]{:S(2)}) collective-permute-start(f32[1,128]{1,0:T(1,128)S(1)} %get-tuple-element.19.refs_0_), channel_id=1, source_target_pairs={{0,7},{1,6},{2,5},{3,4},{4,3},{5,2},{6,1},{7,0},{8,15},{9,14},{10,... | collective-permute-start | bytes 1544 | tf_op jit(solution)/shard_map/score7/ppermute | solution.py:436
  32.9 1.5 %collective-permute-start.13 = (f32[256,128]{1,0:T(8,128)S(1)}, f32[256,128]{1,0:T(8,128)S(1)}, u32[]{:S(2)}, u32[]{:S(2)}) collective-permute-start(f32[256,128]{1,0:T(8,128)S(1)} %row_grads_given.1), channel_id=1, source_target_pairs={{0,1},{1,0},{2,3},{3,2},{4,5},{5,4},{6,7},{7,6},{8,9},{9,8},{10,11... | collective-permute-start | bytes 393224 | tf_op jit(solution)/shard_map/rows/ppermute | solution.py:436
  34.4 4.4 %collective-permute-start.14 = (f32[64,128]{1,0:T(8,128)S(1)}, f32[64,128]{1,0:T(8,128)S(1)}, u32[]{:S(2)}, u32[]{:S(2)}) collective-permute-start(f32[64,128]{1,0:T(8,128)S(1)} %get-tuple-element.22), channel_id=1, source_target_pairs={{0,9},{1,8},{2,11},{3,10},{4,13},{5,12},{6,15},{7,14},{8,1},{9,0},... | collective-permute-start | bytes 98312 | tf_op jit(solution)/shard_map/owned1/ppermute | solution.py:436
  35.9 3.4 %collective-permute-start.15 = (f32[64,128]{1,0:T(8,128)S(1)}, f32[64,128]{1,0:T(8,128)S(1)}, u32[]{:S(2)}, u32[]{:S(2)}) collective-permute-start(f32[64,128]{1,0:T(8,128)S(1)} %get-tuple-element.23), channel_id=1, source_target_pairs={{0,17},{1,16},{2,19},{3,18},{4,21},{5,20},{6,23},{7,22},{8,25},{9,... | collective-permute-start | bytes 98312 | tf_op jit(solution)/shard_map/owned2/ppermute | solution.py:436
  37.1 4.2 %collective-permute-start.16 = (f32[64,128]{1,0:T(8,128)S(1)}, f32[64,128]{1,0:T(8,128)S(1)}, u32[]{:S(2)}, u32[]{:S(2)}) collective-permute-start(f32[64,128]{1,0:T(8,128)S(1)} %get-tuple-element.24), channel_id=1, source_target_pairs={{0,25},{1,24},{2,27},{3,26},{4,29},{5,28},{6,31},{7,30},{8,17},{9,... | collective-permute-start | bytes 98312 | tf_op jit(solution)/shard_map/owned3/ppermute | solution.py:436

commit v5 on v4

--- a/solution.py
+++ b/solution.py
@@ -6,6 +6,7 @@
 from jax.experimental import pallas as pl
 from jax.experimental.pallas import tpu as pltpu
 from jax.sharding import PartitionSpec as P
+
 
 HOT = 64
 GRANT = 8 * 1024 * 1024
@@ -100,7 +101,7 @@
     pre_grad = cotangent * sigmoid_pre * (1.0 + preact * (1.0 - sigmoid_pre))
     pair_grad = jnp.dot(pre_grad, top_pairs.T, precision=lax.Precision.HIGHEST)
     vec_grads = [jnp.zeros_like(vector) for vector in vectors]
-    for place, (former, latter) in enumerate(couples):
+    for former, latter in couples:
         vec_grads[former] = pair_grad * vectors[latter]
         vec_grads[latter] = pair_grad * vectors[former]
     pre_half = pre_grad.astype(jnp.bfloat16)
@@ -167,7 +168,7 @@
     bag = looked.shape[0]
     head = min(HOT + 8, win_size)
 
-    def kernel(starts_ref, looked_ref, bottom_ref, table_ref, hot_ref, places_ref, wide_ref, held, sems):
+    def kernel(starts_ref, looked_ref, bottom_ref, table_ref, hot_ref, places_ref, near_ref, wide_ref, held, sems):
         grp_pos = lax.axis_index("grp")
         shard_pos = lax.axis_index("shard")
         shifts = []
@@ -191,10 +192,12 @@
         found = looked_ref[...]
         window_of = jnp.floor((found.astype(jnp.float32) + 0.5) * (1.0 / win_size)).astype(jnp.int32)
         places = (found - window_of * (win_size - HOT)).astype(jnp.float32)
-        places_ref[...] = jnp.concatenate(
-            [places, jnp.zeros((8 - bag, samples), jnp.float32)], axis=0
-        )
-        wide_ref[...] = bottom_ref[...].astype(jnp.float32)
+        places = jnp.concatenate([places, jnp.zeros((8 - bag, samples), jnp.float32)], axis=0)
+        places_ref[...] = places
+        near_ref[pl.ds(0, 8), :] = places
+        wide = bottom_ref[...].astype(jnp.float32)
+        near_ref[pl.ds(8, samples), :] = wide
+        wide_ref[...] = wide
         for copy in copies:
             copy.wait()
         for window in range(group_count):
@@ -205,10 +208,11 @@
         out_shape=(
             jax.ShapeDtypeStruct((group_count * HOT, width), jnp.float32),
             jax.ShapeDtypeStruct((8, samples), jnp.float32),
+            jax.ShapeDtypeStruct((samples + 8, width), jnp.float32),
             jax.ShapeDtypeStruct((samples, width), jnp.float32),
         ),
         in_specs=[whole(pltpu.SMEM), whole(), whole(), whole(pl.ANY)],
-        out_specs=(whole(), whole(), whole()),
+        out_specs=(whole(), whole(), whole(), whole()),
         scratch_shapes=[
             pltpu.VMEM((group_count, head + HOT, width), jnp.float32),
             pltpu.SemaphoreType.DMA((group_count, 2)),
@@ -242,7 +246,7 @@
         shard_pos = lax.axis_index("shard")
         rows = lax.broadcasted_iota(jnp.int32, (samples, block_rows), 1).astype(jnp.float32)
         columns = jnp.concatenate(
-            [places_ref[...], jnp.zeros((samples - 8, samples), jnp.float32)], axis=0
+            [places_ref[pl.ds(0, 8), :], jnp.zeros((samples - 8, samples), jnp.float32)], axis=0
         ).T
         total = jnp.zeros((samples, width), jnp.float32)
         for side, ref in enumerate((own_ref, other_ref)):
@@ -335,7 +339,8 @@
 
 
 def row_grads(scores, places, wides, bag, group_count, kept):
-    samples, width = wides[0].shape
+    samples = scores[0].shape[1]
+    width = wides[0].shape[1]
     count = len(scores)
 
     def kernel(*refs):
@@ -354,7 +359,7 @@
             for slot in range(bag):
                 times += jnp.where(place_ref[pl.ds(slot, 1), :] == rows, 1.0, 0.0)
             high, low = two_terms(times * score_ref[...])
-            bottom = wide_ref[...].astype(jnp.bfloat16)
+            bottom = wide_ref[pl.ds(wide_ref.shape[0] - samples, samples), :].astype(jnp.bfloat16)
             total += jnp.dot(high, bottom, preferred_element_type=jnp.float32)
             total += jnp.dot(low, bottom, preferred_element_type=jnp.float32)
         refs[-1][...] = total
@@ -426,38 +431,42 @@
     bag = lookups.shape[2]
     win_size = tables.shape[1] // group_count
 
-    def across(label, values, grp_step, shard_step):
+    def across(values, grp_step, shard_step):
         pairs = [
             (grp * shard_count + shard, (grp ^ grp_step) * shard_count + (shard ^ shard_step))
             for grp in range(group_count)
             for shard in range(shard_count)
         ]
-        with jax.named_scope(label):
-            return lax.ppermute(values, ("grp", "shard"), pairs)
-
-    steps = list(range(shard_count - 1, 1, -2))
+        return lax.ppermute(values, ("grp", "shard"), pairs)
+
+    near = 3
+    steps = list(range(shard_count - 1, near, -2))
     looked = lookups[:, 0, :].T
-    hot_own, places_own, wide_own = load_first(starts, looked, bottom_out, tables[0], group_count)
-    hot_other = across("hot", hot_own, 0, 1)
-    places = [places_own] + [across(f"place{step}", places_own, 0, step) for step in steps]
+    hot_own, places_own, near_own, wide_own = load_first(
+        starts, looked, bottom_out, tables[0], group_count
+    )
+    hot_other = across(hot_own, 0, 1)
+    places = [across(places_own, 0, step) for step in steps]
+    near_back = across(near_own, 0, near)
     linear = linear_part(bottom_out, top_dense)
-    sums = [pool_rows(block, hot_own, hot_other, bag) for block in places]
-    parts = [sums[0]] + [
-        across(f"part{step}", part, 0, step) for part, step in zip(sums[1:], steps)
-    ]
-    wides = [wide_own] + [across(f"wide{step}", wide_own, 0, step) for step in steps]
+    own_sums = pool_rows(places_own, hot_own, hot_other, bag)
+    parts = [own_sums]
+    for step, block in zip(steps + [near], places + [near_back]):
+        part = pool_rows(block, hot_own, hot_other, bag)
+        parts.append(across(part, 0, step))
+    wides = [across(wide_own, 0, step) for step in steps]
     score_row, pooled = score(parts, bottom_out, linear, top_pairs, cotangent)
-    scores = [score_row] + [across(f"score{step}", score_row, 0, step) for step in steps]
+    scores = [score_row] + [across(score_row, 0, step) for step in steps + [near]]
     activation, bottom_grad = finish_dense(
         pooled, bottom_out, linear, top_pairs, cotangent, top_dense
     )
+    places = [places_own] + places + [near_back]
+    wides = [near_own] + wides + [near_back]
     given = row_grads(scores, places, wides, bag, group_count, False)
-    received = across("rows", given, 0, 1)
+    received = across(given, 0, 1)
     kept = row_grads(scores, places, wides, bag, group_count, True)
     owned = split_owners(kept, received, group_count)
-    blocks = [owned[0]] + [
-        across(f"owned{step}", owned[step], step, 1) for step in range(1, group_count)
-    ]
+    blocks = [owned[0]] + [across(owned[step], step, 1) for step in range(1, group_count)]
     table_grad = place_rows(starts, blocks, win_size)
     return activation, bottom_grad, table_grad[None, None]
 
@@ -479,7 +488,7 @@
         and is_power(shard_count)
         and tables.shape[1] // group_count % 8 == 0
         and hot_rows <= group_lookups
-        and shard_count % 2 == 0
+        and shard_count >= 8
     )
     plan = by_hot_rows if fits else by_row_sums
     return plan(bottom_out, lookups, starts, tables, top_dense, top_pairs, cotangent)

time: 43.2 us -> 39 us (0.903)
  waiting for transfers between devices: 12.6 us -> 9.73 us
  starting transfers between devices: 21.6 us -> 20.3 us
    ppermute x17 -> x16, waiting for transfers between devices: 12.6 us -> 9.73 us  [across(): return lax.ppermute(values, ('grp', 'shard'), pairs)]
    ppermute x17 -> x16, starting transfers between devices: 21.6 us -> 20.3 us  [across(): return lax.ppermute(values, ('grp', 'shard'), pairs)]
  transfers between devices with their start and end apart: 17 -> 16, of which waited for: 9 -> 6; matrix products, arithmetic and copies ran while one was open for 0% -> 0% of each run, Pallas kernels for 9% -> 11%
where the time goes in v5:
time: 39 us; the launch traced here: 38.8 us
  starting transfers between devices  20.3 us (52%)
  waiting for transfers between devices  9.73 us (25%)
  Pallas kernels  8.03 us (21%)
  between operations  0.76 us (2%)
    ppermute x16, starting transfers between devices, across(): return lax.ppermute(values, ('grp', 'shard'), pairs)  20.3 us
    ppermute x16, waiting for transfers between devices, across(): return lax.ppermute(values, ('grp', 'shard'), pairs)  9.73 us
    pallas_call x4, Pallas kernels, pool_rows(): pl.pallas_call(kernel, out_shape=jax.ShapeDtypeStruct((samples, width), j...  1.94 us
    pallas_call x1, Pallas kernels, load_first(): pl.pallas_call(kernel, out_shape=(jax.ShapeDtypeStruct((group_count * HOT...  1.84 us
    pallas_call x1, Pallas kernels, place_rows(): pl.pallas_call(kernel, out_shape=jax.ShapeDtypeStruct((win_size, width),...  1.62 us
    pallas_call x1, Pallas kernels, finish_dense(): pl.pallas_call(kernel, out_shape=(jax.ShapeDtypeStruct((samples, hidden),...  1.14 us
    pallas_call x2, Pallas kernels, row_grads(): pl.pallas_call(kernel, out_shape=jax.ShapeDtypeStruct((group_count * HOT,...  0.85 us
  transfers between devices with their start and end apart: 16, of which 6 were waited for; matrix products, arithmetic and copies ran while one was open for 0% of the time, Pallas kernels for 11%

profile of v5, /device:TPU:0, one launch (start us, length us, event | category | flops | bytes accessed | tf_op | source)
XLA Modules:
  0.0 38.8 jit_solution(10774105707492972799)
XLA Ops:
  0.7 1.8 %load_first.1 = (f32[256,128]{1,0:T(8,128)S(1)}, f32[8,128]{1,0:T(8,128)S(1)}, f32[136,128]{1,0:T(8,128)S(1)}, f32[128,128]{1,0:T(8,128)S(1)}) custom-call(s32[4,32]{1,0:T(4,128)} %starts_ref.3, s32[4,128]{1,0:T(4,128)} %bitcast.7, bf16[128,128]{1,0:T(8,128)(2,1)} %bottom_ref.5, f32[7872,128]{1,0:T(8,128)} %bitcast.5), custom_call_target="tpu_custom_call" | custom-call | flops 1000000 | bytes 1000000 | tf_op jit(solution)/shard_map/load_first/pallas_call | solution.py:206
  2.5 0.6 %collective-permute-start = (f32[256,128]{1,0:T(8,128)S(1)}, f32[256,128]{1,0:T(8,128)S(1)}, u32[]{:S(2)}, u32[]{:S(2)}) collective-permute-start(f32[256,128]{1,0:T(8,128)S(1)} %get-tuple-element.16.own_ref), channel_id=1, source_target_pairs={{0,1},{1,0},{2,3},{3,2},{4,5},{5,4},{6,7},{7,6},{8,9},{9,8},{10,11... | collective-permute-start | bytes 393224 | tf_op jit(solution)/shard_map/ppermute | solution.py:440
  3.1 2.7 %collective-permute-start.5 = (f32[136,128]{1,0:T(8,128)S(1)}, f32[136,128]{1,0:T(8,128)S(1)}, u32[]{:S(2)}, u32[]{:S(2)}) collective-permute-start(f32[136,128]{1,0:T(8,128)S(1)} %get-tuple-element.17.refs_8_), channel_id=1, source_target_pairs={{0,3},{1,2},{2,1},{3,0},{4,7},{5,6},{6,5},{7,4},{8,11},{9,10},{10,... | collective-permute-start | bytes 208904 | tf_op jit(solution)/shard_map/ppermute | solution.py:440
  5.8 2.2 %collective-permute-start.1 = (f32[8,128]{1,0:T(8,128)S(1)}, f32[8,128]{1,0:T(8,128)S(1)}, u32[]{:S(2)}, u32[]{:S(2)}) collective-permute-start(f32[8,128]{1,0:T(8,128)S(1)} %get-tuple-element.15.places_ref.refs_4_), channel_id=1, source_target_pairs={{0,7},{1,6},{2,5},{3,4},{4,3},{5,2},{6,1},{7,0},{8,15},{9,14},{10,... | collective-permute-start | bytes 12296 | tf_op jit(solution)/shard_map/ppermute | solution.py:440
  8.0 2.6 %collective-permute-done.1.places_ref.refs_5_ = f32[8,128]{1,0:T(8,128)S(1)} collective-permute-done((f32[8,128]{1,0:T(8,128)S(1)}, f32[8,128]{1,0:T(8,128)S(1)}, u32[]{:S(2)}, u32[]{:S(2)}) %collective-permute-start.1) | collective-permute-done | bytes 4128 | tf_op jit(solution)/shard_map/ppermute | solution.py:440
  10.6 0.5 %pool_rows.5 = f32[128,128]{1,0:T(8,128)S(1)} custom-call(f32[8,128]{1,0:T(8,128)S(1)} %collective-permute-done.1.places_ref.refs_5_, f32[256,128]{1,0:T(8,128)S(1)} %get-tuple-element.16.own_ref, f32[256,128]{1,0:T(8,128)S(1)} %collective-permute-done.other_ref), custom_call_target="tpu_custom_call" | custom-call | flops 50000000 | bytes 1000000 | tf_op jit(solution)/shard_map/pool_rows/pallas_call | solution.py:260
  11.1 2.2 %collective-permute-start.2 = (f32[128,128]{1,0:T(8,128)S(1)}, f32[128,128]{1,0:T(8,128)S(1)}, u32[]{:S(2)}, u32[]{:S(2)}) collective-permute-start(f32[128,128]{1,0:T(8,128)S(1)} %pool_rows.5), channel_id=1, source_target_pairs={{0,7},{1,6},{2,5},{3,4},{4,3},{5,2},{6,1},{7,0},{8,15},{9,14},{10,... | collective-permute-start | bytes 196616 | tf_op jit(solution)/shard_map/ppermute | solution.py:440
  13.4 0.5 %pool_rows.6 = f32[128,128]{1,0:T(8,128)S(1)} custom-call(f32[8,128]{1,0:T(8,128)S(1)} %collective-permute-done.3.places_ref.refs_6_, f32[256,128]{1,0:T(8,128)S(1)} %get-tuple-element.16.own_ref, f32[256,128]{1,0:T(8,128)S(1)} %collective-permute-done.other_ref), custom_call_target="tpu_custom_call" | custom-call | flops 50000000 | bytes 1000000 | tf_op jit(solution)/shard_map/pool_rows/pallas_call | solution.py:260
  13.9 0.5 %pool_rows.7 = f32[128,128]{1,0:T(8,128)S(1)} custom-call(f32[136,128]{1,0:T(8,128)S(1)} %collective-permute-done.5.places_ref.refs_7_.refs_11_, f32[256,128]{1,0:T(8,128)S(1)} %get-tuple-element.16.own_ref, f32[256,128]{1,0:T(8,128)S(1)} %collective-permute-done.other_ref), custom_call_target="tpu_custom_call" | custom-call | flops 50000000 | bytes 1000000 | tf_op jit(solution)/shard_map/pool_rows/pallas_call | solution.py:260
  14.4 1.7 %collective-permute-start.6 = (f32[128,128]{1,0:T(8,128)S(1)}, f32[128,128]{1,0:T(8,128)S(1)}, u32[]{:S(2)}, u32[]{:S(2)}) collective-permute-start(f32[128,128]{1,0:T(8,128)S(1)} %pool_rows.7), channel_id=1, source_target_pairs={{0,3},{1,2},{2,1},{3,0},{4,7},{5,6},{6,5},{7,4},{8,11},{9,10},{10,... | collective-permute-start | bytes 196616 | tf_op jit(solution)/shard_map/ppermute | solution.py:440
  16.1 1.0 %collective-permute-start.11 = (f32[128,128]{1,0:T(8,128)S(1)}, f32[128,128]{1,0:T(8,128)S(1)}, u32[]{:S(2)}, u32[]{:S(2)}) collective-permute-start(f32[128,128]{1,0:T(8,128)S(1)} %get-tuple-element.22), channel_id=1, source_target_pairs={{0,5},{1,4},{2,7},{3,6},{4,1},{5,0},{6,3},{7,2},{8,13},{9,12},{10,... | collective-permute-start | bytes 196616 | tf_op jit(solution)/shard_map/ppermute | solution.py:440
  17.2 1.4 %collective-permute-start.10 = (f32[128,128]{1,0:T(8,128)S(1)}, f32[128,128]{1,0:T(8,128)S(1)}, u32[]{:S(2)}, u32[]{:S(2)}) collective-permute-start(f32[128,128]{1,0:T(8,128)S(1)} %get-tuple-element.22), channel_id=1, source_target_pairs={{0,7},{1,6},{2,5},{3,4},{4,3},{5,2},{6,1},{7,0},{8,15},{9,14},{10,... | collective-permute-start | bytes 196616 | tf_op jit(solution)/shard_map/ppermute | solution.py:440
  18.8 0.5 %pool_rows.4.refs_0_ = f32[128,128]{1,0:T(8,128)S(1)} custom-call(f32[8,128]{1,0:T(8,128)S(1)} %get-tuple-element.15.places_ref.refs_4_, f32[256,128]{1,0:T(8,128)S(1)} %get-tuple-element.16.own_ref, f32[256,128]{1,0:T(8,128)S(1)} %collective-permute-done.other_ref), custom_call_target="tpu_custom_call" | custom-call | flops 50000000 | bytes 1000000 | tf_op jit(solution)/shard_map/pool_rows/pallas_call | solution.py:260
  19.3 0.9 %collective-permute-done.4.refs_2_ = f32[128,128]{1,0:T(8,128)S(1)} collective-permute-done((f32[128,128]{1,0:T(8,128)S(1)}, f32[128,128]{1,0:T(8,128)S(1)}, u32[]{:S(2)}, u32[]{:S(2)}) %collective-permute-start.4) | collective-permute-done | bytes 65568 | tf_op jit(solution)/shard_map/ppermute | solution.py:440
  21.0 2.6 %collective-permute-start.8 = (f32[1,128]{1,0:T(1,128)S(1)}, f32[1,128]{1,0:T(1,128)S(1)}, u32[]{:S(2)}, u32[]{:S(2)}) collective-permute-start(f32[1,128]{1,0:T(1,128)S(1)} %get-tuple-element.21.refs_0_), channel_id=1, source_target_pairs={{0,5},{1,4},{2,7},{3,6},{4,1},{5,0},{6,3},{7,2},{8,13},{9,12},{10,... | collective-permute-start | bytes 1544 | tf_op jit(solution)/shard_map/ppermute | solution.py:440
  23.5 1.9 %collective-permute-start.7 = (f32[1,128]{1,0:T(1,128)S(1)}, f32[1,128]{1,0:T(1,128)S(1)}, u32[]{:S(2)}, u32[]{:S(2)}) collective-permute-start(f32[1,128]{1,0:T(1,128)S(1)} %get-tuple-element.21.refs_0_), channel_id=1, source_target_pairs={{0,7},{1,6},{2,5},{3,4},{4,3},{5,2},{6,1},{7,0},{8,15},{9,14},{10,... | collective-permute-start | bytes 1544 | tf_op jit(solution)/shard_map/ppermute | solution.py:440
  25.5 2.8 %collective-permute-done.7.refs_1_ = f32[1,128]{1,0:T(1,128)S(1)} collective-permute-done((f32[1,128]{1,0:T(1,128)S(1)}, f32[1,128]{1,0:T(1,128)S(1)}, u32[]{:S(2)}, u32[]{:S(2)}) %collective-permute-start.7) | collective-permute-done | bytes 544 | tf_op jit(solution)/shard_map/ppermute | solution.py:440
  29.5 0.6 %collective-permute-done.12.received_ref = f32[256,128]{1,0:T(8,128)S(1)} collective-permute-done((f32[256,128]{1,0:T(8,128)S(1)}, f32[256,128]{1,0:T(8,128)S(1)}, u32[]{:S(2)}, u32[]{:S(2)}) %collective-permute-start.12) | collective-permute-done | bytes 131104 | tf_op jit(solution)/shard_map/ppermute | solution.py:440
  30.2 1.4 %collective-permute-start.13 = (f32[64,128]{1,0:T(8,128)S(1)}, f32[64,128]{1,0:T(8,128)S(1)}, u32[]{:S(2)}, u32[]{:S(2)}) collective-permute-start(f32[64,128]{1,0:T(8,128)S(1)} %get-tuple-element.24), channel_id=1, source_target_pairs={{0,9},{1,8},{2,11},{3,10},{4,13},{5,12},{6,15},{7,14},{8,1},{9,0},... | collective-permute-start | bytes 98312 | tf_op jit(solution)/shard_map/ppermute | solution.py:440
  31.6 1.3 %collective-permute-start.14 = (f32[64,128]{1,0:T(8,128)S(1)}, f32[64,128]{1,0:T(8,128)S(1)}, u32[]{:S(2)}, u32[]{:S(2)}) collective-permute-start(f32[64,128]{1,0:T(8,128)S(1)} %get-tuple-element.25), channel_id=1, source_target_pairs={{0,17},{1,16},{2,19},{3,18},{4,21},{5,20},{6,23},{7,22},{8,25},{9,... | collective-permute-start | bytes 98312 | tf_op jit(solution)/shard_map/ppermute | solution.py:440
  33.4 1.1 %finish_dense.1 = (bf16[128,1024]{1,0:T(8,128)(2,1)}, f32[128,128]{1,0:T(8,128)}) custom-call(f32[128,128]{1,0:T(8,128)S(1)} %get-tuple-element.18.pooled_ref, bf16[128,128]{1,0:T(8,128)(2,1)S(1)} %copy-done.2, f32[128,1024]{1,0:T(8,128)S(1)} %linear_part.1.refs_5_.linear_ref, f32[1,1024]{1,0:T(1,128)S(1)} %copy-done.3, f32[128,1024]{1,0:T(8,128)S(1)} %copy-done, ...), custom_call_target="tpu_custom_call" | custom-call | flops 50000000 | bytes 1000000 | tf_op jit(solution)/shard_map/finish_dense/pallas_call | solution.py:327
  34.5 0.5 %collective-permute-done.14.refs_2_ = f32[64,128]{1,0:T(8,128)S(1)} collective-permute-done((f32[64,128]{1,0:T(8,128)S(1)}, f32[64,128]{1,0:T(8,128)S(1)}, u32[]{:S(2)}, u32[]{:S(2)}) %collective-permute-start.14) | collective-permute-done | bytes 32800 | tf_op jit(solution)/shard_map/ppermute | solution.py:440
  35.0 2.2 %collective-permute-done.15.refs_3_ = f32[64,128]{1,0:T(8,128)S(1)} collective-permute-done((f32[64,128]{1,0:T(8,128)S(1)}, f32[64,128]{1,0:T(8,128)S(1)}, u32[]{:S(2)}, u32[]{:S(2)}) %collective-permute-start.15) | collective-permute-done | bytes 32800 | tf_op jit(solution)/shard_map/ppermute | solution.py:440
  37.2 1.6 %place_rows.1 = f32[1968,128]{1,0:T(8,128)} custom-call(s32[4,32]{1,0:T(4,128)S(1)} %copy-done.4, f32[64,128]{1,0:T(8,128)S(1)} %get-tuple-element.23.refs_0_, f32[64,128]{1,0:T(8,128)S(1)} %collective-permute-done.13.refs_1_, f32[64,128]{1,0:T(8,128)S(1)} %collective-permute-done.14.refs_2_, f32[64,128]{1,0:T(8,128)S(1)} %collective-permute-done.15.refs_3_), custom_call_target="tpu_custom_call" | custom-call | flops 1000000 | bytes 2000000 | tf_op jit(solution)/shard_map/place_rows/pallas_call | solution.py:416
  (30 shorter events, 2.8 us)
Async XLA Ops:
  0.6 18.0 %copy-start.2 = (bf16[128,128]{1,0:T(8,128)(2,1)S(1)}, bf16[128,128]{1,0:T(8,128)(2,1)}, u32[]{:S(2)}) copy-start(bf16[128,128]{1,0:T(8,128)(2,1)} %bottom_ref.5) | copy-start | bytes 98308
  0.6 18.0 %copy-start.1 = (bf16[128,1024]{1,0:T(8,128)(2,1)S(1)}, bf16[128,1024]{1,0:T(8,128)(2,1)}, u32[]{:S(2)}) copy-start(bf16[128,1024]{1,0:T(8,128)(2,1)} %dense_ref.3) | copy-start | bytes 786436
  0.7 19.6 %copy-start = (f32[128,1024]{1,0:T(8,128)S(1)}, f32[128,1024]{1,0:T(8,128)}, u32[]{:S(2)}) copy-start(f32[128,1024]{1,0:T(8,128)} %cot_ref.1) | copy-start | bytes 1572868
  0.7 19.6 %copy-start.3 = (f32[1,1024]{1,0:T(1,128)S(1)}, f32[1,1024]{1,0:T(1,128)}, u32[]{:S(2)}) copy-start(f32[1,1024]{1,0:T(1,128)} %pairs_ref.1) | copy-start | bytes 12292
  2.5 34.7 %copy-start.4 = (s32[4,32]{1,0:T(4,128)S(1)}, s32[4,32]{1,0:T(4,128)}, u32[]{:S(2)}) copy-start(s32[4,32]{1,0:T(4,128)} %starts_ref.3) | copy-start | bytes 1540
  2.5 8.1 %collective-permute-start = (f32[256,128]{1,0:T(8,128)S(1)}, f32[256,128]{1,0:T(8,128)S(1)}, u32[]{:S(2)}, u32[]{:S(2)}) collective-permute-start(f32[256,128]{1,0:T(8,128)S(1)} %get-tuple-element.16.own_ref), channel_id=1, source_target_pairs={{0,1},{1,0},{2,3},{3,2},{4,5},{5,4},{6,7},{7,6},{8,9},{9,8},{10,11... | collective-permute-start | bytes 393224 | tf_op jit(solution)/shard_map/ppermute | solution.py:440
  3.1 10.8 %collective-permute-start.5 = (f32[136,128]{1,0:T(8,128)S(1)}, f32[136,128]{1,0:T(8,128)S(1)}, u32[]{:S(2)}, u32[]{:S(2)}) collective-permute-start(f32[136,128]{1,0:T(8,128)S(1)} %get-tuple-element.17.refs_8_), channel_id=1, source_target_pairs={{0,3},{1,2},{2,1},{3,0},{4,7},{5,6},{6,5},{7,4},{8,11},{9,10},{10,... | collective-permute-start | bytes 208904 | tf_op jit(solution)/shard_map/ppermute | solution.py:440
  5.8 4.9 %collective-permute-start.1 = (f32[8,128]{1,0:T(8,128)S(1)}, f32[8,128]{1,0:T(8,128)S(1)}, u32[]{:S(2)}, u32[]{:S(2)}) collective-permute-start(f32[8,128]{1,0:T(8,128)S(1)} %get-tuple-element.15.places_ref.refs_4_), channel_id=1, source_target_pairs={{0,7},{1,6},{2,5},{3,4},{4,3},{5,2},{6,1},{7,0},{8,15},{9,14},{10,... | collective-permute-start | bytes 12296 | tf_op jit(solution)/shard_map/ppermute | solution.py:440
  7.9 5.4 %collective-permute-start.3 = (f32[8,128]{1,0:T(8,128)S(1)}, f32[8,128]{1,0:T(8,128)S(1)}, u32[]{:S(2)}, u32[]{:S(2)}) collective-permute-start(f32[8,128]{1,0:T(8,128)S(1)} %get-tuple-element.15.places_ref.refs_4_), channel_id=1, source_target_pairs={{0,5},{1,4},{2,7},{3,6},{4,1},{5,0},{6,3},{7,2},{8,13},{9,12},{10,... | collective-permute-start | bytes 12296 | tf_op jit(solution)/shard_map/ppermute | solution.py:440
  11.1 8.2 %collective-permute-start.2 = (f32[128,128]{1,0:T(8,128)S(1)}, f32[128,128]{1,0:T(8,128)S(1)}, u32[]{:S(2)}, u32[]{:S(2)}) collective-permute-start(f32[128,128]{1,0:T(8,128)S(1)} %pool_rows.5), channel_id=1, source_target_pairs={{0,7},{1,6},{2,5},{3,4},{4,3},{5,2},{6,1},{7,0},{8,15},{9,14},{10,... | collective-permute-start | bytes 196616 | tf_op jit(solution)/shard_map/ppermute | solution.py:440
  13.8 6.4 %collective-permute-start.4 = (f32[128,128]{1,0:T(8,128)S(1)}, f32[128,128]{1,0:T(8,128)S(1)}, u32[]{:S(2)}, u32[]{:S(2)}) collective-permute-start(f32[128,128]{1,0:T(8,128)S(1)} %pool_rows.6), channel_id=1, source_target_pairs={{0,5},{1,4},{2,7},{3,6},{4,1},{5,0},{6,3},{7,2},{8,13},{9,12},{10,... | collective-permute-start | bytes 196616 | tf_op jit(solution)/shard_map/ppermute | solution.py:440
  14.4 5.8 %collective-permute-start.6 = (f32[128,128]{1,0:T(8,128)S(1)}, f32[128,128]{1,0:T(8,128)S(1)}, u32[]{:S(2)}, u32[]{:S(2)}) collective-permute-start(f32[128,128]{1,0:T(8,128)S(1)} %pool_rows.7), channel_id=1, source_target_pairs={{0,3},{1,2},{2,1},{3,0},{4,7},{5,6},{6,5},{7,4},{8,11},{9,10},{10,... | collective-permute-start | bytes 196616 | tf_op jit(solution)/shard_map/ppermute | solution.py:440
  16.1 9.4 %collective-permute-start.11 = (f32[128,128]{1,0:T(8,128)S(1)}, f32[128,128]{1,0:T(8,128)S(1)}, u32[]{:S(2)}, u32[]{:S(2)}) collective-permute-start(f32[128,128]{1,0:T(8,128)S(1)} %get-tuple-element.22), channel_id=1, source_target_pairs={{0,5},{1,4},{2,7},{3,6},{4,1},{5,0},{6,3},{7,2},{8,13},{9,12},{10,... | collective-permute-start | bytes 196616 | tf_op jit(solution)/shard_map/ppermute | solution.py:440
  17.2 8.3 %collective-permute-start.10 = (f32[128,128]{1,0:T(8,128)S(1)}, f32[128,128]{1,0:T(8,128)S(1)}, u32[]{:S(2)}, u32[]{:S(2)}) collective-permute-start(f32[128,128]{1,0:T(8,128)S(1)} %get-tuple-element.22), channel_id=1, source_target_pairs={{0,7},{1,6},{2,5},{3,4},{4,3},{5,2},{6,1},{7,0},{8,15},{9,14},{10,... | collective-permute-start | bytes 196616 | tf_op jit(solution)/shard_map/ppermute | solution.py:440
  20.7 4.8 %collective-permute-start.9 = (f32[1,128]{1,0:T(1,128)S(1)}, f32[1,128]{1,0:T(1,128)S(1)}, u32[]{:S(2)}, u32[]{:S(2)}) collective-permute-start(f32[1,128]{1,0:T(1,128)S(1)} %get-tuple-element.21.refs_0_), channel_id=1, source_target_pairs={{0,3},{1,2},{2,1},{3,0},{4,7},{5,6},{6,5},{7,4},{8,11},{9,10},{10,... | collective-permute-start | bytes 1544 | tf_op jit(solution)/shard_map/ppermute | solution.py:440
  21.0 4.5 %collective-permute-start.8 = (f32[1,128]{1,0:T(1,128)S(1)}, f32[1,128]{1,0:T(1,128)S(1)}, u32[]{:S(2)}, u32[]{:S(2)}) collective-permute-start(f32[1,128]{1,0:T(1,128)S(1)} %get-tuple-element.21.refs_0_), channel_id=1, source_target_pairs={{0,5},{1,4},{2,7},{3,6},{4,1},{5,0},{6,3},{7,2},{8,13},{9,12},{10,... | collective-permute-start | bytes 1544 | tf_op jit(solution)/shard_map/ppermute | solution.py:440
  23.5 4.8 %collective-permute-start.7 = (f32[1,128]{1,0:T(1,128)S(1)}, f32[1,128]{1,0:T(1,128)S(1)}, u32[]{:S(2)}, u32[]{:S(2)}) collective-permute-start(f32[1,128]{1,0:T(1,128)S(1)} %get-tuple-element.21.refs_0_), channel_id=1, source_target_pairs={{0,7},{1,6},{2,5},{3,4},{4,3},{5,2},{6,1},{7,0},{8,15},{9,14},{10,... | collective-permute-start | bytes 1544 | tf_op jit(solution)/shard_map/ppermute | solution.py:440
  28.8 1.4 %collective-permute-start.12 = (f32[256,128]{1,0:T(8,128)S(1)}, f32[256,128]{1,0:T(8,128)S(1)}, u32[]{:S(2)}, u32[]{:S(2)}) collective-permute-start(f32[256,128]{1,0:T(8,128)S(1)} %row_grads_given.1), channel_id=1, source_target_pairs={{0,1},{1,0},{2,3},{3,2},{4,5},{5,4},{6,7},{7,6},{8,9},{9,8},{10,11... | collective-permute-start | bytes 393224 | tf_op jit(solution)/shard_map/ppermute | solution.py:440
  30.2 4.3 %collective-permute-start.13 = (f32[64,128]{1,0:T(8,128)S(1)}, f32[64,128]{1,0:T(8,128)S(1)}, u32[]{:S(2)}, u32[]{:S(2)}) collective-permute-start(f32[64,128]{1,0:T(8,128)S(1)} %get-tuple-element.24), channel_id=1, source_target_pairs={{0,9},{1,8},{2,11},{3,10},{4,13},{5,12},{6,15},{7,14},{8,1},{9,0},... | collective-permute-start | bytes 98312 | tf_op jit(solution)/shard_map/ppermute | solution.py:440
  31.6 3.3 %collective-permute-start.14 = (f32[64,128]{1,0:T(8,128)S(1)}, f32[64,128]{1,0:T(8,128)S(1)}, u32[]{:S(2)}, u32[]{:S(2)}) collective-permute-start(f32[64,128]{1,0:T(8,128)S(1)} %get-tuple-element.25), channel_id=1, source_target_pairs={{0,17},{1,16},{2,19},{3,18},{4,21},{5,20},{6,23},{7,22},{8,25},{9,... | collective-permute-start | bytes 98312 | tf_op jit(solution)/shard_map/ppermute | solution.py:440
  33.0 4.2 %collective-permute-start.15 = (f32[64,128]{1,0:T(8,128)S(1)}, f32[64,128]{1,0:T(8,128)S(1)}, u32[]{:S(2)}, u32[]{:S(2)}) collective-permute-start(f32[64,128]{1,0:T(8,128)S(1)} %get-tuple-element.26), channel_id=1, source_target_pairs={{0,25},{1,24},{2,27},{3,26},{4,29},{5,28},{6,31},{7,30},{8,17},{9,... | collective-permute-start | bytes 98312 | tf_op jit(solution)/shard_map/ppermute | solution.py:440

commit v6 on v5

--- a/solution.py
+++ b/solution.py
@@ -148,13 +148,6 @@
     high = values.astype(jnp.bfloat16)
     low = (values - high.astype(jnp.float32)).astype(jnp.bfloat16)
     return high, low
-
-
-def dot_two(counts, values):
-    high, low = two_terms(values)
-    return jnp.dot(counts, high, preferred_element_type=jnp.float32) + jnp.dot(
-        counts, low, preferred_element_type=jnp.float32
-    )
 
 
 def stay(values):
@@ -238,34 +231,63 @@
     )(bottom_out, top_dense)
 
 
-def pool_rows(places, hot_own, hot_other, bag):
+def hot_terms(hot_own, hot_other):
     block_rows, width = hot_own.shape
+
+    def kernel(own_ref, other_ref, terms_ref):
+        for side, ref in enumerate((own_ref, other_ref)):
+            high, low = two_terms(ref[...])
+            chosen = pl.ds(side * block_rows, block_rows)
+            terms_ref[chosen, pl.ds(0, width)] = high
+            terms_ref[chosen, pl.ds(width, width)] = low
+
+    return pl.pallas_call(
+        kernel,
+        out_shape=jax.ShapeDtypeStruct((2 * block_rows, 2 * width), jnp.bfloat16),
+        in_specs=[whole()] * 2,
+        out_specs=whole(),
+        cost_estimate=cost(1e6, 1e6),
+        compiler_params=pltpu.CompilerParams(vmem_limit_bytes=GRANT),
+        name="hot_terms",
+    )(hot_own, hot_other)
+
+
+def pool_rows(places, terms, bag):
+    block_rows = terms.shape[0] // 2
+    width = terms.shape[1] // 2
     samples = places.shape[1]
 
-    def kernel(places_ref, own_ref, other_ref, part_ref):
+    def kernel(places_ref, terms_ref, part_ref):
         shard_pos = lax.axis_index("shard")
-        rows = lax.broadcasted_iota(jnp.int32, (samples, block_rows), 1).astype(jnp.float32)
         columns = jnp.concatenate(
             [places_ref[pl.ds(0, 8), :], jnp.zeros((samples - 8, samples), jnp.float32)], axis=0
         ).T
-        total = jnp.zeros((samples, width), jnp.float32)
-        for side, ref in enumerate((own_ref, other_ref)):
-            base = (jnp.bitwise_xor(shard_pos, side) * block_rows).astype(jnp.float32)
-            times = jnp.zeros((samples, block_rows), jnp.float32)
-            for slot in range(bag):
-                times += jnp.where(columns[:, slot : slot + 1] - base == rows, 1.0, 0.0)
-            total += dot_two(times.astype(jnp.bfloat16), ref[...])
-        part_ref[...] = total
+        spread = [
+            jnp.broadcast_to(columns[:, slot : slot + 1], (samples, block_rows)) for slot in range(bag)
+        ]
+        both = []
+        for side in range(2):
+            first = jnp.bitwise_xor(shard_pos, side) * block_rows
+            rows = lax.broadcasted_iota(jnp.int32, (samples, block_rows), 1) + first
+            rows = rows.astype(jnp.float32)
+            times = jnp.where(spread[0] == rows, 1.0, 0.0)
+            for column in spread[1:]:
+                times = jnp.where(column == rows, times + 1.0, times)
+            both.append(times.astype(jnp.bfloat16))
+        total = jnp.dot(
+            jnp.concatenate(both, axis=1), terms_ref[...], preferred_element_type=jnp.float32
+        )
+        part_ref[...] = total[:, :width] + total[:, width:]
 
     return pl.pallas_call(
         kernel,
         out_shape=jax.ShapeDtypeStruct((samples, width), jnp.float32),
-        in_specs=[whole()] * 3,
+        in_specs=[whole()] * 2,
         out_specs=whole(),
         cost_estimate=cost(5e7, 1e6),
         compiler_params=pltpu.CompilerParams(vmem_limit_bytes=GRANT),
         name="pool_rows",
-    )(places, hot_own, hot_other)
+    )(places, terms)
 
 
 def head_terms(pooled, bottom_ref, linear_ref, pairs_ref, cot_ref):
@@ -306,11 +328,17 @@
     )(*parts, bottom_out, linear, top_pairs, cotangent)
 
 
-def finish_dense(pooled, bottom_out, linear, top_pairs, cotangent, top_dense):
+def finish_dense(pooled, bottom_out, linear, top_pairs, cotangent, top_dense, win_size):
     samples, width = bottom_out.shape
     hidden = top_dense.shape[1]
 
-    def kernel(pooled_ref, bottom_ref, linear_ref, pairs_ref, cot_ref, dense_ref, act_ref, grad_ref):
+    def kernel(
+        pooled_ref, bottom_ref, linear_ref, pairs_ref, cot_ref, dense_ref, act_ref, grad_ref,
+        blank_ref, zeros, sem,
+    ):
+        zeros[...] = jnp.zeros_like(zeros)
+        copy = pltpu.make_async_copy(zeros, blank_ref, sem)
+        copy.start()
         pooled = pooled_ref[...]
         preact, sig, pre_grad, pair_grad = head_terms(pooled, bottom_ref, linear_ref, pairs_ref, cot_ref)
         act_ref[...] = (preact * sig).astype(jnp.bfloat16)
@@ -323,15 +351,18 @@
             )
             + pair_grad * pooled
         )
+        copy.wait()
 
     return pl.pallas_call(
         kernel,
         out_shape=(
             jax.ShapeDtypeStruct((samples, hidden), jnp.bfloat16),
             jax.ShapeDtypeStruct((samples, width), jnp.float32),
+            jax.ShapeDtypeStruct((win_size, width), jnp.float32),
         ),
         in_specs=[whole()] * 6,
-        out_specs=(whole(), whole()),
+        out_specs=(whole(), whole(), whole(pltpu.HBM)),
+        scratch_shapes=[pltpu.VMEM((win_size, width), jnp.float32), pltpu.SemaphoreType.DMA],
         cost_estimate=cost(5e7, 1e6),
         compiler_params=pltpu.CompilerParams(vmem_limit_bytes=GRANT),
         name="finish_dense",
@@ -395,34 +426,46 @@
     )(kept, received)
 
 
-def place_rows(starts, blocks, win_size):
-    width = blocks[0].shape[1]
+def place_rows(starts, blocks, blank):
+    win_size, width = blank.shape
     count = len(blocks)
+    head = min(HOT + 8, win_size)
 
     def kernel(starts_ref, *refs):
         block_refs = refs[:count]
-        out_ref, held, sem = refs[count:]
+        out_ref, held, sems = refs[count + 1 :]
         grp_pos = lax.axis_index("grp")
         column = lax.axis_index("shard") * count + grp_pos
         held[...] = jnp.zeros_like(held)
+        firsts = [jnp.int32(0)]
         for step, ref in enumerate(block_refs):
             start = starts_ref[jnp.bitwise_xor(grp_pos, step), column]
+            firsts.append(jnp.minimum(start // 8 * 8, win_size - head))
             held[pl.ds(start, HOT), :] += ref[...]
         held[pl.ds(0, HOT), :] += held[pl.ds(win_size, HOT), :]
-        copy = pltpu.make_async_copy(held.at[pl.ds(0, win_size)], out_ref, sem)
-        copy.start()
-        copy.wait()
+        copies = []
+        for place, first in enumerate(firsts):
+            chosen = pl.ds(pl.multiple_of(first, 8), head)
+            copy = pltpu.make_async_copy(held.at[chosen], out_ref.at[chosen], sems.at[place])
+            copy.start()
+            copies.append(copy)
+        for copy in copies:
+            copy.wait()
 
     return pl.pallas_call(
         kernel,
         out_shape=jax.ShapeDtypeStruct((win_size, width), jnp.float32),
-        in_specs=[whole(pltpu.SMEM)] + [whole()] * count,
-        out_specs=whole(pl.ANY),
-        scratch_shapes=[pltpu.VMEM((win_size + HOT, width), jnp.float32), pltpu.SemaphoreType.DMA],
+        in_specs=[whole(pltpu.SMEM)] + [whole()] * count + [whole(pltpu.HBM)],
+        out_specs=whole(pltpu.HBM),
+        input_output_aliases={1 + count: 0},
+        scratch_shapes=[
+            pltpu.VMEM((win_size + HOT, width), jnp.float32),
+            pltpu.SemaphoreType.DMA((count + 1,)),
+        ],
         cost_estimate=cost(1e6, 2e6),
         compiler_params=pltpu.CompilerParams(vmem_limit_bytes=GRANT),
         name="place_rows",
-    )(starts, *blocks)
+    )(starts, *blocks, blank)
 
 
 def by_hot_rows(bottom_out, lookups, starts, tables, top_dense, top_pairs, cotangent):
@@ -448,17 +491,18 @@
     hot_other = across(hot_own, 0, 1)
     places = [across(places_own, 0, step) for step in steps]
     near_back = across(near_own, 0, near)
+    terms = hot_terms(hot_own, hot_other)
     linear = linear_part(bottom_out, top_dense)
-    own_sums = pool_rows(places_own, hot_own, hot_other, bag)
+    own_sums = pool_rows(places_own, terms, bag)
     parts = [own_sums]
     for step, block in zip(steps + [near], places + [near_back]):
-        part = pool_rows(block, hot_own, hot_other, bag)
+        part = pool_rows(block, terms, bag)
         parts.append(across(part, 0, step))
     wides = [across(wide_own, 0, step) for step in steps]
     score_row, pooled = score(parts, bottom_out, linear, top_pairs, cotangent)
     scores = [score_row] + [across(score_row, 0, step) for step in steps + [near]]
-    activation, bottom_grad = finish_dense(
-        pooled, bottom_out, linear, top_pairs, cotangent, top_dense
+    activation, bottom_grad, blank = finish_dense(
+        pooled, bottom_out, linear, top_pairs, cotangent, top_dense, win_size
     )
     places = [places_own] + places + [near_back]
     wides = [near_own] + wides + [near_back]
@@ -467,7 +511,7 @@
     kept = row_grads(scores, places, wides, bag, group_count, True)
     owned = split_owners(kept, received, group_count)
     blocks = [owned[0]] + [across(owned[step], step, 1) for step in range(1, group_count)]
-    table_grad = place_rows(starts, blocks, win_size)
+    table_grad = place_rows(starts, blocks, blank)
     return activation, bottom_grad, table_grad[None, None]
 
 

time: 39 us -> 38.6 us (0.990)
  starting transfers between devices: 20.3 us -> 19.5 us
    pallas_call x1, Pallas kernels: 1.14 us -> 2.11 us  [finish_dense(): pl.pallas_call(kernel, out_shape=(jax.ShapeDtypeStruct((samples, hidden),...]
    ppermute x16, starting transfers between devices: 20.3 us -> 19.5 us  [across(): return lax.ppermute(values, ('grp', 'shard'), pairs)]
    pallas_call x4, Pallas kernels: 1.94 us -> 1.52 us  [pool_rows(): pl.pallas_call(kernel, out_shape=jax.ShapeDtypeStruct((samples, width), j...]
  transfers between devices with their start and end apart: 16 -> 16, of which waited for: 6 -> 6; matrix products, arithmetic and copies ran while one was open for 0% -> 0% of each run, Pallas kernels for 11% -> 12%
where the time goes in v6:
time: 38.6 us; the launch traced here: 38.5 us
  starting transfers between devices  19.5 us (51%)
  waiting for transfers between devices  9.83 us (25%)
  Pallas kernels  8.37 us (22%)
  between operations  0.78 us (2%)
    ppermute x16, starting transfers between devices, across(): return lax.ppermute(values, ('grp', 'shard'), pairs)  19.5 us
    ppermute x16, waiting for transfers between devices, across(): return lax.ppermute(values, ('grp', 'shard'), pairs)  9.83 us
    pallas_call x1, Pallas kernels, finish_dense(): pl.pallas_call(kernel, out_shape=(jax.ShapeDtypeStruct((samples, hidden),...  2.11 us
    pallas_call x1, Pallas kernels, load_first(): pl.pallas_call(kernel, out_shape=(jax.ShapeDtypeStruct((group_count * HOT...  1.84 us
    pallas_call x4, Pallas kernels, pool_rows(): pl.pallas_call(kernel, out_shape=jax.ShapeDtypeStruct((samples, width), j...  1.52 us
    pallas_call x1, Pallas kernels, place_rows(): pl.pallas_call(kernel, out_shape=jax.ShapeDtypeStruct((win_size, width),...  1.36 us
    pallas_call x2, Pallas kernels, row_grads(): pl.pallas_call(kernel, out_shape=jax.ShapeDtypeStruct((group_count * HOT,...  0.85 us
  transfers between devices with their start and end apart: 16, of which 6 were waited for; matrix products, arithmetic and copies ran while one was open for 0% of the time, Pallas kernels for 12%

profile of v6, /device:TPU:0, one launch (start us, length us, event | category | flops | bytes accessed | tf_op | source)
XLA Modules:
  0.0 38.5 jit_solution(3125133833596633131)
XLA Ops:
  0.7 1.8 %load_first.1 = (f32[256,128]{1,0:T(8,128)S(1)}, f32[8,128]{1,0:T(8,128)S(1)}, f32[136,128]{1,0:T(8,128)S(1)}, f32[128,128]{1,0:T(8,128)S(1)}) custom-call(s32[4,32]{1,0:T(4,128)} %starts_ref.3, s32[4,128]{1,0:T(4,128)} %bitcast.7, bf16[128,128]{1,0:T(8,128)(2,1)} %bottom_ref.5, f32[7872,128]{1,0:T(8,128)} %bitcast.5), custom_call_target="tpu_custom_call" | custom-call | flops 1000000 | bytes 1000000 | tf_op jit(solution)/shard_map/load_first/pallas_call | solution.py:199
  2.5 0.6 %collective-permute-start = (f32[256,128]{1,0:T(8,128)S(1)}, f32[256,128]{1,0:T(8,128)S(1)}, u32[]{:S(2)}, u32[]{:S(2)}) collective-permute-start(f32[256,128]{1,0:T(8,128)S(1)} %get-tuple-element.17.own_ref), channel_id=1, source_target_pairs={{0,1},{1,0},{2,3},{3,2},{4,5},{5,4},{6,7},{7,6},{8,9},{9,8},{10,11... | collective-permute-start | bytes 393224 | tf_op jit(solution)/shard_map/ppermute | solution.py:483
  3.1 2.7 %collective-permute-start.5 = (f32[136,128]{1,0:T(8,128)S(1)}, f32[136,128]{1,0:T(8,128)S(1)}, u32[]{:S(2)}, u32[]{:S(2)}) collective-permute-start(f32[136,128]{1,0:T(8,128)S(1)} %get-tuple-element.18.refs_8_), channel_id=1, source_target_pairs={{0,3},{1,2},{2,1},{3,0},{4,7},{5,6},{6,5},{7,4},{8,11},{9,10},{10,... | collective-permute-start | bytes 208904 | tf_op jit(solution)/shard_map/ppermute | solution.py:483
  5.8 2.2 %collective-permute-start.1 = (f32[8,128]{1,0:T(8,128)S(1)}, f32[8,128]{1,0:T(8,128)S(1)}, u32[]{:S(2)}, u32[]{:S(2)}) collective-permute-start(f32[8,128]{1,0:T(8,128)S(1)} %get-tuple-element.16.places_ref.refs_4_), channel_id=1, source_target_pairs={{0,7},{1,6},{2,5},{3,4},{4,3},{5,2},{6,1},{7,0},{8,15},{9,14},{10,... | collective-permute-start | bytes 12296 | tf_op jit(solution)/shard_map/ppermute | solution.py:483
  8.1 2.5 %collective-permute-done.1.places_ref.refs_5_ = f32[8,128]{1,0:T(8,128)S(1)} collective-permute-done((f32[8,128]{1,0:T(8,128)S(1)}, f32[8,128]{1,0:T(8,128)S(1)}, u32[]{:S(2)}, u32[]{:S(2)}) %collective-permute-start.1) | collective-permute-done | bytes 4128 | tf_op jit(solution)/shard_map/ppermute | solution.py:483
  11.0 2.2 %collective-permute-start.2 = (f32[128,128]{1,0:T(8,128)S(1)}, f32[128,128]{1,0:T(8,128)S(1)}, u32[]{:S(2)}, u32[]{:S(2)}) collective-permute-start(f32[128,128]{1,0:T(8,128)S(1)} %pool_rows.5), channel_id=1, source_target_pairs={{0,7},{1,6},{2,5},{3,4},{4,3},{5,2},{6,1},{7,0},{8,15},{9,14},{10,... | collective-permute-start | bytes 196616 | tf_op jit(solution)/shard_map/ppermute | solution.py:483
  14.1 1.7 %collective-permute-start.6 = (f32[128,128]{1,0:T(8,128)S(1)}, f32[128,128]{1,0:T(8,128)S(1)}, u32[]{:S(2)}, u32[]{:S(2)}) collective-permute-start(f32[128,128]{1,0:T(8,128)S(1)} %pool_rows.7), channel_id=1, source_target_pairs={{0,3},{1,2},{2,1},{3,0},{4,7},{5,6},{6,5},{7,4},{8,11},{9,10},{10,... | collective-permute-start | bytes 196616 | tf_op jit(solution)/shard_map/ppermute | solution.py:483
  15.8 1.1 %collective-permute-start.11 = (f32[128,128]{1,0:T(8,128)S(1)}, f32[128,128]{1,0:T(8,128)S(1)}, u32[]{:S(2)}, u32[]{:S(2)}) collective-permute-start(f32[128,128]{1,0:T(8,128)S(1)} %get-tuple-element.23), channel_id=1, source_target_pairs={{0,5},{1,4},{2,7},{3,6},{4,1},{5,0},{6,3},{7,2},{8,13},{9,12},{10,... | collective-permute-start | bytes 196616 | tf_op jit(solution)/shard_map/ppermute | solution.py:483
  16.8 1.4 %collective-permute-start.10 = (f32[128,128]{1,0:T(8,128)S(1)}, f32[128,128]{1,0:T(8,128)S(1)}, u32[]{:S(2)}, u32[]{:S(2)}) collective-permute-start(f32[128,128]{1,0:T(8,128)S(1)} %get-tuple-element.23), channel_id=1, source_target_pairs={{0,7},{1,6},{2,5},{3,4},{4,3},{5,2},{6,1},{7,0},{8,15},{9,14},{10,... | collective-permute-start | bytes 196616 | tf_op jit(solution)/shard_map/ppermute | solution.py:483
  18.8 1.2 %collective-permute-done.4.refs_2_ = f32[128,128]{1,0:T(8,128)S(1)} collective-permute-done((f32[128,128]{1,0:T(8,128)S(1)}, f32[128,128]{1,0:T(8,128)S(1)}, u32[]{:S(2)}, u32[]{:S(2)}) %collective-permute-start.4) | collective-permute-done | bytes 65568 | tf_op jit(solution)/shard_map/ppermute | solution.py:483
  20.1 0.4 %score.1 = (f32[1,128]{1,0:T(1,128)S(1)}, f32[128,128]{1,0:T(8,128)S(1)}) custom-call(f32[128,128]{1,0:T(8,128)S(1)} %pool_rows.4.refs_0_, f32[128,128]{1,0:T(8,128)S(1)} %collective-permute-done.2.refs_1_, f32[128,128]{1,0:T(8,128)S(1)} %collective-permute-done.4.refs_2_, f32[128,128]{1,0:T(8,128)S(1)} %collective-permute-done.6.refs_3_, ...), custom_call_target="tpu_custom_call" | custom-call | flops 10000000 | bytes 1000000 | tf_op jit(solution)/shard_map/score/pallas_call | solution.py:317
  20.9 2.5 %collective-permute-start.8 = (f32[1,128]{1,0:T(1,128)S(1)}, f32[1,128]{1,0:T(1,128)S(1)}, u32[]{:S(2)}, u32[]{:S(2)}) collective-permute-start(f32[1,128]{1,0:T(1,128)S(1)} %get-tuple-element.22.refs_0_), channel_id=1, source_target_pairs={{0,5},{1,4},{2,7},{3,6},{4,1},{5,0},{6,3},{7,2},{8,13},{9,12},{10,... | collective-permute-start | bytes 1544 | tf_op jit(solution)/shard_map/ppermute | solution.py:483
  23.4 1.0 %collective-permute-start.7 = (f32[1,128]{1,0:T(1,128)S(1)}, f32[1,128]{1,0:T(1,128)S(1)}, u32[]{:S(2)}, u32[]{:S(2)}) collective-permute-start(f32[1,128]{1,0:T(1,128)S(1)} %get-tuple-element.22.refs_0_), channel_id=1, source_target_pairs={{0,7},{1,6},{2,5},{3,4},{4,3},{5,2},{6,1},{7,0},{8,15},{9,14},{10,... | collective-permute-start | bytes 1544 | tf_op jit(solution)/shard_map/ppermute | solution.py:483
  24.5 1.1 %collective-permute-done.8.refs_2_ = f32[1,128]{1,0:T(1,128)S(1)} collective-permute-done((f32[1,128]{1,0:T(1,128)S(1)}, f32[1,128]{1,0:T(1,128)S(1)}, u32[]{:S(2)}, u32[]{:S(2)}) %collective-permute-start.8) | collective-permute-done | bytes 544 | tf_op jit(solution)/shard_map/ppermute | solution.py:483
  25.6 2.6 %collective-permute-done.7.refs_1_ = f32[1,128]{1,0:T(1,128)S(1)} collective-permute-done((f32[1,128]{1,0:T(1,128)S(1)}, f32[1,128]{1,0:T(1,128)S(1)}, u32[]{:S(2)}, u32[]{:S(2)}) %collective-permute-start.7) | collective-permute-done | bytes 544 | tf_op jit(solution)/shard_map/ppermute | solution.py:483
  28.2 0.4 %row_grads_given.1 = f32[256,128]{1,0:T(8,128)S(1)} custom-call(f32[1,128]{1,0:T(1,128)S(1)} %get-tuple-element.22.refs_0_, f32[1,128]{1,0:T(1,128)S(1)} %collective-permute-done.7.refs_1_, f32[1,128]{1,0:T(1,128)S(1)} %collective-permute-done.8.refs_2_, f32[1,128]{1,0:T(1,128)S(1)} %collective-permute-done.9.refs_3_, ...), custom_call_target="tpu_custom_call" | custom-call | flops 100000000 | bytes 1000000 | tf_op jit(solution)/shard_map/row_grads_given/pallas_call | solution.py:398
  29.0 0.4 %row_grads_kept.1.kept_ref = f32[256,128]{1,0:T(8,128)S(1)} custom-call(f32[1,128]{1,0:T(1,128)S(1)} %get-tuple-element.22.refs_0_, f32[1,128]{1,0:T(1,128)S(1)} %collective-permute-done.7.refs_1_, f32[1,128]{1,0:T(1,128)S(1)} %collective-permute-done.8.refs_2_, f32[1,128]{1,0:T(1,128)S(1)} %collective-permute-done.9.refs_3_, ...), custom_call_target="tpu_custom_call" | custom-call | flops 100000000 | bytes 1000000 | tf_op jit(solution)/shard_map/row_grads_kept/pallas_call | solution.py:398
  29.4 0.6 %collective-permute-done.12.received_ref = f32[256,128]{1,0:T(8,128)S(1)} collective-permute-done((f32[256,128]{1,0:T(8,128)S(1)}, f32[256,128]{1,0:T(8,128)S(1)}, u32[]{:S(2)}, u32[]{:S(2)}) %collective-permute-start.12) | collective-permute-done | bytes 131104 | tf_op jit(solution)/shard_map/ppermute | solution.py:483
  30.1 1.5 %collective-permute-start.13 = (f32[64,128]{1,0:T(8,128)S(1)}, f32[64,128]{1,0:T(8,128)S(1)}, u32[]{:S(2)}, u32[]{:S(2)}) collective-permute-start(f32[64,128]{1,0:T(8,128)S(1)} %get-tuple-element.25), channel_id=1, source_target_pairs={{0,9},{1,8},{2,11},{3,10},{4,13},{5,12},{6,15},{7,14},{8,1},{9,0},... | collective-permute-start | bytes 98312 | tf_op jit(solution)/shard_map/ppermute | solution.py:483
  31.5 1.3 %collective-permute-start.14 = (f32[64,128]{1,0:T(8,128)S(1)}, f32[64,128]{1,0:T(8,128)S(1)}, u32[]{:S(2)}, u32[]{:S(2)}) collective-permute-start(f32[64,128]{1,0:T(8,128)S(1)} %get-tuple-element.26), channel_id=1, source_target_pairs={{0,17},{1,16},{2,19},{3,18},{4,21},{5,20},{6,23},{7,22},{8,25},{9,... | collective-permute-start | bytes 98312 | tf_op jit(solution)/shard_map/ppermute | solution.py:483
  32.9 0.4 %collective-permute-start.15 = (f32[64,128]{1,0:T(8,128)S(1)}, f32[64,128]{1,0:T(8,128)S(1)}, u32[]{:S(2)}, u32[]{:S(2)}) collective-permute-start(f32[64,128]{1,0:T(8,128)S(1)} %get-tuple-element.27), channel_id=1, source_target_pairs={{0,25},{1,24},{2,27},{3,26},{4,29},{5,28},{6,31},{7,30},{8,17},{9,... | collective-permute-start | bytes 98312 | tf_op jit(solution)/shard_map/ppermute | solution.py:483
  33.3 2.1 %finish_dense.1 = (bf16[128,1024]{1,0:T(8,128)(2,1)}, f32[128,128]{1,0:T(8,128)}, f32[1968,128]{1,0:T(8,128)}) custom-call(f32[128,128]{1,0:T(8,128)S(1)} %get-tuple-element.19.pooled_ref, bf16[128,128]{1,0:T(8,128)(2,1)S(1)} %copy-done.2, f32[128,1024]{1,0:T(8,128)S(1)} %linear_part.1.refs_5_.linear_ref, f32[1,1024]{1,0:T(1,128)S(1)} %copy-done.3, ...), custom_call_target="tpu_custom_call" | custom-call | flops 50000000 | bytes 1000000 | tf_op jit(solution)/shard_map/finish_dense/pallas_call | solution.py:356
  35.4 1.7 %collective-permute-done.15.refs_3_ = f32[64,128]{1,0:T(8,128)S(1)} collective-permute-done((f32[64,128]{1,0:T(8,128)S(1)}, f32[64,128]{1,0:T(8,128)S(1)}, u32[]{:S(2)}, u32[]{:S(2)}) %collective-permute-start.15) | collective-permute-done | bytes 32800 | tf_op jit(solution)/shard_map/ppermute | solution.py:483
  37.1 1.4 %place_rows.1 = f32[1968,128]{1,0:T(8,128)} custom-call(s32[4,32]{1,0:T(4,128)S(1)} %copy-done.4, f32[64,128]{1,0:T(8,128)S(1)} %get-tuple-element.24.refs_0_, f32[64,128]{1,0:T(8,128)S(1)} %collective-permute-done.13.refs_1_, f32[64,128]{1,0:T(8,128)S(1)} %collective-permute-done.14.refs_2_, ...), custom_call_target="tpu_custom_call", output_to_operand_aliasing={{}: (5, {})} | custom-call | flops 1000000 | bytes 2000000 | tf_op jit(solution)/shard_map/place_rows/pallas_call | solution.py:455
  (31 shorter events, 2.8 us)
Async XLA Ops:
  0.6 17.6 %copy-start.2 = (bf16[128,128]{1,0:T(8,128)(2,1)S(1)}, bf16[128,128]{1,0:T(8,128)(2,1)}, u32[]{:S(2)}) copy-start(bf16[128,128]{1,0:T(8,128)(2,1)} %bottom_ref.5) | copy-start | bytes 98308
  0.6 17.6 %copy-start.1 = (bf16[128,1024]{1,0:T(8,128)(2,1)S(1)}, bf16[128,1024]{1,0:T(8,128)(2,1)}, u32[]{:S(2)}) copy-start(bf16[128,1024]{1,0:T(8,128)(2,1)} %dense_ref.3) | copy-start | bytes 786436
  0.7 19.4 %copy-start = (f32[128,1024]{1,0:T(8,128)S(1)}, f32[128,1024]{1,0:T(8,128)}, u32[]{:S(2)}) copy-start(f32[128,1024]{1,0:T(8,128)} %cot_ref.1) | copy-start | bytes 1572868
  0.7 19.4 %copy-start.3 = (f32[1,1024]{1,0:T(1,128)S(1)}, f32[1,1024]{1,0:T(1,128)}, u32[]{:S(2)}) copy-start(f32[1,1024]{1,0:T(1,128)} %pairs_ref.1) | copy-start | bytes 12292
  2.5 34.6 %copy-start.4 = (s32[4,32]{1,0:T(4,128)S(1)}, s32[4,32]{1,0:T(4,128)}, u32[]{:S(2)}) copy-start(s32[4,32]{1,0:T(4,128)} %starts_ref.3) | copy-start | bytes 1540
  2.5 5.5 %collective-permute-start = (f32[256,128]{1,0:T(8,128)S(1)}, f32[256,128]{1,0:T(8,128)S(1)}, u32[]{:S(2)}, u32[]{:S(2)}) collective-permute-start(f32[256,128]{1,0:T(8,128)S(1)} %get-tuple-element.17.own_ref), channel_id=1, source_target_pairs={{0,1},{1,0},{2,3},{3,2},{4,5},{5,4},{6,7},{7,6},{8,9},{9,8},{10,11... | collective-permute-start | bytes 393224 | tf_op jit(solution)/shard_map/ppermute | solution.py:483
  3.1 10.6 %collective-permute-start.5 = (f32[136,128]{1,0:T(8,128)S(1)}, f32[136,128]{1,0:T(8,128)S(1)}, u32[]{:S(2)}, u32[]{:S(2)}) collective-permute-start(f32[136,128]{1,0:T(8,128)S(1)} %get-tuple-element.18.refs_8_), channel_id=1, source_target_pairs={{0,3},{1,2},{2,1},{3,0},{4,7},{5,6},{6,5},{7,4},{8,11},{9,10},{10,... | collective-permute-start | bytes 208904 | tf_op jit(solution)/shard_map/ppermute | solution.py:483
  5.8 4.9 %collective-permute-start.1 = (f32[8,128]{1,0:T(8,128)S(1)}, f32[8,128]{1,0:T(8,128)S(1)}, u32[]{:S(2)}, u32[]{:S(2)}) collective-permute-start(f32[8,128]{1,0:T(8,128)S(1)} %get-tuple-element.16.places_ref.refs_4_), channel_id=1, source_target_pairs={{0,7},{1,6},{2,5},{3,4},{4,3},{5,2},{6,1},{7,0},{8,15},{9,14},{10,... | collective-permute-start | bytes 12296 | tf_op jit(solution)/shard_map/ppermute | solution.py:483
  7.9 5.3 %collective-permute-start.3 = (f32[8,128]{1,0:T(8,128)S(1)}, f32[8,128]{1,0:T(8,128)S(1)}, u32[]{:S(2)}, u32[]{:S(2)}) collective-permute-start(f32[8,128]{1,0:T(8,128)S(1)} %get-tuple-element.16.places_ref.refs_4_), channel_id=1, source_target_pairs={{0,5},{1,4},{2,7},{3,6},{4,1},{5,0},{6,3},{7,2},{8,13},{9,12},{10,... | collective-permute-start | bytes 12296 | tf_op jit(solution)/shard_map/ppermute | solution.py:483
  11.0 7.8 %collective-permute-start.2 = (f32[128,128]{1,0:T(8,128)S(1)}, f32[128,128]{1,0:T(8,128)S(1)}, u32[]{:S(2)}, u32[]{:S(2)}) collective-permute-start(f32[128,128]{1,0:T(8,128)S(1)} %pool_rows.5), channel_id=1, source_target_pairs={{0,7},{1,6},{2,5},{3,4},{4,3},{5,2},{6,1},{7,0},{8,15},{9,14},{10,... | collective-permute-start | bytes 196616 | tf_op jit(solution)/shard_map/ppermute | solution.py:483
  13.6 6.5 %collective-permute-start.4 = (f32[128,128]{1,0:T(8,128)S(1)}, f32[128,128]{1,0:T(8,128)S(1)}, u32[]{:S(2)}, u32[]{:S(2)}) collective-permute-start(f32[128,128]{1,0:T(8,128)S(1)} %pool_rows.6), channel_id=1, source_target_pairs={{0,5},{1,4},{2,7},{3,6},{4,1},{5,0},{6,3},{7,2},{8,13},{9,12},{10,... | collective-permute-start | bytes 196616 | tf_op jit(solution)/shard_map/ppermute | solution.py:483
  14.1 6.0 %collective-permute-start.6 = (f32[128,128]{1,0:T(8,128)S(1)}, f32[128,128]{1,0:T(8,128)S(1)}, u32[]{:S(2)}, u32[]{:S(2)}) collective-permute-start(f32[128,128]{1,0:T(8,128)S(1)} %pool_rows.7), channel_id=1, source_target_pairs={{0,3},{1,2},{2,1},{3,0},{4,7},{5,6},{6,5},{7,4},{8,11},{9,10},{10,... | collective-permute-start | bytes 196616 | tf_op jit(solution)/shard_map/ppermute | solution.py:483
  15.8 8.7 %collective-permute-start.11 = (f32[128,128]{1,0:T(8,128)S(1)}, f32[128,128]{1,0:T(8,128)S(1)}, u32[]{:S(2)}, u32[]{:S(2)}) collective-permute-start(f32[128,128]{1,0:T(8,128)S(1)} %get-tuple-element.23), channel_id=1, source_target_pairs={{0,5},{1,4},{2,7},{3,6},{4,1},{5,0},{6,3},{7,2},{8,13},{9,12},{10,... | collective-permute-start | bytes 196616 | tf_op jit(solution)/shard_map/ppermute | solution.py:483
  16.8 7.6 %collective-permute-start.10 = (f32[128,128]{1,0:T(8,128)S(1)}, f32[128,128]{1,0:T(8,128)S(1)}, u32[]{:S(2)}, u32[]{:S(2)}) collective-permute-start(f32[128,128]{1,0:T(8,128)S(1)} %get-tuple-element.23), channel_id=1, source_target_pairs={{0,7},{1,6},{2,5},{3,4},{4,3},{5,2},{6,1},{7,0},{8,15},{9,14},{10,... | collective-permute-start | bytes 196616 | tf_op jit(solution)/shard_map/ppermute | solution.py:483
  20.5 3.9 %collective-permute-start.9 = (f32[1,128]{1,0:T(1,128)S(1)}, f32[1,128]{1,0:T(1,128)S(1)}, u32[]{:S(2)}, u32[]{:S(2)}) collective-permute-start(f32[1,128]{1,0:T(1,128)S(1)} %get-tuple-element.22.refs_0_), channel_id=1, source_target_pairs={{0,3},{1,2},{2,1},{3,0},{4,7},{5,6},{6,5},{7,4},{8,11},{9,10},{10,... | collective-permute-start | bytes 1544 | tf_op jit(solution)/shard_map/ppermute | solution.py:483
  20.9 4.6 %collective-permute-start.8 = (f32[1,128]{1,0:T(1,128)S(1)}, f32[1,128]{1,0:T(1,128)S(1)}, u32[]{:S(2)}, u32[]{:S(2)}) collective-permute-start(f32[1,128]{1,0:T(1,128)S(1)} %get-tuple-element.22.refs_0_), channel_id=1, source_target_pairs={{0,5},{1,4},{2,7},{3,6},{4,1},{5,0},{6,3},{7,2},{8,13},{9,12},{10,... | collective-permute-start | bytes 1544 | tf_op jit(solution)/shard_map/ppermute | solution.py:483
  23.4 4.8 %collective-permute-start.7 = (f32[1,128]{1,0:T(1,128)S(1)}, f32[1,128]{1,0:T(1,128)S(1)}, u32[]{:S(2)}, u32[]{:S(2)}) collective-permute-start(f32[1,128]{1,0:T(1,128)S(1)} %get-tuple-element.22.refs_0_), channel_id=1, source_target_pairs={{0,7},{1,6},{2,5},{3,4},{4,3},{5,2},{6,1},{7,0},{8,15},{9,14},{10,... | collective-permute-start | bytes 1544 | tf_op jit(solution)/shard_map/ppermute | solution.py:483
  28.6 1.4 %collective-permute-start.12 = (f32[256,128]{1,0:T(8,128)S(1)}, f32[256,128]{1,0:T(8,128)S(1)}, u32[]{:S(2)}, u32[]{:S(2)}) collective-permute-start(f32[256,128]{1,0:T(8,128)S(1)} %row_grads_given.1), channel_id=1, source_target_pairs={{0,1},{1,0},{2,3},{3,2},{4,5},{5,4},{6,7},{7,6},{8,9},{9,8},{10,11... | collective-permute-start | bytes 393224 | tf_op jit(solution)/shard_map/ppermute | solution.py:483
  30.1 5.3 %collective-permute-start.13 = (f32[64,128]{1,0:T(8,128)S(1)}, f32[64,128]{1,0:T(8,128)S(1)}, u32[]{:S(2)}, u32[]{:S(2)}) collective-permute-start(f32[64,128]{1,0:T(8,128)S(1)} %get-tuple-element.25), channel_id=1, source_target_pairs={{0,9},{1,8},{2,11},{3,10},{4,13},{5,12},{6,15},{7,14},{8,1},{9,0},... | collective-permute-start | bytes 98312 | tf_op jit(solution)/shard_map/ppermute | solution.py:483
  31.5 3.9 %collective-permute-start.14 = (f32[64,128]{1,0:T(8,128)S(1)}, f32[64,128]{1,0:T(8,128)S(1)}, u32[]{:S(2)}, u32[]{:S(2)}) collective-permute-start(f32[64,128]{1,0:T(8,128)S(1)} %get-tuple-element.26), channel_id=1, source_target_pairs={{0,17},{1,16},{2,19},{3,18},{4,21},{5,20},{6,23},{7,22},{8,25},{9,... | collective-permute-start | bytes 98312 | tf_op jit(solution)/shard_map/ppermute | solution.py:483
  32.9 4.2 %collective-permute-start.15 = (f32[64,128]{1,0:T(8,128)S(1)}, f32[64,128]{1,0:T(8,128)S(1)}, u32[]{:S(2)}, u32[]{:S(2)}) collective-permute-start(f32[64,128]{1,0:T(8,128)S(1)} %get-tuple-element.27), channel_id=1, source_target_pairs={{0,25},{1,24},{2,27},{3,26},{4,29},{5,28},{6,31},{7,30},{8,17},{9,... | collective-permute-start | bytes 98312 | tf_op jit(solution)/shard_map/ppermute | solution.py:483

commit v7 on v6

--- a/solution.py
+++ b/solution.py
@@ -436,10 +436,14 @@
         out_ref, held, sems = refs[count + 1 :]
         grp_pos = lax.axis_index("grp")
         column = lax.axis_index("shard") * count + grp_pos
+        known = starts_ref[...]
+        lines = lax.broadcasted_iota(jnp.int32, known.shape, 0)
+        windows = lax.broadcasted_iota(jnp.int32, known.shape, 1)
         held[...] = jnp.zeros_like(held)
         firsts = [jnp.int32(0)]
         for step, ref in enumerate(block_refs):
-            start = starts_ref[jnp.bitwise_xor(grp_pos, step), column]
+            asked = (lines == jnp.bitwise_xor(grp_pos, step)) & (windows == column)
+            start = jnp.sum(jnp.where(asked, known, 0))
             firsts.append(jnp.minimum(start // 8 * 8, win_size - head))
             held[pl.ds(start, HOT), :] += ref[...]
         held[pl.ds(0, HOT), :] += held[pl.ds(win_size, HOT), :]
@@ -455,7 +459,7 @@
     return pl.pallas_call(
         kernel,
         out_shape=jax.ShapeDtypeStruct((win_size, width), jnp.float32),
-        in_specs=[whole(pltpu.SMEM)] + [whole()] * count + [whole(pltpu.HBM)],
+        in_specs=[whole()] * (1 + count) + [whole(pltpu.HBM)],
         out_specs=whole(pltpu.HBM),
         input_output_aliases={1 + count: 0},
         scratch_shapes=[

time: 38.6 us -> 38.2 us (0.990)
  Pallas kernels: 8.37 us -> 7.88 us
    pallas_call x1, Pallas kernels: 1.36 us -> 0.87 us  [place_rows(): pl.pallas_call(kernel, out_shape=jax.ShapeDtypeStruct((win_size, width),...]
where the time goes in v7:
time: 38.2 us; the launch traced here: 38 us
  starting transfers between devices  19.5 us (51%)
  waiting for transfers between devices  9.83 us (26%)
  Pallas kernels  7.88 us (21%)
  between operations  0.78 us (2%)
    ppermute x16, starting transfers between devices, across(): return lax.ppermute(values, ('grp', 'shard'), pairs)  19.5 us
    ppermute x16, waiting for transfers between devices, across(): return lax.ppermute(values, ('grp', 'shard'), pairs)  9.83 us
    pallas_call x1, Pallas kernels, finish_dense(): pl.pallas_call(kernel, out_shape=(jax.ShapeDtypeStruct((samples, hidden),...  2.11 us
    pallas_call x1, Pallas kernels, load_first(): pl.pallas_call(kernel, out_shape=(jax.ShapeDtypeStruct((group_count * HOT...  1.84 us
    pallas_call x4, Pallas kernels, pool_rows(): pl.pallas_call(kernel, out_shape=jax.ShapeDtypeStruct((samples, width), j...  1.52 us
    pallas_call x1, Pallas kernels, place_rows(): pl.pallas_call(kernel, out_shape=jax.ShapeDtypeStruct((win_size, width),...  0.87 us
    pallas_call x2, Pallas kernels, row_grads(): pl.pallas_call(kernel, out_shape=jax.ShapeDtypeStruct((group_count * HOT,...  0.85 us
  transfers between devices with their start and end apart: 16, of which 6 were waited for; matrix products, arithmetic and copies ran while one was open for 0% of the time, Pallas kernels for 12%

profile of v7, /device:TPU:0, one launch (start us, length us, event | category | flops | bytes accessed | tf_op | source)
XLA Modules:
  0.0 38.0 jit_solution(11385086756850518806)
XLA Ops:
  0.7 1.8 %load_first.1 = (f32[256,128]{1,0:T(8,128)S(1)}, f32[8,128]{1,0:T(8,128)S(1)}, f32[136,128]{1,0:T(8,128)S(1)}, f32[128,128]{1,0:T(8,128)S(1)}) custom-call(s32[4,32]{1,0:T(4,128)} %starts_ref.3, s32[4,128]{1,0:T(4,128)} %bitcast.7, bf16[128,128]{1,0:T(8,128)(2,1)} %bottom_ref.5, f32[7872,128]{1,0:T(8,128)} %bitcast.5), custom_call_target="tpu_custom_call" | custom-call | flops 1000000 | bytes 1000000 | tf_op jit(solution)/shard_map/load_first/pallas_call | solution.py:199
  2.5 0.6 %collective-permute-start = (f32[256,128]{1,0:T(8,128)S(1)}, f32[256,128]{1,0:T(8,128)S(1)}, u32[]{:S(2)}, u32[]{:S(2)}) collective-permute-start(f32[256,128]{1,0:T(8,128)S(1)} %get-tuple-element.17.own_ref), channel_id=1, source_target_pairs={{0,1},{1,0},{2,3},{3,2},{4,5},{5,4},{6,7},{7,6},{8,9},{9,8},{10,11... | collective-permute-start | bytes 393224 | tf_op jit(solution)/shard_map/ppermute | solution.py:487
  3.1 2.7 %collective-permute-start.5 = (f32[136,128]{1,0:T(8,128)S(1)}, f32[136,128]{1,0:T(8,128)S(1)}, u32[]{:S(2)}, u32[]{:S(2)}) collective-permute-start(f32[136,128]{1,0:T(8,128)S(1)} %get-tuple-element.18.refs_8_), channel_id=1, source_target_pairs={{0,3},{1,2},{2,1},{3,0},{4,7},{5,6},{6,5},{7,4},{8,11},{9,10},{10,... | collective-permute-start | bytes 208904 | tf_op jit(solution)/shard_map/ppermute | solution.py:487
  5.8 2.2 %collective-permute-start.1 = (f32[8,128]{1,0:T(8,128)S(1)}, f32[8,128]{1,0:T(8,128)S(1)}, u32[]{:S(2)}, u32[]{:S(2)}) collective-permute-start(f32[8,128]{1,0:T(8,128)S(1)} %get-tuple-element.16.places_ref.refs_4_), channel_id=1, source_target_pairs={{0,7},{1,6},{2,5},{3,4},{4,3},{5,2},{6,1},{7,0},{8,15},{9,14},{10,... | collective-permute-start | bytes 12296 | tf_op jit(solution)/shard_map/ppermute | solution.py:487
  8.1 2.5 %collective-permute-done.1.places_ref.refs_5_ = f32[8,128]{1,0:T(8,128)S(1)} collective-permute-done((f32[8,128]{1,0:T(8,128)S(1)}, f32[8,128]{1,0:T(8,128)S(1)}, u32[]{:S(2)}, u32[]{:S(2)}) %collective-permute-start.1) | collective-permute-done | bytes 4128 | tf_op jit(solution)/shard_map/ppermute | solution.py:487
  11.0 2.2 %collective-permute-start.2 = (f32[128,128]{1,0:T(8,128)S(1)}, f32[128,128]{1,0:T(8,128)S(1)}, u32[]{:S(2)}, u32[]{:S(2)}) collective-permute-start(f32[128,128]{1,0:T(8,128)S(1)} %pool_rows.5), channel_id=1, source_target_pairs={{0,7},{1,6},{2,5},{3,4},{4,3},{5,2},{6,1},{7,0},{8,15},{9,14},{10,... | collective-permute-start | bytes 196616 | tf_op jit(solution)/shard_map/ppermute | solution.py:487
  14.1 1.7 %collective-permute-start.6 = (f32[128,128]{1,0:T(8,128)S(1)}, f32[128,128]{1,0:T(8,128)S(1)}, u32[]{:S(2)}, u32[]{:S(2)}) collective-permute-start(f32[128,128]{1,0:T(8,128)S(1)} %pool_rows.7), channel_id=1, source_target_pairs={{0,3},{1,2},{2,1},{3,0},{4,7},{5,6},{6,5},{7,4},{8,11},{9,10},{10,... | collective-permute-start | bytes 196616 | tf_op jit(solution)/shard_map/ppermute | solution.py:487
  15.8 1.1 %collective-permute-start.11 = (f32[128,128]{1,0:T(8,128)S(1)}, f32[128,128]{1,0:T(8,128)S(1)}, u32[]{:S(2)}, u32[]{:S(2)}) collective-permute-start(f32[128,128]{1,0:T(8,128)S(1)} %get-tuple-element.23), channel_id=1, source_target_pairs={{0,5},{1,4},{2,7},{3,6},{4,1},{5,0},{6,3},{7,2},{8,13},{9,12},{10,... | collective-permute-start | bytes 196616 | tf_op jit(solution)/shard_map/ppermute | solution.py:487
  16.8 1.4 %collective-permute-start.10 = (f32[128,128]{1,0:T(8,128)S(1)}, f32[128,128]{1,0:T(8,128)S(1)}, u32[]{:S(2)}, u32[]{:S(2)}) collective-permute-start(f32[128,128]{1,0:T(8,128)S(1)} %get-tuple-element.23), channel_id=1, source_target_pairs={{0,7},{1,6},{2,5},{3,4},{4,3},{5,2},{6,1},{7,0},{8,15},{9,14},{10,... | collective-permute-start | bytes 196616 | tf_op jit(solution)/shard_map/ppermute | solution.py:487
  18.8 1.2 %collective-permute-done.4.refs_2_ = f32[128,128]{1,0:T(8,128)S(1)} collective-permute-done((f32[128,128]{1,0:T(8,128)S(1)}, f32[128,128]{1,0:T(8,128)S(1)}, u32[]{:S(2)}, u32[]{:S(2)}) %collective-permute-start.4) | collective-permute-done | bytes 65568 | tf_op jit(solution)/shard_map/ppermute | solution.py:487
  20.1 0.4 %score.1 = (f32[1,128]{1,0:T(1,128)S(1)}, f32[128,128]{1,0:T(8,128)S(1)}) custom-call(f32[128,128]{1,0:T(8,128)S(1)} %pool_rows.4.refs_0_, f32[128,128]{1,0:T(8,128)S(1)} %collective-permute-done.2.refs_1_, f32[128,128]{1,0:T(8,128)S(1)} %collective-permute-done.4.refs_2_, f32[128,128]{1,0:T(8,128)S(1)} %collective-permute-done.6.refs_3_, ...), custom_call_target="tpu_custom_call" | custom-call | flops 10000000 | bytes 1000000 | tf_op jit(solution)/shard_map/score/pallas_call | solution.py:317
  20.9 2.5 %collective-permute-start.8 = (f32[1,128]{1,0:T(1,128)S(1)}, f32[1,128]{1,0:T(1,128)S(1)}, u32[]{:S(2)}, u32[]{:S(2)}) collective-permute-start(f32[1,128]{1,0:T(1,128)S(1)} %get-tuple-element.22.refs_0_), channel_id=1, source_target_pairs={{0,5},{1,4},{2,7},{3,6},{4,1},{5,0},{6,3},{7,2},{8,13},{9,12},{10,... | collective-permute-start | bytes 1544 | tf_op jit(solution)/shard_map/ppermute | solution.py:487
  23.4 1.0 %collective-permute-start.7 = (f32[1,128]{1,0:T(1,128)S(1)}, f32[1,128]{1,0:T(1,128)S(1)}, u32[]{:S(2)}, u32[]{:S(2)}) collective-permute-start(f32[1,128]{1,0:T(1,128)S(1)} %get-tuple-element.22.refs_0_), channel_id=1, source_target_pairs={{0,7},{1,6},{2,5},{3,4},{4,3},{5,2},{6,1},{7,0},{8,15},{9,14},{10,... | collective-permute-start | bytes 1544 | tf_op jit(solution)/shard_map/ppermute | solution.py:487
  24.5 1.1 %collective-permute-done.8.refs_2_ = f32[1,128]{1,0:T(1,128)S(1)} collective-permute-done((f32[1,128]{1,0:T(1,128)S(1)}, f32[1,128]{1,0:T(1,128)S(1)}, u32[]{:S(2)}, u32[]{:S(2)}) %collective-permute-start.8) | collective-permute-done | bytes 544 | tf_op jit(solution)/shard_map/ppermute | solution.py:487
  25.6 2.6 %collective-permute-done.7.refs_1_ = f32[1,128]{1,0:T(1,128)S(1)} collective-permute-done((f32[1,128]{1,0:T(1,128)S(1)}, f32[1,128]{1,0:T(1,128)S(1)}, u32[]{:S(2)}, u32[]{:S(2)}) %collective-permute-start.7) | collective-permute-done | bytes 544 | tf_op jit(solution)/shard_map/ppermute | solution.py:487
  28.2 0.4 %row_grads_given.1 = f32[256,128]{1,0:T(8,128)S(1)} custom-call(f32[1,128]{1,0:T(1,128)S(1)} %get-tuple-element.22.refs_0_, f32[1,128]{1,0:T(1,128)S(1)} %collective-permute-done.7.refs_1_, f32[1,128]{1,0:T(1,128)S(1)} %collective-permute-done.8.refs_2_, f32[1,128]{1,0:T(1,128)S(1)} %collective-permute-done.9.refs_3_, ...), custom_call_target="tpu_custom_call" | custom-call | flops 100000000 | bytes 1000000 | tf_op jit(solution)/shard_map/row_grads_given/pallas_call | solution.py:398
  29.0 0.4 %row_grads_kept.1.kept_ref = f32[256,128]{1,0:T(8,128)S(1)} custom-call(f32[1,128]{1,0:T(1,128)S(1)} %get-tuple-element.22.refs_0_, f32[1,128]{1,0:T(1,128)S(1)} %collective-permute-done.7.refs_1_, f32[1,128]{1,0:T(1,128)S(1)} %collective-permute-done.8.refs_2_, f32[1,128]{1,0:T(1,128)S(1)} %collective-permute-done.9.refs_3_, ...), custom_call_target="tpu_custom_call" | custom-call | flops 100000000 | bytes 1000000 | tf_op jit(solution)/shard_map/row_grads_kept/pallas_call | solution.py:398
  29.4 0.6 %collective-permute-done.12.received_ref = f32[256,128]{1,0:T(8,128)S(1)} collective-permute-done((f32[256,128]{1,0:T(8,128)S(1)}, f32[256,128]{1,0:T(8,128)S(1)}, u32[]{:S(2)}, u32[]{:S(2)}) %collective-permute-start.12) | collective-permute-done | bytes 131104 | tf_op jit(solution)/shard_map/ppermute | solution.py:487
  30.1 1.5 %collective-permute-start.13 = (f32[64,128]{1,0:T(8,128)S(1)}, f32[64,128]{1,0:T(8,128)S(1)}, u32[]{:S(2)}, u32[]{:S(2)}) collective-permute-start(f32[64,128]{1,0:T(8,128)S(1)} %get-tuple-element.25), channel_id=1, source_target_pairs={{0,9},{1,8},{2,11},{3,10},{4,13},{5,12},{6,15},{7,14},{8,1},{9,0},... | collective-permute-start | bytes 98312 | tf_op jit(solution)/shard_map/ppermute | solution.py:487
  31.5 1.3 %collective-permute-start.14 = (f32[64,128]{1,0:T(8,128)S(1)}, f32[64,128]{1,0:T(8,128)S(1)}, u32[]{:S(2)}, u32[]{:S(2)}) collective-permute-start(f32[64,128]{1,0:T(8,128)S(1)} %get-tuple-element.26), channel_id=1, source_target_pairs={{0,17},{1,16},{2,19},{3,18},{4,21},{5,20},{6,23},{7,22},{8,25},{9,... | collective-permute-start | bytes 98312 | tf_op jit(solution)/shard_map/ppermute | solution.py:487
  32.9 0.4 %collective-permute-start.15 = (f32[64,128]{1,0:T(8,128)S(1)}, f32[64,128]{1,0:T(8,128)S(1)}, u32[]{:S(2)}, u32[]{:S(2)}) collective-permute-start(f32[64,128]{1,0:T(8,128)S(1)} %get-tuple-element.27), channel_id=1, source_target_pairs={{0,25},{1,24},{2,27},{3,26},{4,29},{5,28},{6,31},{7,30},{8,17},{9,... | collective-permute-start | bytes 98312 | tf_op jit(solution)/shard_map/ppermute | solution.py:487
  33.3 2.1 %finish_dense.1 = (bf16[128,1024]{1,0:T(8,128)(2,1)}, f32[128,128]{1,0:T(8,128)}, f32[1968,128]{1,0:T(8,128)}) custom-call(f32[128,128]{1,0:T(8,128)S(1)} %get-tuple-element.19.pooled_ref, bf16[128,128]{1,0:T(8,128)(2,1)S(1)} %copy-done.2, f32[128,1024]{1,0:T(8,128)S(1)} %linear_part.1.refs_5_.linear_ref, f32[1,1024]{1,0:T(1,128)S(1)} %copy-done.3, ...), custom_call_target="tpu_custom_call" | custom-call | flops 50000000 | bytes 1000000 | tf_op jit(solution)/shard_map/finish_dense/pallas_call | solution.py:356
  35.4 1.7 %collective-permute-done.15.refs_3_ = f32[64,128]{1,0:T(8,128)S(1)} collective-permute-done((f32[64,128]{1,0:T(8,128)S(1)}, f32[64,128]{1,0:T(8,128)S(1)}, u32[]{:S(2)}, u32[]{:S(2)}) %collective-permute-start.15) | collective-permute-done | bytes 32800 | tf_op jit(solution)/shard_map/ppermute | solution.py:487
  37.1 0.9 %place_rows.1 = f32[1968,128]{1,0:T(8,128)} custom-call(s32[4,32]{1,0:T(4,128)S(1)} %copy-done.4, f32[64,128]{1,0:T(8,128)S(1)} %get-tuple-element.24.refs_0_, f32[64,128]{1,0:T(8,128)S(1)} %collective-permute-done.13.refs_1_, f32[64,128]{1,0:T(8,128)S(1)} %collective-permute-done.14.refs_2_, ...), custom_call_target="tpu_custom_call", output_to_operand_aliasing={{}: (5, {})} | custom-call | flops 1000000 | bytes 2000000 | tf_op jit(solution)/shard_map/place_rows/pallas_call | solution.py:459
  (31 shorter events, 2.8 us)
Async XLA Ops:
  0.6 17.6 %copy-start.2 = (bf16[128,128]{1,0:T(8,128)(2,1)S(1)}, bf16[128,128]{1,0:T(8,128)(2,1)}, u32[]{:S(2)}) copy-start(bf16[128,128]{1,0:T(8,128)(2,1)} %bottom_ref.5) | copy-start | bytes 98308
  0.6 17.6 %copy-start.1 = (bf16[128,1024]{1,0:T(8,128)(2,1)S(1)}, bf16[128,1024]{1,0:T(8,128)(2,1)}, u32[]{:S(2)}) copy-start(bf16[128,1024]{1,0:T(8,128)(2,1)} %dense_ref.3) | copy-start | bytes 786436
  0.7 19.4 %copy-start = (f32[128,1024]{1,0:T(8,128)S(1)}, f32[128,1024]{1,0:T(8,128)}, u32[]{:S(2)}) copy-start(f32[128,1024]{1,0:T(8,128)} %cot_ref.1) | copy-start | bytes 1572868
  0.7 19.4 %copy-start.3 = (f32[1,1024]{1,0:T(1,128)S(1)}, f32[1,1024]{1,0:T(1,128)}, u32[]{:S(2)}) copy-start(f32[1,1024]{1,0:T(1,128)} %pairs_ref.1) | copy-start | bytes 12292
  2.5 34.6 %copy-start.4 = (s32[4,32]{1,0:T(4,128)S(1)}, s32[4,32]{1,0:T(4,128)}, u32[]{:S(2)}) copy-start(s32[4,32]{1,0:T(4,128)} %starts_ref.3) | copy-start | bytes 1540
  2.5 5.5 %collective-permute-start = (f32[256,128]{1,0:T(8,128)S(1)}, f32[256,128]{1,0:T(8,128)S(1)}, u32[]{:S(2)}, u32[]{:S(2)}) collective-permute-start(f32[256,128]{1,0:T(8,128)S(1)} %get-tuple-element.17.own_ref), channel_id=1, source_target_pairs={{0,1},{1,0},{2,3},{3,2},{4,5},{5,4},{6,7},{7,6},{8,9},{9,8},{10,11... | collective-permute-start | bytes 393224 | tf_op jit(solution)/shard_map/ppermute | solution.py:487
  3.1 10.6 %collective-permute-start.5 = (f32[136,128]{1,0:T(8,128)S(1)}, f32[136,128]{1,0:T(8,128)S(1)}, u32[]{:S(2)}, u32[]{:S(2)}) collective-permute-start(f32[136,128]{1,0:T(8,128)S(1)} %get-tuple-element.18.refs_8_), channel_id=1, source_target_pairs={{0,3},{1,2},{2,1},{3,0},{4,7},{5,6},{6,5},{7,4},{8,11},{9,10},{10,... | collective-permute-start | bytes 208904 | tf_op jit(solution)/shard_map/ppermute | solution.py:487
  5.8 4.9 %collective-permute-start.1 = (f32[8,128]{1,0:T(8,128)S(1)}, f32[8,128]{1,0:T(8,128)S(1)}, u32[]{:S(2)}, u32[]{:S(2)}) collective-permute-start(f32[8,128]{1,0:T(8,128)S(1)} %get-tuple-element.16.places_ref.refs_4_), channel_id=1, source_target_pairs={{0,7},{1,6},{2,5},{3,4},{4,3},{5,2},{6,1},{7,0},{8,15},{9,14},{10,... | collective-permute-start | bytes 12296 | tf_op jit(solution)/shard_map/ppermute | solution.py:487
  7.9 5.3 %collective-permute-start.3 = (f32[8,128]{1,0:T(8,128)S(1)}, f32[8,128]{1,0:T(8,128)S(1)}, u32[]{:S(2)}, u32[]{:S(2)}) collective-permute-start(f32[8,128]{1,0:T(8,128)S(1)} %get-tuple-element.16.places_ref.refs_4_), channel_id=1, source_target_pairs={{0,5},{1,4},{2,7},{3,6},{4,1},{5,0},{6,3},{7,2},{8,13},{9,12},{10,... | collective-permute-start | bytes 12296 | tf_op jit(solution)/shard_map/ppermute | solution.py:487
  11.0 7.8 %collective-permute-start.2 = (f32[128,128]{1,0:T(8,128)S(1)}, f32[128,128]{1,0:T(8,128)S(1)}, u32[]{:S(2)}, u32[]{:S(2)}) collective-permute-start(f32[128,128]{1,0:T(8,128)S(1)} %pool_rows.5), channel_id=1, source_target_pairs={{0,7},{1,6},{2,5},{3,4},{4,3},{5,2},{6,1},{7,0},{8,15},{9,14},{10,... | collective-permute-start | bytes 196616 | tf_op jit(solution)/shard_map/ppermute | solution.py:487
  13.6 6.5 %collective-permute-start.4 = (f32[128,128]{1,0:T(8,128)S(1)}, f32[128,128]{1,0:T(8,128)S(1)}, u32[]{:S(2)}, u32[]{:S(2)}) collective-permute-start(f32[128,128]{1,0:T(8,128)S(1)} %pool_rows.6), channel_id=1, source_target_pairs={{0,5},{1,4},{2,7},{3,6},{4,1},{5,0},{6,3},{7,2},{8,13},{9,12},{10,... | collective-permute-start | bytes 196616 | tf_op jit(solution)/shard_map/ppermute | solution.py:487
  14.1 6.0 %collective-permute-start.6 = (f32[128,128]{1,0:T(8,128)S(1)}, f32[128,128]{1,0:T(8,128)S(1)}, u32[]{:S(2)}, u32[]{:S(2)}) collective-permute-start(f32[128,128]{1,0:T(8,128)S(1)} %pool_rows.7), channel_id=1, source_target_pairs={{0,3},{1,2},{2,1},{3,0},{4,7},{5,6},{6,5},{7,4},{8,11},{9,10},{10,... | collective-permute-start | bytes 196616 | tf_op jit(solution)/shard_map/ppermute | solution.py:487
  15.8 8.7 %collective-permute-start.11 = (f32[128,128]{1,0:T(8,128)S(1)}, f32[128,128]{1,0:T(8,128)S(1)}, u32[]{:S(2)}, u32[]{:S(2)}) collective-permute-start(f32[128,128]{1,0:T(8,128)S(1)} %get-tuple-element.23), channel_id=1, source_target_pairs={{0,5},{1,4},{2,7},{3,6},{4,1},{5,0},{6,3},{7,2},{8,13},{9,12},{10,... | collective-permute-start | bytes 196616 | tf_op jit(solution)/shard_map/ppermute | solution.py:487
  16.8 7.6 %collective-permute-start.10 = (f32[128,128]{1,0:T(8,128)S(1)}, f32[128,128]{1,0:T(8,128)S(1)}, u32[]{:S(2)}, u32[]{:S(2)}) collective-permute-start(f32[128,128]{1,0:T(8,128)S(1)} %get-tuple-element.23), channel_id=1, source_target_pairs={{0,7},{1,6},{2,5},{3,4},{4,3},{5,2},{6,1},{7,0},{8,15},{9,14},{10,... | collective-permute-start | bytes 196616 | tf_op jit(solution)/shard_map/ppermute | solution.py:487
  20.5 3.9 %collective-permute-start.9 = (f32[1,128]{1,0:T(1,128)S(1)}, f32[1,128]{1,0:T(1,128)S(1)}, u32[]{:S(2)}, u32[]{:S(2)}) collective-permute-start(f32[1,128]{1,0:T(1,128)S(1)} %get-tuple-element.22.refs_0_), channel_id=1, source_target_pairs={{0,3},{1,2},{2,1},{3,0},{4,7},{5,6},{6,5},{7,4},{8,11},{9,10},{10,... | collective-permute-start | bytes 1544 | tf_op jit(solution)/shard_map/ppermute | solution.py:487
  20.9 4.6 %collective-permute-start.8 = (f32[1,128]{1,0:T(1,128)S(1)}, f32[1,128]{1,0:T(1,128)S(1)}, u32[]{:S(2)}, u32[]{:S(2)}) collective-permute-start(f32[1,128]{1,0:T(1,128)S(1)} %get-tuple-element.22.refs_0_), channel_id=1, source_target_pairs={{0,5},{1,4},{2,7},{3,6},{4,1},{5,0},{6,3},{7,2},{8,13},{9,12},{10,... | collective-permute-start | bytes 1544 | tf_op jit(solution)/shard_map/ppermute | solution.py:487
  23.4 4.8 %collective-permute-start.7 = (f32[1,128]{1,0:T(1,128)S(1)}, f32[1,128]{1,0:T(1,128)S(1)}, u32[]{:S(2)}, u32[]{:S(2)}) collective-permute-start(f32[1,128]{1,0:T(1,128)S(1)} %get-tuple-element.22.refs_0_), channel_id=1, source_target_pairs={{0,7},{1,6},{2,5},{3,4},{4,3},{5,2},{6,1},{7,0},{8,15},{9,14},{10,... | collective-permute-start | bytes 1544 | tf_op jit(solution)/shard_map/ppermute | solution.py:487
  28.6 1.4 %collective-permute-start.12 = (f32[256,128]{1,0:T(8,128)S(1)}, f32[256,128]{1,0:T(8,128)S(1)}, u32[]{:S(2)}, u32[]{:S(2)}) collective-permute-start(f32[256,128]{1,0:T(8,128)S(1)} %row_grads_given.1), channel_id=1, source_target_pairs={{0,1},{1,0},{2,3},{3,2},{4,5},{5,4},{6,7},{7,6},{8,9},{9,8},{10,11... | collective-permute-start | bytes 393224 | tf_op jit(solution)/shard_map/ppermute | solution.py:487
  30.1 5.3 %collective-permute-start.13 = (f32[64,128]{1,0:T(8,128)S(1)}, f32[64,128]{1,0:T(8,128)S(1)}, u32[]{:S(2)}, u32[]{:S(2)}) collective-permute-start(f32[64,128]{1,0:T(8,128)S(1)} %get-tuple-element.25), channel_id=1, source_target_pairs={{0,9},{1,8},{2,11},{3,10},{4,13},{5,12},{6,15},{7,14},{8,1},{9,0},... | collective-permute-start | bytes 98312 | tf_op jit(solution)/shard_map/ppermute | solution.py:487
  31.5 3.9 %collective-permute-start.14 = (f32[64,128]{1,0:T(8,128)S(1)}, f32[64,128]{1,0:T(8,128)S(1)}, u32[]{:S(2)}, u32[]{:S(2)}) collective-permute-start(f32[64,128]{1,0:T(8,128)S(1)} %get-tuple-element.26), channel_id=1, source_target_pairs={{0,17},{1,16},{2,19},{3,18},{4,21},{5,20},{6,23},{7,22},{8,25},{9,... | collective-permute-start | bytes 98312 | tf_op jit(solution)/shard_map/ppermute | solution.py:487
  32.9 4.2 %collective-permute-start.15 = (f32[64,128]{1,0:T(8,128)S(1)}, f32[64,128]{1,0:T(8,128)S(1)}, u32[]{:S(2)}, u32[]{:S(2)}) collective-permute-start(f32[64,128]{1,0:T(8,128)S(1)} %get-tuple-element.27), channel_id=1, source_target_pairs={{0,25},{1,24},{2,27},{3,26},{4,29},{5,28},{6,31},{7,30},{8,17},{9,... | collective-permute-start | bytes 98312 | tf_op jit(solution)/shard_map/ppermute | solution.py:487

commit v8 on v7

--- a/solution.py
+++ b/solution.py
@@ -369,27 +369,51 @@
     )(pooled, bottom_out, linear, top_pairs, cotangent, top_dense)
 
 
-def row_grads(scores, places, wides, bag, group_count, kept):
+def count_grads(places, bag, group_count):
+    samples = places[0].shape[1]
+    count = len(places)
+    held_rows = group_count * HOT
+
+    def kernel(*refs):
+        place_refs, out_refs = refs[:count], refs[count:]
+        grp_pos = lax.axis_index("grp")
+        shard_pos = lax.axis_index("shard")
+        for kept, out_ref in enumerate(out_refs):
+            ids = []
+            for step in range(group_count):
+                holder = shard_pos if (kept == 1) == (step == 0) else jnp.bitwise_xor(shard_pos, 1)
+                first = (holder * group_count + jnp.bitwise_xor(grp_pos, step)) * HOT
+                ids.append(lax.broadcasted_iota(jnp.int32, (HOT, samples), 0) + first)
+            rows = jnp.concatenate(ids, axis=0).astype(jnp.float32)
+            for place, ref in enumerate(place_refs):
+                times = jnp.zeros(rows.shape, jnp.float32)
+                for slot in range(bag):
+                    times += jnp.where(ref[pl.ds(slot, 1), :] == rows, 1.0, 0.0)
+                out_ref[:, pl.ds(place * samples, samples)] = times
+
+    part = jax.ShapeDtypeStruct((held_rows, count * samples), jnp.float32)
+    return pl.pallas_call(
+        kernel,
+        out_shape=(part, part),
+        in_specs=[whole()] * count,
+        out_specs=(whole(),) * 2,
+        cost_estimate=cost(1e7, 1e6),
+        compiler_params=pltpu.CompilerParams(vmem_limit_bytes=GRANT),
+        name="count_grads",
+    )(*places)
+
+
+def row_grads(times, scores, wides):
     samples = scores[0].shape[1]
     width = wides[0].shape[1]
     count = len(scores)
 
-    def kernel(*refs):
-        score_refs, place_refs, wide_refs = refs[:count], refs[count : 2 * count], refs[2 * count : -1]
-        grp_pos = lax.axis_index("grp")
-        shard_pos = lax.axis_index("shard")
-        ids = []
-        for step in range(group_count):
-            holder = shard_pos if kept == (step == 0) else jnp.bitwise_xor(shard_pos, 1)
-            first = (holder * group_count + jnp.bitwise_xor(grp_pos, step)) * HOT
-            ids.append(lax.broadcasted_iota(jnp.int32, (HOT, samples), 0) + first)
-        rows = jnp.concatenate(ids, axis=0).astype(jnp.float32)
-        total = jnp.zeros((group_count * HOT, width), jnp.float32)
-        for score_ref, place_ref, wide_ref in zip(score_refs, place_refs, wide_refs):
-            times = jnp.zeros(rows.shape, jnp.float32)
-            for slot in range(bag):
-                times += jnp.where(place_ref[pl.ds(slot, 1), :] == rows, 1.0, 0.0)
-            high, low = two_terms(times * score_ref[...])
+    def kernel(times_ref, *refs):
+        score_refs, wide_refs = refs[:count], refs[count:-1]
+        total = jnp.zeros((times_ref.shape[0], width), jnp.float32)
+        for place, (score_ref, wide_ref) in enumerate(zip(score_refs, wide_refs)):
+            weights = times_ref[:, pl.ds(place * samples, samples)] * score_ref[...]
+            high, low = two_terms(weights)
             bottom = wide_ref[pl.ds(wide_ref.shape[0] - samples, samples), :].astype(jnp.bfloat16)
             total += jnp.dot(high, bottom, preferred_element_type=jnp.float32)
             total += jnp.dot(low, bottom, preferred_element_type=jnp.float32)
@@ -397,13 +421,13 @@
 
     return pl.pallas_call(
         kernel,
-        out_shape=jax.ShapeDtypeStruct((group_count * HOT, width), jnp.float32),
-        in_specs=[whole()] * (3 * count),
+        out_shape=jax.ShapeDtypeStruct((times.shape[0], width), jnp.float32),
+        in_specs=[whole()] * (1 + 2 * count),
         out_specs=whole(),
         cost_estimate=cost(1e8, 1e6),
         compiler_params=pltpu.CompilerParams(vmem_limit_bytes=GRANT),
-        name="row_grads_kept" if kept else "row_grads_given",
-    )(*scores, *places, *wides)
+        name="row_grads",
+    )(times, *scores, *wides)
 
 
 def split_owners(kept, received, group_count):
@@ -472,6 +496,10 @@
     )(starts, *blocks, blank)
 
 
+def far_steps(shard_count):
+    return [2 * chips + chips % 2 for chips in range(shard_count // 2 - 1, 1, -1)]
+
+
 def by_hot_rows(bottom_out, lookups, starts, tables, top_dense, top_pairs, cotangent):
     group_count = lax.axis_size("grp")
     shard_count = lax.axis_size("shard")
@@ -486,8 +514,7 @@
         ]
         return lax.ppermute(values, ("grp", "shard"), pairs)
 
-    near = 3
-    steps = list(range(shard_count - 1, near, -2))
+    near, steps = 3, far_steps(shard_count)
     looked = lookups[:, 0, :].T
     hot_own, places_own, near_own, wide_own = load_first(
         starts, looked, bottom_out, tables[0], group_count
@@ -510,9 +537,10 @@
     )
     places = [places_own] + places + [near_back]
     wides = [near_own] + wides + [near_back]
-    given = row_grads(scores, places, wides, bag, group_count, False)
+    times_given, times_kept = count_grads(places, bag, group_count)
+    given = row_grads(times_given, scores, wides)
     received = across(given, 0, 1)
-    kept = row_grads(scores, places, wides, bag, group_count, True)
+    kept = row_grads(times_kept, scores, wides)
     owned = split_owners(kept, received, group_count)
     blocks = [owned[0]] + [across(owned[step], step, 1) for step in range(1, group_count)]
     table_grad = place_rows(starts, blocks, blank)

time: 38.2 us -> 38 us (level)
  waiting for transfers between devices: 9.83 us -> 7.41 us
  starting transfers between devices: 19.5 us -> 21.6 us
    ppermute x16, waiting for transfers between devices: 9.83 us -> 7.41 us  [across(): return lax.ppermute(values, ('grp', 'shard'), pairs)]
    ppermute x16, starting transfers between devices: 19.5 us -> 21.6 us  [across(): return lax.ppermute(values, ('grp', 'shard'), pairs)]
    pallas_call x2 -> x3, Pallas kernels: 0.85 us -> 0.97 us  [the longest x2 0.58 us: row_grads(): pl.pallas_call(kernel, out_shape=jax.ShapeDtypeStruct((times.shape[0], wi...]
  transfers between devices with their start and end apart: 16 -> 16, of which waited for: 6 -> 6; matrix products, arithmetic and copies ran while one was open for 0% -> 0% of each run, Pallas kernels for 12% -> 13%
where the time goes in v8:
time: 38 us; the launch traced here: 37.8 us
  starting transfers between devices  21.6 us (57%)
  Pallas kernels  8 us (21%)
  waiting for transfers between devices  7.41 us (20%)
  between operations  0.81 us (2%)
    ppermute x16, starting transfers between devices, across(): return lax.ppermute(values, ('grp', 'shard'), pairs)  21.6 us
    ppermute x16, waiting for transfers between devices, across(): return lax.ppermute(values, ('grp', 'shard'), pairs)  7.41 us
    pallas_call x1, Pallas kernels, finish_dense(): pl.pallas_call(kernel, out_shape=(jax.ShapeDtypeStruct((samples, hidden),...  2.12 us
    pallas_call x1, Pallas kernels, load_first(): pl.pallas_call(kernel, out_shape=(jax.ShapeDtypeStruct((group_count * HOT...  1.84 us
    pallas_call x4, Pallas kernels, pool_rows(): pl.pallas_call(kernel, out_shape=jax.ShapeDtypeStruct((samples, width), j...  1.52 us
    pallas_call x1, Pallas kernels, place_rows(): pl.pallas_call(kernel, out_shape=jax.ShapeDtypeStruct((win_size, width),...  0.87 us
  transfers between devices with their start and end apart: 16, of which 6 were waited for; matrix products, arithmetic and copies ran while one was open for 0% of the time, Pallas kernels for 13%

profile of v8, /device:TPU:0, one launch (start us, length us, event | category | flops | bytes accessed | tf_op | source)
XLA Modules:
  0.0 37.8 jit_solution(12937222730198613103)
XLA Ops:
  0.7 1.8 %load_first.1 = (f32[256,128]{1,0:T(8,128)S(1)}, f32[8,128]{1,0:T(8,128)S(1)}, f32[136,128]{1,0:T(8,128)S(1)}, f32[128,128]{1,0:T(8,128)S(1)}) custom-call(s32[4,32]{1,0:T(4,128)} %starts_ref.3, s32[4,128]{1,0:T(4,128)} %bitcast.7, bf16[128,128]{1,0:T(8,128)(2,1)} %bottom_ref.5, f32[7872,128]{1,0:T(8,128)} %bitcast.5), custom_call_target="tpu_custom_call" | custom-call | flops 1000000 | bytes 1000000 | tf_op jit(solution)/shard_map/load_first/pallas_call | solution.py:199
  2.5 0.6 %collective-permute-start = (f32[256,128]{1,0:T(8,128)S(1)}, f32[256,128]{1,0:T(8,128)S(1)}, u32[]{:S(2)}, u32[]{:S(2)}) collective-permute-start(f32[256,128]{1,0:T(8,128)S(1)} %get-tuple-element.19.own_ref), channel_id=1, source_target_pairs={{0,1},{1,0},{2,3},{3,2},{4,5},{5,4},{6,7},{7,6},{8,9},{9,8},{10,11... | collective-permute-start | bytes 393224 | tf_op jit(solution)/shard_map/ppermute | solution.py:515
  3.1 2.7 %collective-permute-start.5 = (f32[136,128]{1,0:T(8,128)S(1)}, f32[136,128]{1,0:T(8,128)S(1)}, u32[]{:S(2)}, u32[]{:S(2)}) collective-permute-start(f32[136,128]{1,0:T(8,128)S(1)} %get-tuple-element.20.refs_4_), channel_id=1, source_target_pairs={{0,3},{1,2},{2,1},{3,0},{4,7},{5,6},{6,5},{7,4},{8,11},{9,10},{10,... | collective-permute-start | bytes 208904 | tf_op jit(solution)/shard_map/ppermute | solution.py:515
  5.8 2.6 %collective-permute-start.3 = (f32[8,128]{1,0:T(8,128)S(1)}, f32[8,128]{1,0:T(8,128)S(1)}, u32[]{:S(2)}, u32[]{:S(2)}) collective-permute-start(f32[8,128]{1,0:T(8,128)S(1)} %get-tuple-element.18.places_ref.refs_0_), channel_id=1, source_target_pairs={{0,4},{1,5},{2,6},{3,7},{4,0},{5,1},{6,2},{7,3},{8,12},{9,13},{10,... | collective-permute-start | bytes 12296 | tf_op jit(solution)/shard_map/ppermute | solution.py:515
  8.4 0.4 %pool_rows.7 = f32[128,128]{1,0:T(8,128)S(1)} custom-call(f32[136,128]{1,0:T(8,128)S(1)} %collective-permute-done.5.places_ref.refs_3_.refs_7_, bf16[512,256]{1,0:T(8,128)(2,1)S(1)} %hot_terms.1.terms_ref), custom_call_target="tpu_custom_call" | custom-call | flops 50000000 | bytes 1000000 | tf_op jit(solution)/shard_map/pool_rows/pallas_call | solution.py:282
  8.8 1.3 %collective-permute-start.6 = (f32[128,128]{1,0:T(8,128)S(1)}, f32[128,128]{1,0:T(8,128)S(1)}, u32[]{:S(2)}, u32[]{:S(2)}) collective-permute-start(f32[128,128]{1,0:T(8,128)S(1)} %pool_rows.7), channel_id=1, source_target_pairs={{0,3},{1,2},{2,1},{3,0},{4,7},{5,6},{6,5},{7,4},{8,11},{9,10},{10,... | collective-permute-start | bytes 196616 | tf_op jit(solution)/shard_map/ppermute | solution.py:515
  10.3 0.4 %pool_rows.6 = f32[128,128]{1,0:T(8,128)S(1)} custom-call(f32[8,128]{1,0:T(8,128)S(1)} %collective-permute-done.3.places_ref.refs_2_, bf16[512,256]{1,0:T(8,128)(2,1)S(1)} %hot_terms.1.terms_ref), custom_call_target="tpu_custom_call" | custom-call | flops 50000000 | bytes 1000000 | tf_op jit(solution)/shard_map/pool_rows/pallas_call | solution.py:282
  10.7 2.8 %collective-permute-start.4 = (f32[128,128]{1,0:T(8,128)S(1)}, f32[128,128]{1,0:T(8,128)S(1)}, u32[]{:S(2)}, u32[]{:S(2)}) collective-permute-start(f32[128,128]{1,0:T(8,128)S(1)} %pool_rows.6), channel_id=1, source_target_pairs={{0,4},{1,5},{2,6},{3,7},{4,0},{5,1},{6,2},{7,3},{8,12},{9,13},{10,... | collective-permute-start | bytes 196616 | tf_op jit(solution)/shard_map/ppermute | solution.py:515
  13.4 0.4 %pool_rows.5 = f32[128,128]{1,0:T(8,128)S(1)} custom-call(f32[8,128]{1,0:T(8,128)S(1)} %collective-permute-done.1.places_ref.refs_1_, bf16[512,256]{1,0:T(8,128)(2,1)S(1)} %hot_terms.1.terms_ref), custom_call_target="tpu_custom_call" | custom-call | flops 50000000 | bytes 1000000 | tf_op jit(solution)/shard_map/pool_rows/pallas_call | solution.py:282
  13.9 3.5 %collective-permute-start.10 = (f32[128,128]{1,0:T(8,128)S(1)}, f32[128,128]{1,0:T(8,128)S(1)}, u32[]{:S(2)}, u32[]{:S(2)}) collective-permute-start(f32[128,128]{1,0:T(8,128)S(1)} %get-tuple-element.26), channel_id=1, source_target_pairs={{0,7},{1,6},{2,5},{3,4},{4,3},{5,2},{6,1},{7,0},{8,15},{9,14},{10,... | collective-permute-start | bytes 196616 | tf_op jit(solution)/shard_map/ppermute | solution.py:515
  17.6 0.4 %pool_rows.4.refs_0_ = f32[128,128]{1,0:T(8,128)S(1)} custom-call(f32[8,128]{1,0:T(8,128)S(1)} %get-tuple-element.18.places_ref.refs_0_, bf16[512,256]{1,0:T(8,128)(2,1)S(1)} %hot_terms.1.terms_ref), custom_call_target="tpu_custom_call" | custom-call | flops 50000000 | bytes 1000000 | tf_op jit(solution)/shard_map/pool_rows/pallas_call | solution.py:282
  18.0 2.1 %collective-permute-done.2.refs_1_ = f32[128,128]{1,0:T(8,128)S(1)} collective-permute-done((f32[128,128]{1,0:T(8,128)S(1)}, f32[128,128]{1,0:T(8,128)S(1)}, u32[]{:S(2)}, u32[]{:S(2)}) %collective-permute-start.2) | collective-permute-done | bytes 65568 | tf_op jit(solution)/shard_map/ppermute | solution.py:515
  20.1 0.4 %score.1 = (f32[1,128]{1,0:T(1,128)S(1)}, f32[128,128]{1,0:T(8,128)S(1)}) custom-call(f32[128,128]{1,0:T(8,128)S(1)} %pool_rows.4.refs_0_, f32[128,128]{1,0:T(8,128)S(1)} %collective-permute-done.2.refs_1_, f32[128,128]{1,0:T(8,128)S(1)} %collective-permute-done.4.refs_2_, f32[128,128]{1,0:T(8,128)S(1)} %collective-permute-done.6.refs_3_, ...), custom_call_target="tpu_custom_call" | custom-call | flops 10000000 | bytes 1000000 | tf_op jit(solution)/shard_map/score/pallas_call | solution.py:317
  20.9 4.3 %collective-permute-start.8 = (f32[1,128]{1,0:T(1,128)S(1)}, f32[1,128]{1,0:T(1,128)S(1)}, u32[]{:S(2)}, u32[]{:S(2)}) collective-permute-start(f32[1,128]{1,0:T(1,128)S(1)} %get-tuple-element.25.refs_0_), channel_id=1, source_target_pairs={{0,4},{1,5},{2,6},{3,7},{4,0},{5,1},{6,2},{7,3},{8,12},{9,13},{10,... | collective-permute-start | bytes 1544 | tf_op jit(solution)/shard_map/ppermute | solution.py:515
  25.2 0.4 %count_grads.1 = (f32[256,512]{1,0:T(8,128)S(1)}, f32[256,512]{1,0:T(8,128)S(1)}) custom-call(f32[8,128]{1,0:T(8,128)S(1)} %get-tuple-element.18.places_ref.refs_0_, f32[8,128]{1,0:T(8,128)S(1)} %collective-permute-done.1.places_ref.refs_1_, f32[8,128]{1,0:T(8,128)S(1)} %collective-permute-done.3.places_ref.refs_2_, ...), custom_call_target="tpu_custom_call" | custom-call | flops 10000000 | bytes 1000000 | tf_op jit(solution)/shard_map/count_grads/pallas_call | solution.py:395
  25.7 1.1 %collective-permute-done.8.refs_2_ = f32[1,128]{1,0:T(1,128)S(1)} collective-permute-done((f32[1,128]{1,0:T(1,128)S(1)}, f32[1,128]{1,0:T(1,128)S(1)}, u32[]{:S(2)}, u32[]{:S(2)}) %collective-permute-start.8) | collective-permute-done | bytes 544 | tf_op jit(solution)/shard_map/ppermute | solution.py:515
  26.8 1.4 %collective-permute-done.9.refs_3_ = f32[1,128]{1,0:T(1,128)S(1)} collective-permute-done((f32[1,128]{1,0:T(1,128)S(1)}, f32[1,128]{1,0:T(1,128)S(1)}, u32[]{:S(2)}, u32[]{:S(2)}) %collective-permute-start.9) | collective-permute-done | bytes 544 | tf_op jit(solution)/shard_map/ppermute | solution.py:515
  29.1 0.8 %collective-permute-done.12.received_ref = f32[256,128]{1,0:T(8,128)S(1)} collective-permute-done((f32[256,128]{1,0:T(8,128)S(1)}, f32[256,128]{1,0:T(8,128)S(1)}, u32[]{:S(2)}, u32[]{:S(2)}) %collective-permute-start.12) | collective-permute-done | bytes 131104 | tf_op jit(solution)/shard_map/ppermute | solution.py:515
  30.0 1.4 %collective-permute-start.13 = (f32[64,128]{1,0:T(8,128)S(1)}, f32[64,128]{1,0:T(8,128)S(1)}, u32[]{:S(2)}, u32[]{:S(2)}) collective-permute-start(f32[64,128]{1,0:T(8,128)S(1)} %get-tuple-element.29), channel_id=1, source_target_pairs={{0,9},{1,8},{2,11},{3,10},{4,13},{5,12},{6,15},{7,14},{8,1},{9,0},... | collective-permute-start | bytes 98312 | tf_op jit(solution)/shard_map/ppermute | solution.py:515
  31.4 1.3 %collective-permute-start.14 = (f32[64,128]{1,0:T(8,128)S(1)}, f32[64,128]{1,0:T(8,128)S(1)}, u32[]{:S(2)}, u32[]{:S(2)}) collective-permute-start(f32[64,128]{1,0:T(8,128)S(1)} %get-tuple-element.30), channel_id=1, source_target_pairs={{0,17},{1,16},{2,19},{3,18},{4,21},{5,20},{6,23},{7,22},{8,25},{9,... | collective-permute-start | bytes 98312 | tf_op jit(solution)/shard_map/ppermute | solution.py:515
  32.7 0.4 %collective-permute-start.15 = (f32[64,128]{1,0:T(8,128)S(1)}, f32[64,128]{1,0:T(8,128)S(1)}, u32[]{:S(2)}, u32[]{:S(2)}) collective-permute-start(f32[64,128]{1,0:T(8,128)S(1)} %get-tuple-element.31), channel_id=1, source_target_pairs={{0,25},{1,24},{2,27},{3,26},{4,29},{5,28},{6,31},{7,30},{8,17},{9,... | collective-permute-start | bytes 98312 | tf_op jit(solution)/shard_map/ppermute | solution.py:515
  33.1 2.1 %finish_dense.1 = (bf16[128,1024]{1,0:T(8,128)(2,1)}, f32[128,128]{1,0:T(8,128)}, f32[1968,128]{1,0:T(8,128)}) custom-call(f32[128,128]{1,0:T(8,128)S(1)} %get-tuple-element.21.pooled_ref, bf16[128,128]{1,0:T(8,128)(2,1)S(1)} %copy-done.2, f32[128,1024]{1,0:T(8,128)S(1)} %linear_part.1.refs_5_.linear_ref, f32[1,1024]{1,0:T(1,128)S(1)} %copy-done.3, ...), custom_call_target="tpu_custom_call" | custom-call | flops 50000000 | bytes 1000000 | tf_op jit(solution)/shard_map/finish_dense/pallas_call | solution.py:356
  35.2 1.7 %collective-permute-done.15.refs_3_ = f32[64,128]{1,0:T(8,128)S(1)} collective-permute-done((f32[64,128]{1,0:T(8,128)S(1)}, f32[64,128]{1,0:T(8,128)S(1)}, u32[]{:S(2)}, u32[]{:S(2)}) %collective-permute-start.15) | collective-permute-done | bytes 32800 | tf_op jit(solution)/shard_map/ppermute | solution.py:515
  36.9 0.9 %place_rows.1 = f32[1968,128]{1,0:T(8,128)} custom-call(s32[4,32]{1,0:T(4,128)S(1)} %copy-done.4, f32[64,128]{1,0:T(8,128)S(1)} %get-tuple-element.28.refs_0_, f32[64,128]{1,0:T(8,128)S(1)} %collective-permute-done.13.refs_1_, f32[64,128]{1,0:T(8,128)S(1)} %collective-permute-done.14.refs_2_, ...), custom_call_target="tpu_custom_call", output_to_operand_aliasing={{}: (5, {})} | custom-call | flops 1000000 | bytes 2000000 | tf_op jit(solution)/shard_map/place_rows/pallas_call | solution.py:483
  (32 shorter events, 1.8 us)
Async XLA Ops:
  0.6 16.8 %copy-start.2 = (bf16[128,128]{1,0:T(8,128)(2,1)S(1)}, bf16[128,128]{1,0:T(8,128)(2,1)}, u32[]{:S(2)}) copy-start(bf16[128,128]{1,0:T(8,128)(2,1)} %bottom_ref.5) | copy-start | bytes 98308
  0.6 16.8 %copy-start.1 = (bf16[128,1024]{1,0:T(8,128)(2,1)S(1)}, bf16[128,1024]{1,0:T(8,128)(2,1)}, u32[]{:S(2)}) copy-start(bf16[128,1024]{1,0:T(8,128)(2,1)} %dense_ref.3) | copy-start | bytes 786436
  0.7 19.5 %copy-start.3 = (f32[1,1024]{1,0:T(1,128)S(1)}, f32[1,1024]{1,0:T(1,128)}, u32[]{:S(2)}) copy-start(f32[1,1024]{1,0:T(1,128)} %pairs_ref.1) | copy-start | bytes 12292
  0.7 19.5 %copy-start = (f32[128,1024]{1,0:T(8,128)S(1)}, f32[128,1024]{1,0:T(8,128)}, u32[]{:S(2)}) copy-start(f32[128,1024]{1,0:T(8,128)} %cot_ref.1) | copy-start | bytes 1572868
  2.5 34.4 %copy-start.4 = (s32[4,32]{1,0:T(4,128)S(1)}, s32[4,32]{1,0:T(4,128)}, u32[]{:S(2)}) copy-start(s32[4,32]{1,0:T(4,128)} %starts_ref.3) | copy-start | bytes 1540
  2.5 5.8 %collective-permute-start = (f32[256,128]{1,0:T(8,128)S(1)}, f32[256,128]{1,0:T(8,128)S(1)}, u32[]{:S(2)}, u32[]{:S(2)}) collective-permute-start(f32[256,128]{1,0:T(8,128)S(1)} %get-tuple-element.19.own_ref), channel_id=1, source_target_pairs={{0,1},{1,0},{2,3},{3,2},{4,5},{5,4},{6,7},{7,6},{8,9},{9,8},{10,11... | collective-permute-start | bytes 393224 | tf_op jit(solution)/shard_map/ppermute | solution.py:515
  3.1 5.3 %collective-permute-start.5 = (f32[136,128]{1,0:T(8,128)S(1)}, f32[136,128]{1,0:T(8,128)S(1)}, u32[]{:S(2)}, u32[]{:S(2)}) collective-permute-start(f32[136,128]{1,0:T(8,128)S(1)} %get-tuple-element.20.refs_4_), channel_id=1, source_target_pairs={{0,3},{1,2},{2,1},{3,0},{4,7},{5,6},{6,5},{7,4},{8,11},{9,10},{10,... | collective-permute-start | bytes 208904 | tf_op jit(solution)/shard_map/ppermute | solution.py:515
  5.8 4.5 %collective-permute-start.3 = (f32[8,128]{1,0:T(8,128)S(1)}, f32[8,128]{1,0:T(8,128)S(1)}, u32[]{:S(2)}, u32[]{:S(2)}) collective-permute-start(f32[8,128]{1,0:T(8,128)S(1)} %get-tuple-element.18.places_ref.refs_0_), channel_id=1, source_target_pairs={{0,4},{1,5},{2,6},{3,7},{4,0},{5,1},{6,2},{7,3},{8,12},{9,13},{10,... | collective-permute-start | bytes 12296 | tf_op jit(solution)/shard_map/ppermute | solution.py:515
  8.4 5.1 %collective-permute-start.1 = (f32[8,128]{1,0:T(8,128)S(1)}, f32[8,128]{1,0:T(8,128)S(1)}, u32[]{:S(2)}, u32[]{:S(2)}) collective-permute-start(f32[8,128]{1,0:T(8,128)S(1)} %get-tuple-element.18.places_ref.refs_0_), channel_id=1, source_target_pairs={{0,7},{1,6},{2,5},{3,4},{4,3},{5,2},{6,1},{7,0},{8,15},{9,14},{10,... | collective-permute-start | bytes 12296 | tf_op jit(solution)/shard_map/ppermute | solution.py:515
  8.8 9.2 %collective-permute-start.6 = (f32[128,128]{1,0:T(8,128)S(1)}, f32[128,128]{1,0:T(8,128)S(1)}, u32[]{:S(2)}, u32[]{:S(2)}) collective-permute-start(f32[128,128]{1,0:T(8,128)S(1)} %pool_rows.7), channel_id=1, source_target_pairs={{0,3},{1,2},{2,1},{3,0},{4,7},{5,6},{6,5},{7,4},{8,11},{9,10},{10,... | collective-permute-start | bytes 196616 | tf_op jit(solution)/shard_map/ppermute | solution.py:515
  10.7 7.4 %collective-permute-start.4 = (f32[128,128]{1,0:T(8,128)S(1)}, f32[128,128]{1,0:T(8,128)S(1)}, u32[]{:S(2)}, u32[]{:S(2)}) collective-permute-start(f32[128,128]{1,0:T(8,128)S(1)} %pool_rows.6), channel_id=1, source_target_pairs={{0,4},{1,5},{2,6},{3,7},{4,0},{5,1},{6,2},{7,3},{8,12},{9,13},{10,... | collective-permute-start | bytes 196616 | tf_op jit(solution)/shard_map/ppermute | solution.py:515
  13.8 6.3 %collective-permute-start.2 = (f32[128,128]{1,0:T(8,128)S(1)}, f32[128,128]{1,0:T(8,128)S(1)}, u32[]{:S(2)}, u32[]{:S(2)}) collective-permute-start(f32[128,128]{1,0:T(8,128)S(1)} %pool_rows.5), channel_id=1, source_target_pairs={{0,7},{1,6},{2,5},{3,4},{4,3},{5,2},{6,1},{7,0},{8,15},{9,14},{10,... | collective-permute-start | bytes 196616 | tf_op jit(solution)/shard_map/ppermute | solution.py:515
  13.9 11.8 %collective-permute-start.10 = (f32[128,128]{1,0:T(8,128)S(1)}, f32[128,128]{1,0:T(8,128)S(1)}, u32[]{:S(2)}, u32[]{:S(2)}) collective-permute-start(f32[128,128]{1,0:T(8,128)S(1)} %get-tuple-element.26), channel_id=1, source_target_pairs={{0,7},{1,6},{2,5},{3,4},{4,3},{5,2},{6,1},{7,0},{8,15},{9,14},{10,... | collective-permute-start | bytes 196616 | tf_op jit(solution)/shard_map/ppermute | solution.py:515
  17.4 8.2 %collective-permute-start.11 = (f32[128,128]{1,0:T(8,128)S(1)}, f32[128,128]{1,0:T(8,128)S(1)}, u32[]{:S(2)}, u32[]{:S(2)}) collective-permute-start(f32[128,128]{1,0:T(8,128)S(1)} %get-tuple-element.26), channel_id=1, source_target_pairs={{0,4},{1,5},{2,6},{3,7},{4,0},{5,1},{6,2},{7,3},{8,12},{9,13},{10,... | collective-permute-start | bytes 196616 | tf_op jit(solution)/shard_map/ppermute | solution.py:515
  20.6 5.1 %collective-permute-start.7 = (f32[1,128]{1,0:T(1,128)S(1)}, f32[1,128]{1,0:T(1,128)S(1)}, u32[]{:S(2)}, u32[]{:S(2)}) collective-permute-start(f32[1,128]{1,0:T(1,128)S(1)} %get-tuple-element.25.refs_0_), channel_id=1, source_target_pairs={{0,7},{1,6},{2,5},{3,4},{4,3},{5,2},{6,1},{7,0},{8,15},{9,14},{10,... | collective-permute-start | bytes 1544 | tf_op jit(solution)/shard_map/ppermute | solution.py:515
  20.9 5.9 %collective-permute-start.8 = (f32[1,128]{1,0:T(1,128)S(1)}, f32[1,128]{1,0:T(1,128)S(1)}, u32[]{:S(2)}, u32[]{:S(2)}) collective-permute-start(f32[1,128]{1,0:T(1,128)S(1)} %get-tuple-element.25.refs_0_), channel_id=1, source_target_pairs={{0,4},{1,5},{2,6},{3,7},{4,0},{5,1},{6,2},{7,3},{8,12},{9,13},{10,... | collective-permute-start | bytes 1544 | tf_op jit(solution)/shard_map/ppermute | solution.py:515
  25.2 3.0 %collective-permute-start.9 = (f32[1,128]{1,0:T(1,128)S(1)}, f32[1,128]{1,0:T(1,128)S(1)}, u32[]{:S(2)}, u32[]{:S(2)}) collective-permute-start(f32[1,128]{1,0:T(1,128)S(1)} %get-tuple-element.25.refs_0_), channel_id=1, source_target_pairs={{0,3},{1,2},{2,1},{3,0},{4,7},{5,6},{6,5},{7,4},{8,11},{9,10},{10,... | collective-permute-start | bytes 1544 | tf_op jit(solution)/shard_map/ppermute | solution.py:515
  28.5 1.4 %collective-permute-start.12 = (f32[256,128]{1,0:T(8,128)S(1)}, f32[256,128]{1,0:T(8,128)S(1)}, u32[]{:S(2)}, u32[]{:S(2)}) collective-permute-start(f32[256,128]{1,0:T(8,128)S(1)} %row_grads.3), channel_id=1, source_target_pairs={{0,1},{1,0},{2,3},{3,2},{4,5},{5,4},{6,7},{7,6},{8,9},{9,8},{10,11... | collective-permute-start | bytes 393224 | tf_op jit(solution)/shard_map/ppermute | solution.py:515
  30.0 5.2 %collective-permute-start.13 = (f32[64,128]{1,0:T(8,128)S(1)}, f32[64,128]{1,0:T(8,128)S(1)}, u32[]{:S(2)}, u32[]{:S(2)}) collective-permute-start(f32[64,128]{1,0:T(8,128)S(1)} %get-tuple-element.29), channel_id=1, source_target_pairs={{0,9},{1,8},{2,11},{3,10},{4,13},{5,12},{6,15},{7,14},{8,1},{9,0},... | collective-permute-start | bytes 98312 | tf_op jit(solution)/shard_map/ppermute | solution.py:515
  31.4 3.9 %collective-permute-start.14 = (f32[64,128]{1,0:T(8,128)S(1)}, f32[64,128]{1,0:T(8,128)S(1)}, u32[]{:S(2)}, u32[]{:S(2)}) collective-permute-start(f32[64,128]{1,0:T(8,128)S(1)} %get-tuple-element.30), channel_id=1, source_target_pairs={{0,17},{1,16},{2,19},{3,18},{4,21},{5,20},{6,23},{7,22},{8,25},{9,... | collective-permute-start | bytes 98312 | tf_op jit(solution)/shard_map/ppermute | solution.py:515
  32.7 4.2 %collective-permute-start.15 = (f32[64,128]{1,0:T(8,128)S(1)}, f32[64,128]{1,0:T(8,128)S(1)}, u32[]{:S(2)}, u32[]{:S(2)}) collective-permute-start(f32[64,128]{1,0:T(8,128)S(1)} %get-tuple-element.31), channel_id=1, source_target_pairs={{0,25},{1,24},{2,27},{3,26},{4,29},{5,28},{6,31},{7,30},{8,17},{9,... | collective-permute-start | bytes 98312 | tf_op jit(solution)/shard_map/ppermute | solution.py:515

commit v9 on v8

--- a/solution.py
+++ b/solution.py
@@ -161,9 +161,28 @@
     bag = looked.shape[0]
     head = min(HOT + 8, win_size)
 
-    def kernel(starts_ref, looked_ref, bottom_ref, table_ref, hot_ref, places_ref, near_ref, wide_ref, held, sems):
+    def kernel(
+        starts_hbm, looked_hbm, bottom_hbm, table_ref, hot_ref, places_ref, near_ref, wide_ref,
+        starts_ref, looked_ref, bottom_ref, held, sems, small,
+    ):
         grp_pos = lax.axis_index("grp")
         shard_pos = lax.axis_index("shard")
+        from_starts = pltpu.make_async_copy(starts_hbm, starts_ref, small.at[0])
+        from_starts.start()
+        from_looked = pltpu.make_async_copy(looked_hbm, looked_ref, small.at[1])
+        from_looked.start()
+        from_bottom = pltpu.make_async_copy(bottom_hbm, bottom_ref, small.at[2])
+        from_bottom.start()
+        tails = []
+        for window in range(group_count):
+            tail = pltpu.make_async_copy(
+                table_ref.at[pl.ds(window * win_size, HOT)],
+                held.at[window, pl.ds(head, HOT)],
+                sems.at[window, 1],
+            )
+            tail.start()
+            tails.append(tail)
+        from_starts.wait()
         shifts = []
         copies = []
         for window in range(group_count):
@@ -176,12 +195,10 @@
                 held.at[window, pl.ds(0, head)],
                 sems.at[window, 0],
             )
-            second = pltpu.make_async_copy(
-                table_ref.at[pl.ds(base, HOT)], held.at[window, pl.ds(head, HOT)], sems.at[window, 1]
-            )
             first.start()
-            second.start()
-            copies += [first, second]
+            copies += [first, tails[window]]
+        from_looked.wait()
+        from_bottom.wait()
         found = looked_ref[...]
         window_of = jnp.floor((found.astype(jnp.float32) + 0.5) * (1.0 / win_size)).astype(jnp.int32)
         places = (found - window_of * (win_size - HOT)).astype(jnp.float32)
@@ -204,11 +221,15 @@
             jax.ShapeDtypeStruct((samples + 8, width), jnp.float32),
             jax.ShapeDtypeStruct((samples, width), jnp.float32),
         ),
-        in_specs=[whole(pltpu.SMEM), whole(), whole(), whole(pl.ANY)],
+        in_specs=[whole(pltpu.HBM)] * 4,
         out_specs=(whole(), whole(), whole(), whole()),
         scratch_shapes=[
+            pltpu.SMEM(starts.shape, starts.dtype),
+            pltpu.VMEM(looked.shape, looked.dtype),
+            pltpu.VMEM(bottom_out.shape, bottom_out.dtype),
             pltpu.VMEM((group_count, head + HOT, width), jnp.float32),
             pltpu.SemaphoreType.DMA((group_count, 2)),
+            pltpu.SemaphoreType.DMA((3,)),
         ],
         cost_estimate=cost(1e6, 1e6),
         compiler_params=pltpu.CompilerParams(vmem_limit_bytes=GRANT),

time: 38 us -> 37.9 us (level)
  no operation moved by 1% of the time
where the time goes in v9:
time: 37.9 us; the launch traced here: 37.7 us
  starting transfers between devices  21.6 us (57%)
  Pallas kernels  7.94 us (21%)
  waiting for transfers between devices  7.4 us (20%)
  between operations  0.81 us (2%)
    ppermute x16, starting transfers between devices, across(): return lax.ppermute(values, ('grp', 'shard'), pairs)  21.6 us
    ppermute x16, waiting for transfers between devices, across(): return lax.ppermute(values, ('grp', 'shard'), pairs)  7.4 us
    pallas_call x1, Pallas kernels, finish_dense(): pl.pallas_call(kernel, out_shape=(jax.ShapeDtypeStruct((samples, hidden),...  2.11 us
    pallas_call x1, Pallas kernels, load_first(): pl.pallas_call(kernel, out_shape=(jax.ShapeDtypeStruct((group_count * HOT...  1.78 us
    pallas_call x4, Pallas kernels, pool_rows(): pl.pallas_call(kernel, out_shape=jax.ShapeDtypeStruct((samples, width), j...  1.52 us
    pallas_call x1, Pallas kernels, place_rows(): pl.pallas_call(kernel, out_shape=jax.ShapeDtypeStruct((win_size, width),...  0.87 us
  transfers between devices with their start and end apart: 16, of which 6 were waited for; matrix products, arithmetic and copies ran while one was open for 0% of the time, Pallas kernels for 13%

profile of v9, /device:TPU:0, one launch (start us, length us, event | category | flops | bytes accessed | tf_op | source)
XLA Modules:
  0.0 37.7 jit_solution(2811705663450914631)
XLA Ops:
  0.7 1.8 %load_first.1 = (f32[256,128]{1,0:T(8,128)S(1)}, f32[8,128]{1,0:T(8,128)S(1)}, f32[136,128]{1,0:T(8,128)S(1)}, f32[128,128]{1,0:T(8,128)S(1)}) custom-call(s32[4,32]{1,0:T(4,128)} %starts_ref.1, s32[4,128]{1,0:T(4,128)} %bitcast.7, bf16[128,128]{1,0:T(8,128)(2,1)} %bottom_ref.3, f32[7872,128]{1,0:T(8,128)} %bitcast.5), custom_call_target="tpu_custom_call" | custom-call | flops 1000000 | bytes 1000000 | tf_op jit(solution)/shard_map/load_first/pallas_call | solution.py:216
  2.5 0.6 %collective-permute-start = (f32[256,128]{1,0:T(8,128)S(1)}, f32[256,128]{1,0:T(8,128)S(1)}, u32[]{:S(2)}, u32[]{:S(2)}) collective-permute-start(f32[256,128]{1,0:T(8,128)S(1)} %get-tuple-element.19.own_ref), channel_id=1, source_target_pairs={{0,1},{1,0},{2,3},{3,2},{4,5},{5,4},{6,7},{7,6},{8,9},{9,8},{10,11... | collective-permute-start | bytes 393224 | tf_op jit(solution)/shard_map/ppermute | solution.py:536
  3.0 2.7 %collective-permute-start.5 = (f32[136,128]{1,0:T(8,128)S(1)}, f32[136,128]{1,0:T(8,128)S(1)}, u32[]{:S(2)}, u32[]{:S(2)}) collective-permute-start(f32[136,128]{1,0:T(8,128)S(1)} %get-tuple-element.20.refs_4_), channel_id=1, source_target_pairs={{0,3},{1,2},{2,1},{3,0},{4,7},{5,6},{6,5},{7,4},{8,11},{9,10},{10,... | collective-permute-start | bytes 208904 | tf_op jit(solution)/shard_map/ppermute | solution.py:536
  5.7 2.6 %collective-permute-start.3 = (f32[8,128]{1,0:T(8,128)S(1)}, f32[8,128]{1,0:T(8,128)S(1)}, u32[]{:S(2)}, u32[]{:S(2)}) collective-permute-start(f32[8,128]{1,0:T(8,128)S(1)} %get-tuple-element.18.places_ref.refs_0_), channel_id=1, source_target_pairs={{0,4},{1,5},{2,6},{3,7},{4,0},{5,1},{6,2},{7,3},{8,12},{9,13},{10,... | collective-permute-start | bytes 12296 | tf_op jit(solution)/shard_map/ppermute | solution.py:536
  8.4 0.4 %pool_rows.7 = f32[128,128]{1,0:T(8,128)S(1)} custom-call(f32[136,128]{1,0:T(8,128)S(1)} %collective-permute-done.5.places_ref.refs_3_.refs_7_, bf16[512,256]{1,0:T(8,128)(2,1)S(1)} %hot_terms.1.terms_ref), custom_call_target="tpu_custom_call" | custom-call | flops 50000000 | bytes 1000000 | tf_op jit(solution)/shard_map/pool_rows/pallas_call | solution.py:303
  8.7 1.3 %collective-permute-start.6 = (f32[128,128]{1,0:T(8,128)S(1)}, f32[128,128]{1,0:T(8,128)S(1)}, u32[]{:S(2)}, u32[]{:S(2)}) collective-permute-start(f32[128,128]{1,0:T(8,128)S(1)} %pool_rows.7), channel_id=1, source_target_pairs={{0,3},{1,2},{2,1},{3,0},{4,7},{5,6},{6,5},{7,4},{8,11},{9,10},{10,... | collective-permute-start | bytes 196616 | tf_op jit(solution)/shard_map/ppermute | solution.py:536
  10.2 0.4 %pool_rows.6 = f32[128,128]{1,0:T(8,128)S(1)} custom-call(f32[8,128]{1,0:T(8,128)S(1)} %collective-permute-done.3.places_ref.refs_2_, bf16[512,256]{1,0:T(8,128)(2,1)S(1)} %hot_terms.1.terms_ref), custom_call_target="tpu_custom_call" | custom-call | flops 50000000 | bytes 1000000 | tf_op jit(solution)/shard_map/pool_rows/pallas_call | solution.py:303
  10.6 2.8 %collective-permute-start.4 = (f32[128,128]{1,0:T(8,128)S(1)}, f32[128,128]{1,0:T(8,128)S(1)}, u32[]{:S(2)}, u32[]{:S(2)}) collective-permute-start(f32[128,128]{1,0:T(8,128)S(1)} %pool_rows.6), channel_id=1, source_target_pairs={{0,4},{1,5},{2,6},{3,7},{4,0},{5,1},{6,2},{7,3},{8,12},{9,13},{10,... | collective-permute-start | bytes 196616 | tf_op jit(solution)/shard_map/ppermute | solution.py:536
  13.4 0.4 %pool_rows.5 = f32[128,128]{1,0:T(8,128)S(1)} custom-call(f32[8,128]{1,0:T(8,128)S(1)} %collective-permute-done.1.places_ref.refs_1_, bf16[512,256]{1,0:T(8,128)(2,1)S(1)} %hot_terms.1.terms_ref), custom_call_target="tpu_custom_call" | custom-call | flops 50000000 | bytes 1000000 | tf_op jit(solution)/shard_map/pool_rows/pallas_call | solution.py:303
  13.8 3.5 %collective-permute-start.10 = (f32[128,128]{1,0:T(8,128)S(1)}, f32[128,128]{1,0:T(8,128)S(1)}, u32[]{:S(2)}, u32[]{:S(2)}) collective-permute-start(f32[128,128]{1,0:T(8,128)S(1)} %get-tuple-element.26), channel_id=1, source_target_pairs={{0,7},{1,6},{2,5},{3,4},{4,3},{5,2},{6,1},{7,0},{8,15},{9,14},{10,... | collective-permute-start | bytes 196616 | tf_op jit(solution)/shard_map/ppermute | solution.py:536
  17.6 0.4 %pool_rows.4.refs_0_ = f32[128,128]{1,0:T(8,128)S(1)} custom-call(f32[8,128]{1,0:T(8,128)S(1)} %get-tuple-element.18.places_ref.refs_0_, bf16[512,256]{1,0:T(8,128)(2,1)S(1)} %hot_terms.1.terms_ref), custom_call_target="tpu_custom_call" | custom-call | flops 50000000 | bytes 1000000 | tf_op jit(solution)/shard_map/pool_rows/pallas_call | solution.py:303
  18.0 2.1 %collective-permute-done.2.refs_1_ = f32[128,128]{1,0:T(8,128)S(1)} collective-permute-done((f32[128,128]{1,0:T(8,128)S(1)}, f32[128,128]{1,0:T(8,128)S(1)}, u32[]{:S(2)}, u32[]{:S(2)}) %collective-permute-start.2) | collective-permute-done | bytes 65568 | tf_op jit(solution)/shard_map/ppermute | solution.py:536
  20.1 0.4 %score.1 = (f32[1,128]{1,0:T(1,128)S(1)}, f32[128,128]{1,0:T(8,128)S(1)}) custom-call(f32[128,128]{1,0:T(8,128)S(1)} %pool_rows.4.refs_0_, f32[128,128]{1,0:T(8,128)S(1)} %collective-permute-done.2.refs_1_, f32[128,128]{1,0:T(8,128)S(1)} %collective-permute-done.4.refs_2_, f32[128,128]{1,0:T(8,128)S(1)} %collective-permute-done.6.refs_3_, ...), custom_call_target="tpu_custom_call" | custom-call | flops 10000000 | bytes 1000000 | tf_op jit(solution)/shard_map/score/pallas_call | solution.py:338
  20.9 4.3 %collective-permute-start.8 = (f32[1,128]{1,0:T(1,128)S(1)}, f32[1,128]{1,0:T(1,128)S(1)}, u32[]{:S(2)}, u32[]{:S(2)}) collective-permute-start(f32[1,128]{1,0:T(1,128)S(1)} %get-tuple-element.25.refs_0_), channel_id=1, source_target_pairs={{0,4},{1,5},{2,6},{3,7},{4,0},{5,1},{6,2},{7,3},{8,12},{9,13},{10,... | collective-permute-start | bytes 1544 | tf_op jit(solution)/shard_map/ppermute | solution.py:536
  25.2 0.4 %count_grads.1 = (f32[256,512]{1,0:T(8,128)S(1)}, f32[256,512]{1,0:T(8,128)S(1)}) custom-call(f32[8,128]{1,0:T(8,128)S(1)} %get-tuple-element.18.places_ref.refs_0_, f32[8,128]{1,0:T(8,128)S(1)} %collective-permute-done.1.places_ref.refs_1_, f32[8,128]{1,0:T(8,128)S(1)} %collective-permute-done.3.places_ref.refs_2_, ...), custom_call_target="tpu_custom_call" | custom-call | flops 10000000 | bytes 1000000 | tf_op jit(solution)/shard_map/count_grads/pallas_call | solution.py:416
  25.6 1.1 %collective-permute-done.8.refs_2_ = f32[1,128]{1,0:T(1,128)S(1)} collective-permute-done((f32[1,128]{1,0:T(1,128)S(1)}, f32[1,128]{1,0:T(1,128)S(1)}, u32[]{:S(2)}, u32[]{:S(2)}) %collective-permute-start.8) | collective-permute-done | bytes 544 | tf_op jit(solution)/shard_map/ppermute | solution.py:536
  26.7 1.4 %collective-permute-done.9.refs_3_ = f32[1,128]{1,0:T(1,128)S(1)} collective-permute-done((f32[1,128]{1,0:T(1,128)S(1)}, f32[1,128]{1,0:T(1,128)S(1)}, u32[]{:S(2)}, u32[]{:S(2)}) %collective-permute-start.9) | collective-permute-done | bytes 544 | tf_op jit(solution)/shard_map/ppermute | solution.py:536
  29.1 0.8 %collective-permute-done.12.received_ref = f32[256,128]{1,0:T(8,128)S(1)} collective-permute-done((f32[256,128]{1,0:T(8,128)S(1)}, f32[256,128]{1,0:T(8,128)S(1)}, u32[]{:S(2)}, u32[]{:S(2)}) %collective-permute-start.12) | collective-permute-done | bytes 131104 | tf_op jit(solution)/shard_map/ppermute | solution.py:536
  29.9 1.4 %collective-permute-start.13 = (f32[64,128]{1,0:T(8,128)S(1)}, f32[64,128]{1,0:T(8,128)S(1)}, u32[]{:S(2)}, u32[]{:S(2)}) collective-permute-start(f32[64,128]{1,0:T(8,128)S(1)} %get-tuple-element.29), channel_id=1, source_target_pairs={{0,9},{1,8},{2,11},{3,10},{4,13},{5,12},{6,15},{7,14},{8,1},{9,0},... | collective-permute-start | bytes 98312 | tf_op jit(solution)/shard_map/ppermute | solution.py:536
  31.3 1.3 %collective-permute-start.14 = (f32[64,128]{1,0:T(8,128)S(1)}, f32[64,128]{1,0:T(8,128)S(1)}, u32[]{:S(2)}, u32[]{:S(2)}) collective-permute-start(f32[64,128]{1,0:T(8,128)S(1)} %get-tuple-element.30), channel_id=1, source_target_pairs={{0,17},{1,16},{2,19},{3,18},{4,21},{5,20},{6,23},{7,22},{8,25},{9,... | collective-permute-start | bytes 98312 | tf_op jit(solution)/shard_map/ppermute | solution.py:536
  32.6 0.4 %collective-permute-start.15 = (f32[64,128]{1,0:T(8,128)S(1)}, f32[64,128]{1,0:T(8,128)S(1)}, u32[]{:S(2)}, u32[]{:S(2)}) collective-permute-start(f32[64,128]{1,0:T(8,128)S(1)} %get-tuple-element.31), channel_id=1, source_target_pairs={{0,25},{1,24},{2,27},{3,26},{4,29},{5,28},{6,31},{7,30},{8,17},{9,... | collective-permute-start | bytes 98312 | tf_op jit(solution)/shard_map/ppermute | solution.py:536
  33.0 2.1 %finish_dense.1 = (bf16[128,1024]{1,0:T(8,128)(2,1)}, f32[128,128]{1,0:T(8,128)}, f32[1968,128]{1,0:T(8,128)}) custom-call(f32[128,128]{1,0:T(8,128)S(1)} %get-tuple-element.21.pooled_ref, bf16[128,128]{1,0:T(8,128)(2,1)S(1)} %copy-done.2, f32[128,1024]{1,0:T(8,128)S(1)} %linear_part.1.refs_5_.linear_ref, f32[1,1024]{1,0:T(1,128)S(1)} %copy-done.3, ...), custom_call_target="tpu_custom_call" | custom-call | flops 50000000 | bytes 1000000 | tf_op jit(solution)/shard_map/finish_dense/pallas_call | solution.py:377
  35.2 1.7 %collective-permute-done.15.refs_3_ = f32[64,128]{1,0:T(8,128)S(1)} collective-permute-done((f32[64,128]{1,0:T(8,128)S(1)}, f32[64,128]{1,0:T(8,128)S(1)}, u32[]{:S(2)}, u32[]{:S(2)}) %collective-permute-start.15) | collective-permute-done | bytes 32800 | tf_op jit(solution)/shard_map/ppermute | solution.py:536
  36.9 0.9 %place_rows.1 = f32[1968,128]{1,0:T(8,128)} custom-call(s32[4,32]{1,0:T(4,128)S(1)} %copy-done.4, f32[64,128]{1,0:T(8,128)S(1)} %get-tuple-element.28.refs_0_, f32[64,128]{1,0:T(8,128)S(1)} %collective-permute-done.13.refs_1_, f32[64,128]{1,0:T(8,128)S(1)} %collective-permute-done.14.refs_2_, ...), custom_call_target="tpu_custom_call", output_to_operand_aliasing={{}: (5, {})} | custom-call | flops 1000000 | bytes 2000000 | tf_op jit(solution)/shard_map/place_rows/pallas_call | solution.py:504
  (32 shorter events, 1.8 us)
Async XLA Ops:
  0.6 16.7 %copy-start.2 = (bf16[128,128]{1,0:T(8,128)(2,1)S(1)}, bf16[128,128]{1,0:T(8,128)(2,1)}, u32[]{:S(2)}) copy-start(bf16[128,128]{1,0:T(8,128)(2,1)} %bottom_ref.3) | copy-start | bytes 98308
  0.6 16.7 %copy-start.1 = (bf16[128,1024]{1,0:T(8,128)(2,1)S(1)}, bf16[128,1024]{1,0:T(8,128)(2,1)}, u32[]{:S(2)}) copy-start(bf16[128,1024]{1,0:T(8,128)(2,1)} %dense_ref.3) | copy-start | bytes 786436
  0.7 19.4 %copy-start.3 = (f32[1,1024]{1,0:T(1,128)S(1)}, f32[1,1024]{1,0:T(1,128)}, u32[]{:S(2)}) copy-start(f32[1,1024]{1,0:T(1,128)} %pairs_ref.1) | copy-start | bytes 12292
  0.7 19.4 %copy-start = (f32[128,1024]{1,0:T(8,128)S(1)}, f32[128,1024]{1,0:T(8,128)}, u32[]{:S(2)}) copy-start(f32[128,1024]{1,0:T(8,128)} %cot_ref.1) | copy-start | bytes 1572868
  2.5 34.4 %copy-start.4 = (s32[4,32]{1,0:T(4,128)S(1)}, s32[4,32]{1,0:T(4,128)}, u32[]{:S(2)}) copy-start(s32[4,32]{1,0:T(4,128)} %starts_ref.1) | copy-start | bytes 1540
  2.5 5.8 %collective-permute-start = (f32[256,128]{1,0:T(8,128)S(1)}, f32[256,128]{1,0:T(8,128)S(1)}, u32[]{:S(2)}, u32[]{:S(2)}) collective-permute-start(f32[256,128]{1,0:T(8,128)S(1)} %get-tuple-element.19.own_ref), channel_id=1, source_target_pairs={{0,1},{1,0},{2,3},{3,2},{4,5},{5,4},{6,7},{7,6},{8,9},{9,8},{10,11... | collective-permute-start | bytes 393224 | tf_op jit(solution)/shard_map/ppermute | solution.py:536
  3.0 5.3 %collective-permute-start.5 = (f32[136,128]{1,0:T(8,128)S(1)}, f32[136,128]{1,0:T(8,128)S(1)}, u32[]{:S(2)}, u32[]{:S(2)}) collective-permute-start(f32[136,128]{1,0:T(8,128)S(1)} %get-tuple-element.20.refs_4_), channel_id=1, source_target_pairs={{0,3},{1,2},{2,1},{3,0},{4,7},{5,6},{6,5},{7,4},{8,11},{9,10},{10,... | collective-permute-start | bytes 208904 | tf_op jit(solution)/shard_map/ppermute | solution.py:536
  5.7 4.5 %collective-permute-start.3 = (f32[8,128]{1,0:T(8,128)S(1)}, f32[8,128]{1,0:T(8,128)S(1)}, u32[]{:S(2)}, u32[]{:S(2)}) collective-permute-start(f32[8,128]{1,0:T(8,128)S(1)} %get-tuple-element.18.places_ref.refs_0_), channel_id=1, source_target_pairs={{0,4},{1,5},{2,6},{3,7},{4,0},{5,1},{6,2},{7,3},{8,12},{9,13},{10,... | collective-permute-start | bytes 12296 | tf_op jit(solution)/shard_map/ppermute | solution.py:536
  8.3 5.1 %collective-permute-start.1 = (f32[8,128]{1,0:T(8,128)S(1)}, f32[8,128]{1,0:T(8,128)S(1)}, u32[]{:S(2)}, u32[]{:S(2)}) collective-permute-start(f32[8,128]{1,0:T(8,128)S(1)} %get-tuple-element.18.places_ref.refs_0_), channel_id=1, source_target_pairs={{0,7},{1,6},{2,5},{3,4},{4,3},{5,2},{6,1},{7,0},{8,15},{9,14},{10,... | collective-permute-start | bytes 12296 | tf_op jit(solution)/shard_map/ppermute | solution.py:536
  8.7 9.2 %collective-permute-start.6 = (f32[128,128]{1,0:T(8,128)S(1)}, f32[128,128]{1,0:T(8,128)S(1)}, u32[]{:S(2)}, u32[]{:S(2)}) collective-permute-start(f32[128,128]{1,0:T(8,128)S(1)} %pool_rows.7), channel_id=1, source_target_pairs={{0,3},{1,2},{2,1},{3,0},{4,7},{5,6},{6,5},{7,4},{8,11},{9,10},{10,... | collective-permute-start | bytes 196616 | tf_op jit(solution)/shard_map/ppermute | solution.py:536
  10.6 7.4 %collective-permute-start.4 = (f32[128,128]{1,0:T(8,128)S(1)}, f32[128,128]{1,0:T(8,128)S(1)}, u32[]{:S(2)}, u32[]{:S(2)}) collective-permute-start(f32[128,128]{1,0:T(8,128)S(1)} %pool_rows.6), channel_id=1, source_target_pairs={{0,4},{1,5},{2,6},{3,7},{4,0},{5,1},{6,2},{7,3},{8,12},{9,13},{10,... | collective-permute-start | bytes 196616 | tf_op jit(solution)/shard_map/ppermute | solution.py:536
  13.8 6.3 %collective-permute-start.2 = (f32[128,128]{1,0:T(8,128)S(1)}, f32[128,128]{1,0:T(8,128)S(1)}, u32[]{:S(2)}, u32[]{:S(2)}) collective-permute-start(f32[128,128]{1,0:T(8,128)S(1)} %pool_rows.5), channel_id=1, source_target_pairs={{0,7},{1,6},{2,5},{3,4},{4,3},{5,2},{6,1},{7,0},{8,15},{9,14},{10,... | collective-permute-start | bytes 196616 | tf_op jit(solution)/shard_map/ppermute | solution.py:536
  13.8 11.7 %collective-permute-start.10 = (f32[128,128]{1,0:T(8,128)S(1)}, f32[128,128]{1,0:T(8,128)S(1)}, u32[]{:S(2)}, u32[]{:S(2)}) collective-permute-start(f32[128,128]{1,0:T(8,128)S(1)} %get-tuple-element.26), channel_id=1, source_target_pairs={{0,7},{1,6},{2,5},{3,4},{4,3},{5,2},{6,1},{7,0},{8,15},{9,14},{10,... | collective-permute-start | bytes 196616 | tf_op jit(solution)/shard_map/ppermute | solution.py:536
  17.4 8.2 %collective-permute-start.11 = (f32[128,128]{1,0:T(8,128)S(1)}, f32[128,128]{1,0:T(8,128)S(1)}, u32[]{:S(2)}, u32[]{:S(2)}) collective-permute-start(f32[128,128]{1,0:T(8,128)S(1)} %get-tuple-element.26), channel_id=1, source_target_pairs={{0,4},{1,5},{2,6},{3,7},{4,0},{5,1},{6,2},{7,3},{8,12},{9,13},{10,... | collective-permute-start | bytes 196616 | tf_op jit(solution)/shard_map/ppermute | solution.py:536
  20.5 5.1 %collective-permute-start.7 = (f32[1,128]{1,0:T(1,128)S(1)}, f32[1,128]{1,0:T(1,128)S(1)}, u32[]{:S(2)}, u32[]{:S(2)}) collective-permute-start(f32[1,128]{1,0:T(1,128)S(1)} %get-tuple-element.25.refs_0_), channel_id=1, source_target_pairs={{0,7},{1,6},{2,5},{3,4},{4,3},{5,2},{6,1},{7,0},{8,15},{9,14},{10,... | collective-permute-start | bytes 1544 | tf_op jit(solution)/shard_map/ppermute | solution.py:536
  20.9 5.9 %collective-permute-start.8 = (f32[1,128]{1,0:T(1,128)S(1)}, f32[1,128]{1,0:T(1,128)S(1)}, u32[]{:S(2)}, u32[]{:S(2)}) collective-permute-start(f32[1,128]{1,0:T(1,128)S(1)} %get-tuple-element.25.refs_0_), channel_id=1, source_target_pairs={{0,4},{1,5},{2,6},{3,7},{4,0},{5,1},{6,2},{7,3},{8,12},{9,13},{10,... | collective-permute-start | bytes 1544 | tf_op jit(solution)/shard_map/ppermute | solution.py:536
  25.2 3.0 %collective-permute-start.9 = (f32[1,128]{1,0:T(1,128)S(1)}, f32[1,128]{1,0:T(1,128)S(1)}, u32[]{:S(2)}, u32[]{:S(2)}) collective-permute-start(f32[1,128]{1,0:T(1,128)S(1)} %get-tuple-element.25.refs_0_), channel_id=1, source_target_pairs={{0,3},{1,2},{2,1},{3,0},{4,7},{5,6},{6,5},{7,4},{8,11},{9,10},{10,... | collective-permute-start | bytes 1544 | tf_op jit(solution)/shard_map/ppermute | solution.py:536
  28.5 1.4 %collective-permute-start.12 = (f32[256,128]{1,0:T(8,128)S(1)}, f32[256,128]{1,0:T(8,128)S(1)}, u32[]{:S(2)}, u32[]{:S(2)}) collective-permute-start(f32[256,128]{1,0:T(8,128)S(1)} %row_grads.3), channel_id=1, source_target_pairs={{0,1},{1,0},{2,3},{3,2},{4,5},{5,4},{6,7},{7,6},{8,9},{9,8},{10,11... | collective-permute-start | bytes 393224 | tf_op jit(solution)/shard_map/ppermute | solution.py:536
  29.9 5.2 %collective-permute-start.13 = (f32[64,128]{1,0:T(8,128)S(1)}, f32[64,128]{1,0:T(8,128)S(1)}, u32[]{:S(2)}, u32[]{:S(2)}) collective-permute-start(f32[64,128]{1,0:T(8,128)S(1)} %get-tuple-element.29), channel_id=1, source_target_pairs={{0,9},{1,8},{2,11},{3,10},{4,13},{5,12},{6,15},{7,14},{8,1},{9,0},... | collective-permute-start | bytes 98312 | tf_op jit(solution)/shard_map/ppermute | solution.py:536
  31.3 3.9 %collective-permute-start.14 = (f32[64,128]{1,0:T(8,128)S(1)}, f32[64,128]{1,0:T(8,128)S(1)}, u32[]{:S(2)}, u32[]{:S(2)}) collective-permute-start(f32[64,128]{1,0:T(8,128)S(1)} %get-tuple-element.30), channel_id=1, source_target_pairs={{0,17},{1,16},{2,19},{3,18},{4,21},{5,20},{6,23},{7,22},{8,25},{9,... | collective-permute-start | bytes 98312 | tf_op jit(solution)/shard_map/ppermute | solution.py:536
  32.6 4.2 %collective-permute-start.15 = (f32[64,128]{1,0:T(8,128)S(1)}, f32[64,128]{1,0:T(8,128)S(1)}, u32[]{:S(2)}, u32[]{:S(2)}) collective-permute-start(f32[64,128]{1,0:T(8,128)S(1)} %get-tuple-element.31), channel_id=1, source_target_pairs={{0,25},{1,24},{2,27},{3,26},{4,29},{5,28},{6,31},{7,30},{8,17},{9,... | collective-permute-start | bytes 98312 | tf_op jit(solution)/shard_map/ppermute | solution.py:536
